TPU v7x, 512 devices: a whole 4x8x8 slice. The times are simulated.
512 devices in a mesh: dp: 8 (over y_hi, core), expert: 64 (over y_lo, x, z).
Axes of the slice: x: 4, y: 8 (y_hi: 4, y_lo: 2; y = y_hi * 2 + y_lo), z: 8, core: 2. Of those that a mesh axis runs over, the one named last changes fastest.
Arguments:
- weights: bfloat16 [16, 3584, 512], P(None, ('dp', 'expert')), may hold values from -0.09375 to 0.09375
- first_moment: float32 [16, 3584, 512], P(None, ('dp', 'expert')), may hold values from -3 to 3
- second_moment: float32 [16, 3584, 512], P(None, ('dp', 'expert')), may hold values from 0.05 to 2
- placement: int32 [64], replicated, may hold values from 0 to 15, as said below
- block_counts: int32 [8, 64], P('dp', 'expert'), may hold values from 1 to 2
- tokens: bfloat16 [8, 64, 256, 3584], P('dp', 'expert'), may hold values from -6 to 6
- hidden_grad: bfloat16 [8, 64, 256, 256], P('dp', 'expert'), may hold values from -1.1953125 to 1.1953125
Outputs:
- new_weights: bfloat16 [64, 3584, 512], P('expert', 'dp')
- new_first: float32 [64, 3584, 512], P('expert', 'dp')
- new_second: float32 [64, 3584, 512], P('expert', 'dp')
Inputs may be any that keep to these rules, and one draw needn't show every extreme that they name: `placement`: every expert block 0 to 15 is owned by at least one device. `block_counts`: the rows after a device's live blocks are padding.
All inputs are finite; a program needn't handle non-finite values.
Results may differ from a plain program's by a relative error of at most 0.015.
Values may be sent and summed in bfloat16 or wider, within the bound.
No kernel may reach another device: no remote copies, remote signals or barrier semaphores. Data moves between devices by JAX's collectives and lax.ppermute only.
A program may use at most 64 MiB of HBM per device.

v0:
```python
import jax
import jax.numpy as jnp
from jax import lax
from jax.experimental import pallas as pl
from jax.experimental.pallas import tpu as pltpu
from jax.sharding import PartitionSpec as P


BLOCK = 128


beta_first = 0.9
beta_second = 0.95
learning_rate = 0.001
weight_decay = 0.1
adam_epsilon = 1e-08
adam_steps = 10.0


def adam_update(params, first_moment, second_moment, gradient):
    moment_one = beta_first * first_moment + (1.0 - beta_first) * gradient
    moment_two = beta_second * second_moment + (1.0 - beta_second) * gradient * gradient
    correct_one = 1.0 - beta_first**adam_steps
    correct_two = 1.0 - beta_second**adam_steps
    params_full = params.astype(jnp.float32)
    step_size = (
        moment_one / correct_one / (jnp.sqrt(moment_two / correct_two) + adam_epsilon)
        + weight_decay * params_full
    )
    return ((params_full - learning_rate * step_size).astype(jnp.bfloat16), moment_one, moment_two)


def grad_halves(projected, upstream):
    half_width = projected.shape[1] // 2
    gate_part = projected[:, :half_width]
    upward = projected[:, half_width:]
    sigmoid_gate = jax.nn.sigmoid(gate_part)
    masked = upstream.astype(jnp.float32)
    grad_gate = masked * upward * sigmoid_gate * (1.0 + gate_part * (1.0 - sigmoid_gate))
    grad_upward = masked * gate_part * sigmoid_gate
    return grad_gate.astype(jnp.bfloat16), grad_upward.astype(jnp.bfloat16)


def term_rows(turned_ref, grad_ref, start, count):
    rows = turned_ref[pl.ds(pl.multiple_of(start, 16), count), :]
    return jnp.dot(rows, grad_ref[...], preferred_element_type=jnp.float32).astype(jnp.bfloat16)


def piece_start(place, step, side, count):
    return pl.multiple_of((2 * ((place[0] + step) % 4) + (place[1] + side) % 2) * count, 16)


def block_start(place, step, count):
    return pl.multiple_of(((place[0] + step) % 4) * 2 * count, 128)


def join(place, block, mine, theirs):
    count = mine.shape[0]
    core = place[1]
    block[pl.ds(pl.multiple_of(core * count, 16), count), :] = mine[...]
    block[pl.ds(pl.multiple_of((1 - core) * count, 16), count), :] = theirs[...]


def partial_kernel(place, tok_mine, tok_theirs, *rest):
    pieces, partial, block = rest[:6], rest[6], rest[7]
    count = pieces[0].shape[0]
    half = tok_mine.shape[0]
    for slot in range(3):
        join(place, block.at[slot], pieces[2 * slot], pieces[2 * slot + 1])
    for low, tok in ((0, tok_mine), (half, tok_theirs)):
        total = None
        for slot, step in enumerate((0, 1, 3)):
            part = jnp.dot(
                tok[:, pl.ds(block_start(place, step, count), 2 * count)],
                block[slot],
                preferred_element_type=jnp.float32,
            )
            total = part if total is None else total + part
        partial[low : low + half, :] = total


def project_kernel(
    place, partial, hid_mine, hid_theirs, piece_mine, piece_theirs, tok_mine, tok_theirs, turned,
    grad_ref, far_mine, last_mine, block, far_tok, far_rows, last_rows, sems,
):
    count = piece_mine.shape[0]
    half = hid_mine.shape[0]
    lanes = pl.ds(block_start(place, 2, count), 2 * count)
    copies = [
        pltpu.make_async_copy(tok_mine.at[:, lanes], far_tok.at[0:half], sems.at[0]),
        pltpu.make_async_copy(tok_theirs.at[:, lanes], far_tok.at[half : 2 * half], sems.at[1]),
        pltpu.make_async_copy(
            turned.at[pl.ds(piece_start(place, 2, 0, count), count)], far_rows, sems.at[2]
        ),
        pltpu.make_async_copy(
            turned.at[pl.ds(piece_start(place, 3, 0, count), count)], last_rows, sems.at[3]
        ),
    ]
    for copy in copies:
        copy.start()
    join(place, block, piece_mine, piece_theirs)
    width = block.shape[1] // 2
    copies[0].wait()
    copies[1].wait()
    for hid, low in ((hid_mine, 0), (hid_theirs, half)):
        projected = partial[low : low + half, :] + jnp.dot(
            far_tok[low : low + half, :], block[...], preferred_element_type=jnp.float32
        )
        grad_gate, grad_up = grad_halves(projected, hid[...])
        grad_ref[low : low + half, :width] = grad_gate
        grad_ref[low : low + half, width:] = grad_up
    copies[2].wait()
    copies[3].wait()
    grads = grad_ref[...]
    far_mine[...] = jnp.dot(far_rows[...], grads, preferred_element_type=jnp.float32).astype(jnp.bfloat16)
    last_mine[...] = jnp.dot(last_rows[...], grads, preferred_element_type=jnp.float32).astype(jnp.bfloat16)


def turn_kernel(tok_mine, tok_theirs, turned):
    half, wide = tok_mine.shape
    for low, tok in ((0, tok_mine), (half, tok_theirs)):
        for begin in range(0, wide, 512):
            turned[begin : begin + 512, low : low + half] = tok[:, begin : begin + 512].T


def term_kernel(place, turned, grad_ref, *outs):
    count = outs[0].shape[0]
    for slot, (step, side) in enumerate(((2, 1), (1, 0), (1, 1), (3, 1), (0, 0), (0, 1))):
        outs[slot][...] = term_rows(turned, grad_ref, piece_start(place, step, side, count), count)


def adam_kernel(place, params, first, second, gradient, updated, moment_one, moment_two):
    lanes = params.shape[1] // 4
    for kind in range(2):
        for side in range(2):
            read = pl.ds((2 * side + kind) * lanes, lanes)
            into = pl.ds(pl.multiple_of((2 * kind + (place[1] + side) % 2) * lanes, 128), lanes)
            new_params, new_one, new_two = adam_update(
                params[:, read],
                first[:, read].astype(jnp.float32),
                second[:, read].astype(jnp.float32),
                gradient[:, read].astype(jnp.float32),
            )
            updated[0, :, into] = new_params
            moment_one[0, :, into] = new_one
            moment_two[0, :, into] = new_two


def in_vmem(count):
    return [pl.BlockSpec(memory_space=pltpu.VMEM) for _ in range(count)]


def in_smem():
    return [pl.BlockSpec(memory_space=pltpu.SMEM)]


def in_any(count):
    return [pl.BlockSpec(memory_space=pl.ANY) for _ in range(count)]


def on_device(weights, first_moment, second_moment, placement, block_counts, tokens, hidden_grad):
    expert_count = lax.axis_size("expert")
    dp_count = lax.axis_size("dp")
    chip_count = dp_count // 2
    block_total = weights.shape[0]
    span_rows = weights.shape[1]
    col_total = weights.shape[2]
    inputs = tokens[0, 0]
    row_total, wide = inputs.shape
    narrow = jnp.bfloat16
    own_count = expert_count * span_rows
    quarter = col_total // 4
    part_cols = 2 * quarter
    position = lax.axis_index("dp")
    chip, core = position // 2, position % 2
    place = jnp.stack([chip, core]).astype(jnp.int32)
    pick = (placement[:, None] == jnp.arange(block_total)[None, :]).astype(narrow)
    same = (placement[:, None] == placement[None, :]).astype(narrow)

    def exchange(values):
        return lax.all_to_all(values, "expert", split_axis=0, concat_axis=0, tiled=True)

    def choose(table, values):
        return jnp.einsum("jk,krc->jrc", table, values, preferred_element_type=jnp.float32).astype(narrow)

    def shift(value, step):
        pairs = [
            (2 * h + c, 2 * ((h + step) % chip_count) + c) for h in range(chip_count) for c in range(2)
        ]
        return lax.ppermute(value, "dp", pairs)

    def swap(value):
        return lax.ppermute(value, "dp", [(i, i ^ 1) for i in range(dp_count)])

    def halves(value):
        starts = range(0, value.shape[-1], 2 * quarter)
        even = jnp.concatenate([value[..., k : k + quarter] for k in starts], axis=-1)
        odd = jnp.concatenate([value[..., k + quarter : k + 2 * quarter] for k in starts], axis=-1)
        return jnp.where(core == 0, even, odd), jnp.where(core == 0, odd, even)

    def ordered(value):
        return jnp.concatenate(halves(value), axis=-1)

    def rows_of(value):
        return lax.optimization_barrier(value.reshape(own_count, value.shape[-1]))

    def add(*values):
        total = values[0].astype(jnp.float32)
        for value in values[1:]:
            total = total + value.astype(jnp.float32)
        return total.astype(narrow)

    live_mask = (jnp.arange(row_total) < BLOCK * block_counts[0, 0])[:, None]
    masked = jnp.where(live_mask, hidden_grad[0, 0], jnp.zeros((), narrow))
    hid_mine, hid_give = halves(masked)
    own_rows = exchange(choose(pick, ordered(weights))).reshape(own_count, col_total)
    mine, give = own_rows[:, :part_cols], own_rows[:, part_cols:]
    tok_theirs = swap(inputs)
    hid_theirs = swap(hid_give)
    plus_mine = shift(mine, 1)
    minus_mine = shift(mine, -1)
    theirs = swap(give)
    minus_theirs = shift(theirs, -1)
    plus_theirs = shift(theirs, 1)
    far_mine = shift(plus_mine, 1)
    far_theirs = shift(minus_theirs, -1)

    moments = ordered(jnp.concatenate([first_moment, second_moment], axis=1).astype(narrow))
    moments_sent, _ = lax.optimization_barrier((choose(pick, moments), own_rows))
    moments_here = exchange(moments_sent)

    turned = pl.pallas_call(
        turn_kernel,
        in_specs=in_vmem(2),
        out_specs=in_vmem(1)[0],
        out_shape=jax.ShapeDtypeStruct((wide, 2 * row_total), narrow),
        name="turn",
    )(inputs, tok_theirs)
    piece = jax.ShapeDtypeStruct((own_count, part_cols), narrow)
    partial = pl.pallas_call(
        partial_kernel,
        in_specs=in_smem() + in_vmem(8),
        out_specs=in_vmem(1)[0],
        out_shape=jax.ShapeDtypeStruct((2 * row_total, part_cols), jnp.float32),
        scratch_shapes=[pltpu.VMEM((3, 2 * own_count, part_cols), narrow)],
        name="partial",
    )(place, inputs, tok_theirs, mine, theirs, minus_mine, minus_theirs, plus_mine, plus_theirs)
    grad_proj, send_mine, last_mine = pl.pallas_call(
        project_kernel,
        in_specs=in_smem() + in_vmem(5) + in_any(3),
        out_specs=in_vmem(3),
        out_shape=[jax.ShapeDtypeStruct((2 * row_total, part_cols), narrow), piece, piece],
        scratch_shapes=[
            pltpu.VMEM((2 * own_count, part_cols), narrow),
            pltpu.VMEM((2 * row_total, 2 * own_count), narrow),
            pltpu.VMEM((own_count, 2 * row_total), narrow),
            pltpu.VMEM((own_count, 2 * row_total), narrow),
            pltpu.SemaphoreType.DMA((4,)),
        ],
        name="project",
    )(place, partial, hid_mine, hid_theirs, far_mine, far_theirs, inputs, tok_theirs, turned)
    got_plus = shift(send_mine, 1)
    early_mine = shift(last_mine, -1)
    send_theirs, next_mine, next_theirs, last_theirs, sum_mine, sum_theirs = pl.pallas_call(
        term_kernel,
        in_specs=in_smem() + in_vmem(2),
        out_specs=in_vmem(6),
        out_shape=[piece] * 6,
        name="terms",
    )(place, turned, grad_proj)
    got_minus = shift(send_theirs, -1)
    late_sent, next_theirs, moments_here = lax.optimization_barrier(
        (add(next_mine, got_plus), next_theirs, moments_here)
    )
    late_mine = shift(late_sent, 1)
    early_theirs = shift(next_theirs, 1)
    late_theirs = shift(add(last_theirs, got_minus), -1)
    total_mine = add(sum_mine, early_mine, late_mine)
    home_mine = exchange(total_mine.reshape(expert_count, span_rows, part_cols))
    total_other = swap(add(sum_theirs, early_theirs, late_theirs))
    home_other = exchange(total_other.reshape(expert_count, span_rows, part_cols))
    sums = jnp.concatenate([choose(same, home_mine), choose(same, home_other)], axis=-1)
    grad_rows = rows_of(exchange(sums))
    bands = chip_count
    band = own_count // bands
    spec = pl.BlockSpec((band, col_total), lambda i: (i, 0))
    out_spec = pl.BlockSpec((1, band, col_total), lambda i: (0, i, 0))
    shape = (1, own_count, col_total)
    return pl.pallas_call(
        adam_kernel,
        grid=(bands,),
        in_specs=in_smem() + [spec] * 4,
        out_specs=[out_spec] * 3,
        out_shape=[
            jax.ShapeDtypeStruct(shape, narrow),
            jax.ShapeDtypeStruct(shape, jnp.float32),
            jax.ShapeDtypeStruct(shape, jnp.float32),
        ],
        name="adam",
    )(
        place, own_rows, rows_of(moments_here[:, :span_rows]), rows_of(moments_here[:, span_rows:]),
        grad_rows,
    )


def solution(mesh):
    in_specs = (
        P(None, ("dp", "expert"), None),
        P(None, ("dp", "expert"), None),
        P(None, ("dp", "expert"), None),
        P(),
        P("dp", "expert"),
        P("dp", "expert", None, None),
        P("dp", "expert", None, None),
    )
    out_specs = (P("expert", "dp", None), P("expert", "dp", None), P("expert", "dp", None))

    return jax.shard_map(on_device, mesh=mesh, in_specs=in_specs, out_specs=out_specs, check_vma=False)
```

profile of v0, /device:TPU:16, one launch (start us, length us, event | category | flops | bytes accessed | tf_op | source)
XLA Modules:
  0.0 210.7 jit_solution(2469681869057423222)
XLA Ops:
  0.7 1.0 fusion.32
  1.7 1.0 convolution_convert_fusion.1
  2.7 1.1 copy.22
  3.7 15.1 %all-to-all-start = ((bf16[64,7,512]{2,1,0:T(8,128)(2,1)}), bf16[64,7,512]{2,1,0:T(8,128)(2,1)}, u32[]{:S(2)}, u32[]{:S(2)}) async-start(bf16[64,7,512]{2,1,0:T(8,128)(2,1)} %copy.22), calls=%async_computation | async-start | bytes 1048576 | tf_op jit(solution)/shard_map/all_to_all | solution.py:181
  18.8 1.9 collective-permute-start
  21.4 16.3 %all-to-all-done = bf16[64,7,512]{2,1,0:T(8,128)(2,1)} async-done(((bf16[64,7,512]{2,1,0:T(8,128)(2,1)}), bf16[64,7,512]{2,1,0:T(8,128)(2,1)}, u32[]{:S(2)}, u32[]{:S(2)}) %all-to-all-start) | async-done | bytes 458784 | tf_op jit(solution)/shard_map/all_to_all | solution.py:181
  37.6 1.2 reshape.32.params
  38.9 1.5 copy.23
  40.4 4.8 %all-to-all-start.1 = ((bf16[64,14,512]{2,1,0:T(8,128)(2,1)}), bf16[64,14,512]{2,1,0:T(8,128)(2,1)S(1)}, u32[]{:S(2)}, u32[]{:S(2)}) async-start(bf16[64,14,512]{2,1,0:T(8,128)(2,1)} %copy.23), calls=%async_computation.1 | async-start | bytes 2097152 | tf_op jit(solution)/shard_map/all_to_all | solution.py:181
  45.2 0.8 fusion.31
  46.0 1.9 collective-permute-start.1
  48.6 4.8 %collective-permute-start.4 = (bf16[448,256]{1,0:T(8,128)(2,1)}, bf16[448,256]{1,0:T(8,128)(2,1)S(1)}, u32[]{:S(2)}, u32[]{:S(2)}) collective-permute-start(bf16[448,256]{1,0:T(8,128)(2,1)} %get-tuple-element.32.rest_0_), channel_id=1, source_target_pairs={{0,128},{64,192},{128,256},{192,320},{256,384},{320,448},{384,0},{... | collective-permute-start | bytes 688136 | tf_op jit(solution)/shard_map/ppermute | solution.py:190
  53.4 1.9 collective-permute-start.3
  55.5 3.5 %collective-permute-start.2 = (bf16[448,256]{1,0:T(8,128)(2,1)}, bf16[448,256]{1,0:T(8,128)(2,1)}, u32[]{:S(2)}, u32[]{:S(2)}) collective-permute-start(bf16[448,256]{1,0:T(8,128)(2,1)} %get-tuple-element.32.rest_0_), channel_id=1, source_target_pairs={{0,384},{64,448},{128,0},{192,64},{256,128},{320,192},{384,256},{4... | collective-permute-start | bytes 688136 | tf_op jit(solution)/shard_map/ppermute | solution.py:190
  58.9 4.5 %collective-permute-start.5 = (bf16[448,256]{1,0:T(8,128)(2,1)S(1)}, bf16[448,256]{1,0:T(8,128)(2,1)}, u32[]{:S(2)}, u32[]{:S(2)}) collective-permute-start(bf16[448,256]{1,0:T(8,128)(2,1)S(1)} %collective-permute-done.1.rest_1_), channel_id=1, source_target_pairs={{0,128},{64,192},{128,256},{192,320},{256,384},{320,448},{384,0},{... | collective-permute-start | bytes 688136 | tf_op jit(solution)/shard_map/ppermute | solution.py:190
  63.4 4.7 %collective-permute-done.4.rest_4_ = bf16[448,256]{1,0:T(8,128)(2,1)S(1)} collective-permute-done((bf16[448,256]{1,0:T(8,128)(2,1)}, bf16[448,256]{1,0:T(8,128)(2,1)S(1)}, u32[]{:S(2)}, u32[]{:S(2)}) %collective-permute-start.4) | collective-permute-done | bytes 229408 | tf_op jit(solution)/shard_map/ppermute | solution.py:190
  68.1 5.7 %collective-permute-start.7 = (bf16[448,256]{1,0:T(8,128)(2,1)S(1)}, bf16[448,256]{1,0:T(8,128)(2,1)}, u32[]{:S(2)}, u32[]{:S(2)}) collective-permute-start(bf16[448,256]{1,0:T(8,128)(2,1)S(1)} %collective-permute-done.4.rest_4_), channel_id=1, source_target_pairs={{0,128},{64,192},{128,256},{192,320},{256,384},{320,448},{384,0},{... | collective-permute-start | bytes 688136 | tf_op jit(solution)/shard_map/ppermute | solution.py:190
  73.8 1.9 collective-permute-start.8
  76.4 1.9 collective-permute-start.6
  78.9 4.8 %turn.1.turned = bf16[3584,512]{1,0:T(8,128)(2,1)} custom-call(bf16[256,3584]{1,0:T(8,128)(2,1)} %bitcast.15, bf16[256,3584]{1,0:T(8,128)(2,1)} %collective-permute-done.tok_theirs), custom_call_target="tpu_custom_call" | custom-call | tf_op jit(solution)/shard_map/turn/pallas_call | solution.py:232
  83.8 4.3 %partial.1 = f32[512,256]{1,0:T(8,128)} custom-call(s32[2]{0:T(128)} %pad_add_fusion.place, bf16[256,3584]{1,0:T(8,128)(2,1)} %bitcast.16, bf16[256,3584]{1,0:T(8,128)(2,1)} %collective-permute-done.tok_theirs, bf16[448,256]{1,0:T(8,128)(2,1)} %get-tuple-element.32.rest_0_, bf16[448,256]{1,0:T(8,128)(2,1)} %copy-done.5, ...), custom_call_target="tpu_custom_call" | custom-call | tf_op jit(solution)/shard_map/partial/pallas_call | solution.py:240
  88.1 0.9 collective-permute-done.8.piece_theirs
  89.0 4.2 %project.1 = (bf16[512,256]{1,0:T(8,128)(2,1)}, bf16[448,256]{1,0:T(8,128)(2,1)}, bf16[448,256]{1,0:T(8,128)(2,1)}) custom-call(s32[2]{0:T(128)} %pad_add_fusion.place, f32[512,256]{1,0:T(8,128)} %partial.1, bf16[256,128]{1,0:T(8,128)(2,1)} %get-tuple-element.39.hid_mine, bf16[256,128]{1,0:T(8,128)(2,1)} %copy-done.8, ...), custom_call_target="tpu_custom_call" | custom-call | tf_op jit(solution)/shard_map/project/pallas_call | solution.py:248
  93.1 5.8 %collective-permute-start.9 = (bf16[448,256]{1,0:T(8,128)(2,1)}, bf16[448,256]{1,0:T(8,128)(2,1)S(1)}, u32[]{:S(2)}, u32[]{:S(2)}) collective-permute-start(bf16[448,256]{1,0:T(8,128)(2,1)} %get-tuple-element.18), channel_id=1, source_target_pairs={{0,128},{64,192},{128,256},{192,320},{256,384},{320,448},{384,0},{... | collective-permute-start | bytes 688136 | tf_op jit(solution)/shard_map/ppermute | solution.py:190
  98.9 3.8 %terms.1 = (bf16[448,256]{1,0:T(8,128)(2,1)}, bf16[448,256]{1,0:T(8,128)(2,1)}, bf16[448,256]{1,0:T(8,128)(2,1)}, bf16[448,256]{1,0:T(8,128)(2,1)}, bf16[448,256]{1,0:T(8,128)(2,1)}, /*index=5*/bf16[448,256]{1,0:T(8,128)(2,1)}) custom-call(s32[2]{0:T(128)} %pad_add_fusion.place, bf16[3584,512]{1,0:T(8,128)(2,1)} %turn.1.turned, ...), custom_call_target="tpu_custom_call" | custom-call | tf_op jit(solution)/shard_map/terms/pallas_call | solution.py:264
  102.7 2.0 collective-permute-start.10
  104.7 5.6 %collective-permute-start.13 = (bf16[448,256]{1,0:T(8,128)(2,1)}, bf16[448,256]{1,0:T(8,128)(2,1)S(1)}, u32[]{:S(2)}, u32[]{:S(2)}) collective-permute-start(bf16[448,256]{1,0:T(8,128)(2,1)} %get-tuple-element.28), channel_id=1, source_target_pairs={{0,384},{64,448},{128,0},{192,64},{256,128},{320,192},{384,256},{4... | collective-permute-start | bytes 688136 | tf_op jit(solution)/shard_map/ppermute | solution.py:190
  110.3 1.0 add_convert_fusion.3
  111.3 5.7 %collective-permute-start.11 = (bf16[448,256]{1,0:T(8,128)(2,1)S(1)}, bf16[448,256]{1,0:T(8,128)(2,1)S(1)}, u32[]{:S(2)}, u32[]{:S(2)}) collective-permute-start(bf16[448,256]{1,0:T(8,128)(2,1)S(1)} %add_convert_fusion.3), channel_id=1, source_target_pairs={{0,128},{64,192},{128,256},{192,320},{256,384},{320,448},{384,0},{... | collective-permute-start | bytes 688136 | tf_op jit(solution)/shard_map/ppermute | solution.py:190
  117.0 7.6 %collective-permute-done.13 = bf16[448,256]{1,0:T(8,128)(2,1)S(1)} collective-permute-done((bf16[448,256]{1,0:T(8,128)(2,1)}, bf16[448,256]{1,0:T(8,128)(2,1)S(1)}, u32[]{:S(2)}, u32[]{:S(2)}) %collective-permute-start.13) | collective-permute-done | bytes 229408 | tf_op jit(solution)/shard_map/ppermute | solution.py:190
  124.6 1.0 add_convert_fusion.1
  125.6 5.4 %collective-permute-start.14 = (bf16[448,256]{1,0:T(8,128)(2,1)S(1)}, bf16[448,256]{1,0:T(8,128)(2,1)S(1)}, u32[]{:S(2)}, u32[]{:S(2)}) collective-permute-start(bf16[448,256]{1,0:T(8,128)(2,1)S(1)} %add_convert_fusion.1), channel_id=1, source_target_pairs={{0,384},{64,448},{128,0},{192,64},{256,128},{320,192},{384,256},{4... | collective-permute-start | bytes 688136 | tf_op jit(solution)/shard_map/ppermute | solution.py:190
  131.0 2.5 %collective-permute-start.12 = (bf16[448,256]{1,0:T(8,128)(2,1)}, bf16[448,256]{1,0:T(8,128)(2,1)S(1)}, u32[]{:S(2)}, u32[]{:S(2)}) collective-permute-start(bf16[448,256]{1,0:T(8,128)(2,1)} %get-tuple-element.26), channel_id=1, source_target_pairs={{0,128},{64,192},{128,256},{192,320},{256,384},{320,448},{384,0},{... | collective-permute-start | bytes 688136 | tf_op jit(solution)/shard_map/ppermute | solution.py:190
  133.6 1.0 add_convert_fusion.2
  134.6 0.8 reshape.35
  135.4 15.6 %all-to-all-start.2 = ((bf16[64,7,256]{2,1,0:T(8,128)(2,1)}), bf16[64,7,256]{2,1,0:T(8,128)(2,1)S(1)}, u32[]{:S(2)}, u32[]{:S(2)}) async-start(bf16[64,7,256]{2,1,0:T(8,128)(2,1)} %reshape.35), calls=%async_computation.2 | async-start | bytes 524288 | tf_op jit(solution)/shard_map/all_to_all | solution.py:181
  151.1 1.9 collective-permute-start.15
  153.0 1.5 collective-permute-done.15
  155.3 8.1 %all-to-all-done.2 = bf16[64,7,256]{2,1,0:T(8,128)(2,1)S(1)} async-done(((bf16[64,7,256]{2,1,0:T(8,128)(2,1)}), bf16[64,7,256]{2,1,0:T(8,128)(2,1)S(1)}, u32[]{:S(2)}, u32[]{:S(2)}) %all-to-all-start.2) | async-done | bytes 229408 | tf_op jit(solution)/shard_map/all_to_all | solution.py:181
  163.4 4.6 %all-to-all-start.3 = ((bf16[64,7,256]{2,1,0:T(8,128)(2,1)}), bf16[64,7,256]{2,1,0:T(8,128)(2,1)S(1)}, u32[]{:S(2)}, u32[]{:S(2)}) async-start(bf16[64,7,256]{2,1,0:T(8,128)(2,1)} %reshape.36), calls=%async_computation.3 | async-start | bytes 524288 | tf_op jit(solution)/shard_map/all_to_all | solution.py:181
  168.3 12.7 %all-to-all-done.3 = bf16[64,7,256]{2,1,0:T(8,128)(2,1)S(1)} async-done(((bf16[64,7,256]{2,1,0:T(8,128)(2,1)}), bf16[64,7,256]{2,1,0:T(8,128)(2,1)S(1)}, u32[]{:S(2)}, u32[]{:S(2)}) %all-to-all-start.3) | async-done | bytes 229408 | tf_op jit(solution)/shard_map/all_to_all | solution.py:181
  181.3 1.1 copy.26
  182.3 4.6 %all-to-all-start.4 = ((bf16[64,7,512]{2,1,0:T(8,128)(2,1)}), bf16[64,7,512]{2,1,0:T(8,128)(2,1)S(1)}, u32[]{:S(2)}, u32[]{:S(2)}) async-start(bf16[64,7,512]{2,1,0:T(8,128)(2,1)} %copy.26), calls=%async_computation.4 | async-start | bytes 1048576 | tf_op jit(solution)/shard_map/all_to_all | solution.py:181
  187.2 0.9 reshape.33.first
  188.1 0.9 reshape.34.second
  189.0 16.6 %all-to-all-done.4 = bf16[64,7,512]{2,1,0:T(8,128)(2,1)S(1)} async-done(((bf16[64,7,512]{2,1,0:T(8,128)(2,1)}), bf16[64,7,512]{2,1,0:T(8,128)(2,1)S(1)}, u32[]{:S(2)}, u32[]{:S(2)}) %all-to-all-start.4) | async-done | bytes 458784 | tf_op jit(solution)/shard_map/all_to_all | solution.py:181
  205.6 0.9 reshape.37.gradient
  206.6 4.1 %adam.1 = (bf16[1,448,512]{2,1,0:T(8,128)(2,1)}, f32[1,448,512]{2,1,0:T(8,128)}, f32[1,448,512]{2,1,0:T(8,128)}) custom-call(s32[2]{0:T(128)} %pad_add_fusion.place, bf16[448,512]{1,0:T(8,128)(2,1)} %copy-done.1, bf16[448,512]{1,0:T(8,128)(2,1)} %reshape.33.first, bf16[448,512]{1,0:T(8,128)(2,1)} %reshape.34.second, bf16[448,512]{1,0:T(8,128)(2,1)} %reshape.37.gradient), custom_call_target="tpu_custom_call" | custom-call | tf_op jit(solution)/shard_map/adam/pallas_call | solution.py:289
  (51 shorter events, 3.7 us)
Async XLA Ops:
  0.6 18.2 %copy-start = (bf16[1,1,256,3584]{3,2,1,0:T(8,128)(2,1)S(1)}, bf16[1,1,256,3584]{3,2,1,0:T(8,128)(2,1)}, u32[]{:S(2)}) copy-start(bf16[1,1,256,3584]{3,2,1,0:T(8,128)(2,1)} %param.12) | copy-start | bytes 5505028
  0.6 20.1 %copy-start.3 = (f32[16,7,512]{2,0,1:T(8,128)S(1)}, f32[16,7,512]{2,0,1:T(8,128)}, u32[]{:S(2)}) copy-start(f32[16,7,512]{2,0,1:T(8,128)} %param.8) | copy-start | bytes 688132
  0.7 20.1 %copy-start.4 = (f32[16,7,512]{2,0,1:T(8,128)S(1)}, f32[16,7,512]{2,0,1:T(8,128)}, u32[]{:S(2)}) copy-start(f32[16,7,512]{2,0,1:T(8,128)} %param.9) | copy-start | bytes 688132
  2.7 18.2 %copy-start.9 = (s32[64]{0:T(128)S(1)}, s32[64]{0:T(128)}, u32[]{:S(2)}) copy-start(s32[64]{0:T(128)} %param.10) | copy-start | bytes 772
  3.7 33.9 %all-to-all-start = ((bf16[64,7,512]{2,1,0:T(8,128)(2,1)}), bf16[64,7,512]{2,1,0:T(8,128)(2,1)}, u32[]{:S(2)}, u32[]{:S(2)}) async-start(bf16[64,7,512]{2,1,0:T(8,128)(2,1)} %copy.22), calls=%async_computation | async-start | bytes 1048576 | tf_op jit(solution)/shard_map/all_to_all | solution.py:181
  18.8 57.6 %collective-permute-start = (bf16[256,3584]{1,0:T(8,128)(2,1)S(1)}, bf16[256,3584]{1,0:T(8,128)(2,1)}, u32[]{:S(2)}, u32[]{:S(2)}) collective-permute-start(bf16[256,3584]{1,0:T(8,128)(2,1)S(1)} %bitcast.18), channel_id=1, source_target_pairs={{0,64},{64,0},{128,192},{192,128},{256,320},{320,256},{384,448},{4... | collective-permute-start | bytes 5505032 | tf_op jit(solution)/shard_map/ppermute | solution.py:193
  38.8 6.3 %copy-start.1 = (bf16[448,512]{1,0:T(8,128)(2,1)}, bf16[448,512]{1,0:T(8,128)(2,1)S(1)}, u32[]{:S(2)}) copy-start(bf16[448,512]{1,0:T(8,128)(2,1)S(1)} %reshape.32.params) | copy-start | bytes 1376260
  40.4 15.0 %copy-start.7 = (bf16[1,1,256,256]{3,2,1,0:T(8,128)(2,1)S(1)}, bf16[1,1,256,256]{3,2,1,0:T(8,128)(2,1)}, u32[]{:S(2)}) copy-start(bf16[1,1,256,256]{3,2,1,0:T(8,128)(2,1)} %param.13) | copy-start | bytes 393220
  40.4 71.0 %all-to-all-start.1 = ((bf16[64,14,512]{2,1,0:T(8,128)(2,1)}), bf16[64,14,512]{2,1,0:T(8,128)(2,1)S(1)}, u32[]{:S(2)}, u32[]{:S(2)}) async-start(bf16[64,14,512]{2,1,0:T(8,128)(2,1)} %copy.23), calls=%async_computation.1 | async-start | bytes 2097152 | tf_op jit(solution)/shard_map/all_to_all | solution.py:181
  46.0 7.4 %collective-permute-start.1 = (bf16[448,256]{1,0:T(8,128)(2,1)}, bf16[448,256]{1,0:T(8,128)(2,1)S(1)}, u32[]{:S(2)}, u32[]{:S(2)}) collective-permute-start(bf16[448,256]{1,0:T(8,128)(2,1)} %get-tuple-element.31), channel_id=1, source_target_pairs={{0,64},{64,0},{128,192},{192,128},{256,320},{320,256},{384,448},{4... | collective-permute-start | bytes 688136 | tf_op jit(solution)/shard_map/ppermute | solution.py:193
  48.6 19.5 %collective-permute-start.4 = (bf16[448,256]{1,0:T(8,128)(2,1)}, bf16[448,256]{1,0:T(8,128)(2,1)S(1)}, u32[]{:S(2)}, u32[]{:S(2)}) collective-permute-start(bf16[448,256]{1,0:T(8,128)(2,1)} %get-tuple-element.32.rest_0_), channel_id=1, source_target_pairs={{0,128},{64,192},{128,256},{192,320},{256,384},{320,448},{384,0},{... | collective-permute-start | bytes 688136 | tf_op jit(solution)/shard_map/ppermute | solution.py:190
  53.4 30.4 %copy-start.5 = (bf16[448,256]{1,0:T(8,128)(2,1)}, bf16[448,256]{1,0:T(8,128)(2,1)S(1)}, u32[]{:S(2)}) copy-start(bf16[448,256]{1,0:T(8,128)(2,1)S(1)} %collective-permute-done.1.rest_1_) | copy-start | bytes 688132
  53.4 20.4 %collective-permute-start.3 = (bf16[448,256]{1,0:T(8,128)(2,1)S(1)}, bf16[448,256]{1,0:T(8,128)(2,1)}, u32[]{:S(2)}, u32[]{:S(2)}) collective-permute-start(bf16[448,256]{1,0:T(8,128)(2,1)S(1)} %collective-permute-done.1.rest_1_), channel_id=1, source_target_pairs={{0,384},{64,448},{128,0},{192,64},{256,128},{320,192},{384,256},{4... | collective-permute-start | bytes 688136 | tf_op jit(solution)/shard_map/ppermute | solution.py:190
  55.5 28.3 %collective-permute-start.2 = (bf16[448,256]{1,0:T(8,128)(2,1)}, bf16[448,256]{1,0:T(8,128)(2,1)}, u32[]{:S(2)}, u32[]{:S(2)}) collective-permute-start(bf16[448,256]{1,0:T(8,128)(2,1)} %get-tuple-element.32.rest_0_), channel_id=1, source_target_pairs={{0,384},{64,448},{128,0},{192,64},{256,128},{320,192},{384,256},{4... | collective-permute-start | bytes 688136 | tf_op jit(solution)/shard_map/ppermute | solution.py:190
  58.9 24.9 %collective-permute-start.5 = (bf16[448,256]{1,0:T(8,128)(2,1)S(1)}, bf16[448,256]{1,0:T(8,128)(2,1)}, u32[]{:S(2)}, u32[]{:S(2)}) collective-permute-start(bf16[448,256]{1,0:T(8,128)(2,1)S(1)} %collective-permute-done.1.rest_1_), channel_id=1, source_target_pairs={{0,128},{64,192},{128,256},{192,320},{256,384},{320,448},{384,0},{... | collective-permute-start | bytes 688136 | tf_op jit(solution)/shard_map/ppermute | solution.py:190
  68.1 15.7 %copy-start.6 = (bf16[448,256]{1,0:T(8,128)(2,1)}, bf16[448,256]{1,0:T(8,128)(2,1)S(1)}, u32[]{:S(2)}) copy-start(bf16[448,256]{1,0:T(8,128)(2,1)S(1)} %collective-permute-done.4.rest_4_) | copy-start | bytes 688132
  68.1 20.0 %collective-permute-start.7 = (bf16[448,256]{1,0:T(8,128)(2,1)S(1)}, bf16[448,256]{1,0:T(8,128)(2,1)}, u32[]{:S(2)}, u32[]{:S(2)}) collective-permute-start(bf16[448,256]{1,0:T(8,128)(2,1)S(1)} %collective-permute-done.4.rest_4_), channel_id=1, source_target_pairs={{0,128},{64,192},{128,256},{192,320},{256,384},{320,448},{384,0},{... | collective-permute-start | bytes 688136 | tf_op jit(solution)/shard_map/ppermute | solution.py:190
  73.8 15.2 %collective-permute-start.8 = (bf16[448,256]{1,0:T(8,128)(2,1)}, bf16[448,256]{1,0:T(8,128)(2,1)}, u32[]{:S(2)}, u32[]{:S(2)}) collective-permute-start(bf16[448,256]{1,0:T(8,128)(2,1)} %collective-permute-done.3.rest_3_), channel_id=1, source_target_pairs={{0,384},{64,448},{128,0},{192,64},{256,128},{320,192},{384,256},{4... | collective-permute-start | bytes 688136 | tf_op jit(solution)/shard_map/ppermute | solution.py:190
  76.4 11.7 %collective-permute-start.6 = (bf16[256,128]{1,0:T(8,128)(2,1)S(1)}, bf16[256,128]{1,0:T(8,128)(2,1)S(1)}, u32[]{:S(2)}, u32[]{:S(2)}) collective-permute-start(bf16[256,128]{1,0:T(8,128)(2,1)S(1)} %get-tuple-element.38), channel_id=1, source_target_pairs={{0,64},{64,0},{128,192},{192,128},{256,320},{320,256},{384,448},{4... | collective-permute-start | bytes 196616 | tf_op jit(solution)/shard_map/ppermute | solution.py:193
  88.1 0.9 copy-start.8
  93.1 17.2 %collective-permute-start.9 = (bf16[448,256]{1,0:T(8,128)(2,1)}, bf16[448,256]{1,0:T(8,128)(2,1)S(1)}, u32[]{:S(2)}, u32[]{:S(2)}) collective-permute-start(bf16[448,256]{1,0:T(8,128)(2,1)} %get-tuple-element.18), channel_id=1, source_target_pairs={{0,128},{64,192},{128,256},{192,320},{256,384},{320,448},{384,0},{... | collective-permute-start | bytes 688136 | tf_op jit(solution)/shard_map/ppermute | solution.py:190
  98.9 3.8 %copy-start.10 = (bf16[448,256]{1,0:T(8,128)(2,1)S(1)}, bf16[448,256]{1,0:T(8,128)(2,1)}, u32[]{:S(2)}) copy-start(bf16[448,256]{1,0:T(8,128)(2,1)} %get-tuple-element.23) | copy-start | bytes 688132
  102.7 48.3 %copy-start.2 = (bf16[448,256]{1,0:T(8,128)(2,1)S(1)}, bf16[448,256]{1,0:T(8,128)(2,1)}, u32[]{:S(2)}) copy-start(bf16[448,256]{1,0:T(8,128)(2,1)} %get-tuple-element.25) | copy-start | bytes 688132
  102.7 30.9 %collective-permute-start.10 = (bf16[448,256]{1,0:T(8,128)(2,1)S(1)}, bf16[448,256]{1,0:T(8,128)(2,1)S(1)}, u32[]{:S(2)}, u32[]{:S(2)}) collective-permute-start(bf16[448,256]{1,0:T(8,128)(2,1)S(1)} %copy-done.10), channel_id=1, source_target_pairs={{0,384},{64,448},{128,0},{192,64},{256,128},{320,192},{384,256},{4... | collective-permute-start | bytes 688136 | tf_op jit(solution)/shard_map/ppermute | solution.py:190
  104.7 19.9 %collective-permute-start.13 = (bf16[448,256]{1,0:T(8,128)(2,1)}, bf16[448,256]{1,0:T(8,128)(2,1)S(1)}, u32[]{:S(2)}, u32[]{:S(2)}) collective-permute-start(bf16[448,256]{1,0:T(8,128)(2,1)} %get-tuple-element.28), channel_id=1, source_target_pairs={{0,384},{64,448},{128,0},{192,64},{256,128},{320,192},{384,256},{4... | collective-permute-start | bytes 688136 | tf_op jit(solution)/shard_map/ppermute | solution.py:190
  111.3 22.2 %collective-permute-start.11 = (bf16[448,256]{1,0:T(8,128)(2,1)S(1)}, bf16[448,256]{1,0:T(8,128)(2,1)S(1)}, u32[]{:S(2)}, u32[]{:S(2)}) collective-permute-start(bf16[448,256]{1,0:T(8,128)(2,1)S(1)} %add_convert_fusion.3), channel_id=1, source_target_pairs={{0,128},{64,192},{128,256},{192,320},{256,384},{320,448},{384,0},{... | collective-permute-start | bytes 688136 | tf_op jit(solution)/shard_map/ppermute | solution.py:190
  125.6 25.4 %collective-permute-start.14 = (bf16[448,256]{1,0:T(8,128)(2,1)S(1)}, bf16[448,256]{1,0:T(8,128)(2,1)S(1)}, u32[]{:S(2)}, u32[]{:S(2)}) collective-permute-start(bf16[448,256]{1,0:T(8,128)(2,1)S(1)} %add_convert_fusion.1), channel_id=1, source_target_pairs={{0,384},{64,448},{128,0},{192,64},{256,128},{320,192},{384,256},{4... | collective-permute-start | bytes 688136 | tf_op jit(solution)/shard_map/ppermute | solution.py:190
  131.0 20.0 %collective-permute-start.12 = (bf16[448,256]{1,0:T(8,128)(2,1)}, bf16[448,256]{1,0:T(8,128)(2,1)S(1)}, u32[]{:S(2)}, u32[]{:S(2)}) collective-permute-start(bf16[448,256]{1,0:T(8,128)(2,1)} %get-tuple-element.26), channel_id=1, source_target_pairs={{0,128},{64,192},{128,256},{192,320},{256,384},{320,448},{384,0},{... | collective-permute-start | bytes 688136 | tf_op jit(solution)/shard_map/ppermute | solution.py:190
  135.4 28.0 %all-to-all-start.2 = ((bf16[64,7,256]{2,1,0:T(8,128)(2,1)}), bf16[64,7,256]{2,1,0:T(8,128)(2,1)S(1)}, u32[]{:S(2)}, u32[]{:S(2)}) async-start(bf16[64,7,256]{2,1,0:T(8,128)(2,1)} %reshape.35), calls=%async_computation.2 | async-start | bytes 524288 | tf_op jit(solution)/shard_map/all_to_all | solution.py:181
  151.1 3.4 %collective-permute-start.15 = (bf16[448,256]{1,0:T(8,128)(2,1)S(1)}, bf16[448,256]{1,0:T(8,128)(2,1)S(1)}, u32[]{:S(2)}, u32[]{:S(2)}) collective-permute-start(bf16[448,256]{1,0:T(8,128)(2,1)S(1)} %add_convert_fusion), channel_id=1, source_target_pairs={{0,64},{64,0},{128,192},{192,128},{256,320},{320,256},{384,448},{4... | collective-permute-start | bytes 688136 | tf_op jit(solution)/shard_map/ppermute | solution.py:193
  163.4 17.6 %all-to-all-start.3 = ((bf16[64,7,256]{2,1,0:T(8,128)(2,1)}), bf16[64,7,256]{2,1,0:T(8,128)(2,1)S(1)}, u32[]{:S(2)}, u32[]{:S(2)}) async-start(bf16[64,7,256]{2,1,0:T(8,128)(2,1)} %reshape.36), calls=%async_computation.3 | async-start | bytes 524288 | tf_op jit(solution)/shard_map/all_to_all | solution.py:181
  182.3 23.3 %all-to-all-start.4 = ((bf16[64,7,512]{2,1,0:T(8,128)(2,1)}), bf16[64,7,512]{2,1,0:T(8,128)(2,1)S(1)}, u32[]{:S(2)}, u32[]{:S(2)}) async-start(bf16[64,7,512]{2,1,0:T(8,128)(2,1)} %copy.26), calls=%async_computation.4 | async-start | bytes 1048576 | tf_op jit(solution)/shard_map/all_to_all | solution.py:181
where the time goes:
time: 212 us; the launch traced here: 211 us
  starting transfers between devices  102 us (48%)
  waiting for transfers between devices  68.3 us (32%)
  Pallas kernels  21.2 us (10%)
  local copies, waits for them, and re-layouts  11.1 us (5%)
  other arithmetic  4.68 us (2%)
    all_to_all x5, waiting for transfers between devices, exchange(): lax.all_to_all(values, 'expert', split_axis=0, concat_axis=0, tiled=True)  53.7 us
    ppermute x12, starting transfers between devices, shift(): return lax.ppermute(value, 'dp', pairs)  49.3 us
    all_to_all x5, starting transfers between devices, exchange(): lax.all_to_all(values, 'expert', split_axis=0, concat_axis=0, tiled=True)  44.7 us
    ppermute x12, waiting for transfers between devices, shift(): return lax.ppermute(value, 'dp', pairs)  13.1 us
    ppermute x4, starting transfers between devices, swap(): return lax.ppermute(value, 'dp', [(i, i ^ 1) for i in range(dp_count)])  7.66 us
    pallas_call x1, Pallas kernels, on_device(): pl.pallas_call(turn_kernel, in_specs=in_vmem(2), out_specs=in_vmem(1)[0],...  4.84 us
    pallas_call x1, Pallas kernels, on_device(): pl.pallas_call(partial_kernel, in_specs=in_smem() + in_vmem(8), out_specs...  4.27 us
  transfers between devices with their start and end apart: 21, of which 8 were waited for; matrix products, arithmetic and copies ran while one was open for 6% of the time, Pallas kernels for 8%

commit v1 on v0

--- a/solution.py
+++ b/solution.py
@@ -213,7 +213,8 @@
     live_mask = (jnp.arange(row_total) < BLOCK * block_counts[0, 0])[:, None]
     masked = jnp.where(live_mask, hidden_grad[0, 0], jnp.zeros((), narrow))
     hid_mine, hid_give = halves(masked)
-    own_rows = exchange(choose(pick, ordered(weights))).reshape(own_count, col_total)
+    arrived = exchange(choose(pick, ordered(weights)))
+    own_rows = arrived.reshape(own_count, col_total)
     mine, give = own_rows[:, :part_cols], own_rows[:, part_cols:]
     tok_theirs = swap(inputs)
     hid_theirs = swap(hid_give)
@@ -225,8 +226,9 @@
     far_mine = shift(plus_mine, 1)
     far_theirs = shift(minus_theirs, -1)
 
-    moments = ordered(jnp.concatenate([first_moment, second_moment], axis=1).astype(narrow))
-    moments_sent, _ = lax.optimization_barrier((choose(pick, moments), own_rows))
+    moments_sent = choose(
+        pick, ordered(jnp.concatenate([first_moment, second_moment], axis=1).astype(narrow))
+    )
     moments_here = exchange(moments_sent)
 
     turned = pl.pallas_call(

time: 212 us -> 210 us (level)
  starting transfers between devices: 102 us -> 98.6 us
where the time goes in v1:
time: 210 us; the launch traced here: 208 us
  starting transfers between devices  98.6 us (47%)
  waiting for transfers between devices  68.2 us (32%)
  Pallas kernels  21.2 us (10%)
  local copies, waits for them, and re-layouts  12 us (6%)
  other arithmetic  4.67 us (2%)
    all_to_all x5, waiting for transfers between devices, exchange(): lax.all_to_all(values, 'expert', split_axis=0, concat_axis=0, tiled=True)  52.2 us
    ppermute x12, starting transfers between devices, shift(): return lax.ppermute(value, 'dp', pairs)  47.3 us
    all_to_all x5, starting transfers between devices, exchange(): lax.all_to_all(values, 'expert', split_axis=0, concat_axis=0, tiled=True)  43.6 us
    ppermute x12, waiting for transfers between devices, shift(): return lax.ppermute(value, 'dp', pairs)  14.5 us
    ppermute x4, starting transfers between devices, swap(): return lax.ppermute(value, 'dp', [(i, i ^ 1) for i in range(dp_count)])  7.66 us
    pallas_call x1, Pallas kernels, on_device(): pl.pallas_call(turn_kernel, in_specs=in_vmem(2), out_specs=in_vmem(1)[0],...  4.84 us
    pallas_call x1, Pallas kernels, on_device(): pl.pallas_call(partial_kernel, in_specs=in_smem() + in_vmem(8), out_specs...  4.27 us
  transfers between devices with their start and end apart: 21, of which 8 were waited for; matrix products, arithmetic and copies ran while one was open for 6% of the time, Pallas kernels for 8%

profile of v1, /device:TPU:16, one launch (start us, length us, event | category | flops | bytes accessed | tf_op | source)
XLA Modules:
  0.0 208.4 jit_solution(16590193775998563191)
XLA Ops:
  0.7 1.0 fusion.32
  1.7 1.0 convolution_convert_fusion.1
  2.7 1.1 copy.22
  3.7 14.8 %all-to-all-start = ((bf16[64,7,512]{2,1,0:T(8,128)(2,1)}), bf16[64,7,512]{2,1,0:T(8,128)(2,1)S(1)}, u32[]{:S(2)}, u32[]{:S(2)}) async-start(bf16[64,7,512]{2,1,0:T(8,128)(2,1)} %copy.22), calls=%async_computation | async-start | bytes 1048576 | tf_op jit(solution)/shard_map/all_to_all | solution.py:181
  18.5 1.9 collective-permute-start
  21.1 1.5 copy.23
  22.6 14.9 %all-to-all-done = bf16[64,7,512]{2,1,0:T(8,128)(2,1)S(1)} async-done(((bf16[64,7,512]{2,1,0:T(8,128)(2,1)}), bf16[64,7,512]{2,1,0:T(8,128)(2,1)S(1)}, u32[]{:S(2)}, u32[]{:S(2)}) %all-to-all-start) | async-done | bytes 458784 | tf_op jit(solution)/shard_map/all_to_all | solution.py:181
  37.5 0.8 copy-done.2
  38.3 4.7 %all-to-all-start.1 = ((bf16[64,14,512]{2,1,0:T(8,128)(2,1)}), bf16[64,14,512]{2,1,0:T(8,128)(2,1)S(1)}, u32[]{:S(2)}, u32[]{:S(2)}) async-start(bf16[64,14,512]{2,1,0:T(8,128)(2,1)} %copy.23), calls=%async_computation.1 | async-start | bytes 2097152 | tf_op jit(solution)/shard_map/all_to_all | solution.py:181
  43.0 1.2 reshape.32.params
  44.2 0.9 fusion.31
  45.1 1.9 collective-permute-start.1
  47.7 4.8 %collective-permute-start.4 = (bf16[448,256]{1,0:T(8,128)(2,1)}, bf16[448,256]{1,0:T(8,128)(2,1)}, u32[]{:S(2)}, u32[]{:S(2)}) collective-permute-start(bf16[448,256]{1,0:T(8,128)(2,1)} %get-tuple-element.30.rest_0_), channel_id=1, source_target_pairs={{0,128},{64,192},{128,256},{192,320},{256,384},{320,448},{384,0},{... | collective-permute-start | bytes 688136 | tf_op jit(solution)/shard_map/ppermute | solution.py:190
  52.5 1.9 collective-permute-start.3
  54.5 3.5 %collective-permute-start.2 = (bf16[448,256]{1,0:T(8,128)(2,1)}, bf16[448,256]{1,0:T(8,128)(2,1)}, u32[]{:S(2)}, u32[]{:S(2)}) collective-permute-start(bf16[448,256]{1,0:T(8,128)(2,1)} %get-tuple-element.30.rest_0_), channel_id=1, source_target_pairs={{0,384},{64,448},{128,0},{192,64},{256,128},{320,192},{384,256},{4... | collective-permute-start | bytes 688136 | tf_op jit(solution)/shard_map/ppermute | solution.py:190
  58.0 4.5 %collective-permute-start.5 = (bf16[448,256]{1,0:T(8,128)(2,1)}, bf16[448,256]{1,0:T(8,128)(2,1)}, u32[]{:S(2)}, u32[]{:S(2)}) collective-permute-start(bf16[448,256]{1,0:T(8,128)(2,1)} %collective-permute-done.1.rest_1_), channel_id=1, source_target_pairs={{0,128},{64,192},{128,256},{192,320},{256,384},{320,448},{384,0},{... | collective-permute-start | bytes 688136 | tf_op jit(solution)/shard_map/ppermute | solution.py:190
  62.5 3.1 %collective-permute-done.4.rest_4_ = bf16[448,256]{1,0:T(8,128)(2,1)} collective-permute-done((bf16[448,256]{1,0:T(8,128)(2,1)}, bf16[448,256]{1,0:T(8,128)(2,1)}, u32[]{:S(2)}, u32[]{:S(2)}) %collective-permute-start.4) | collective-permute-done | bytes 229408 | tf_op jit(solution)/shard_map/ppermute | solution.py:190
  65.6 5.6 %collective-permute-start.7 = (bf16[448,256]{1,0:T(8,128)(2,1)}, bf16[448,256]{1,0:T(8,128)(2,1)}, u32[]{:S(2)}, u32[]{:S(2)}) collective-permute-start(bf16[448,256]{1,0:T(8,128)(2,1)} %collective-permute-done.4.rest_4_), channel_id=1, source_target_pairs={{0,128},{64,192},{128,256},{192,320},{256,384},{320,448},{384,0},{... | collective-permute-start | bytes 688136 | tf_op jit(solution)/shard_map/ppermute | solution.py:190
  71.2 1.9 collective-permute-start.8
  73.8 1.9 collective-permute-start.6
  76.3 4.8 %turn.1.turned = bf16[3584,512]{1,0:T(8,128)(2,1)} custom-call(bf16[256,3584]{1,0:T(8,128)(2,1)} %bitcast.15, bf16[256,3584]{1,0:T(8,128)(2,1)} %collective-permute-done.tok_theirs), custom_call_target="tpu_custom_call" | custom-call | tf_op jit(solution)/shard_map/turn/pallas_call | solution.py:234
  81.2 4.3 %partial.1 = f32[512,256]{1,0:T(8,128)} custom-call(s32[2]{0:T(128)} %pad_add_fusion.place, bf16[256,3584]{1,0:T(8,128)(2,1)} %bitcast.16, bf16[256,3584]{1,0:T(8,128)(2,1)} %collective-permute-done.tok_theirs, bf16[448,256]{1,0:T(8,128)(2,1)} %get-tuple-element.30.rest_0_, bf16[448,256]{1,0:T(8,128)(2,1)} %collective-permute-done.1.rest_1_, ...), custom_call_target="tpu_custom_call" | custom-call | tf_op jit(solution)/shard_map/partial/pallas_call | solution.py:242
  85.5 3.8 %collective-permute-done.8.piece_theirs = bf16[448,256]{1,0:T(8,128)(2,1)} collective-permute-done((bf16[448,256]{1,0:T(8,128)(2,1)}, bf16[448,256]{1,0:T(8,128)(2,1)}, u32[]{:S(2)}, u32[]{:S(2)}) %collective-permute-start.8) | collective-permute-done | bytes 229408 | tf_op jit(solution)/shard_map/ppermute | solution.py:190
  89.3 4.2 %project.1 = (bf16[512,256]{1,0:T(8,128)(2,1)}, bf16[448,256]{1,0:T(8,128)(2,1)}, bf16[448,256]{1,0:T(8,128)(2,1)}) custom-call(s32[2]{0:T(128)} %pad_add_fusion.place, f32[512,256]{1,0:T(8,128)} %partial.1, bf16[256,128]{1,0:T(8,128)(2,1)} %get-tuple-element.37.hid_mine, bf16[256,128]{1,0:T(8,128)(2,1)} %copy-done.7, ...), custom_call_target="tpu_custom_call" | custom-call | tf_op jit(solution)/shard_map/project/pallas_call | solution.py:250
  93.5 2.8 %collective-permute-start.9 = (bf16[448,256]{1,0:T(8,128)(2,1)}, bf16[448,256]{1,0:T(8,128)(2,1)S(1)}, u32[]{:S(2)}, u32[]{:S(2)}) collective-permute-start(bf16[448,256]{1,0:T(8,128)(2,1)} %get-tuple-element.17), channel_id=1, source_target_pairs={{0,128},{64,192},{128,256},{192,320},{256,384},{320,448},{384,0},{... | collective-permute-start | bytes 688136 | tf_op jit(solution)/shard_map/ppermute | solution.py:190
  96.3 3.8 %terms.1 = (bf16[448,256]{1,0:T(8,128)(2,1)}, bf16[448,256]{1,0:T(8,128)(2,1)}, bf16[448,256]{1,0:T(8,128)(2,1)}, bf16[448,256]{1,0:T(8,128)(2,1)}, bf16[448,256]{1,0:T(8,128)(2,1)}, /*index=5*/bf16[448,256]{1,0:T(8,128)(2,1)}) custom-call(s32[2]{0:T(128)} %pad_add_fusion.place, bf16[3584,512]{1,0:T(8,128)(2,1)} %turn.1.turned, ...), custom_call_target="tpu_custom_call" | custom-call | tf_op jit(solution)/shard_map/terms/pallas_call | solution.py:266
  100.1 4.1 %collective-permute-start.10 = (bf16[448,256]{1,0:T(8,128)(2,1)S(1)}, bf16[448,256]{1,0:T(8,128)(2,1)S(1)}, u32[]{:S(2)}, u32[]{:S(2)}) collective-permute-start(bf16[448,256]{1,0:T(8,128)(2,1)S(1)} %copy-done.9), channel_id=1, source_target_pairs={{0,384},{64,448},{128,0},{192,64},{256,128},{320,192},{384,256},{4... | collective-permute-start | bytes 688136 | tf_op jit(solution)/shard_map/ppermute | solution.py:190
  104.2 4.0 %collective-permute-start.13 = (bf16[448,256]{1,0:T(8,128)(2,1)}, bf16[448,256]{1,0:T(8,128)(2,1)S(1)}, u32[]{:S(2)}, u32[]{:S(2)}) collective-permute-start(bf16[448,256]{1,0:T(8,128)(2,1)} %get-tuple-element.26), channel_id=1, source_target_pairs={{0,384},{64,448},{128,0},{192,64},{256,128},{320,192},{384,256},{4... | collective-permute-start | bytes 688136 | tf_op jit(solution)/shard_map/ppermute | solution.py:190
  108.2 1.0 add_convert_fusion.3
  109.2 5.3 %collective-permute-start.11 = (bf16[448,256]{1,0:T(8,128)(2,1)S(1)}, bf16[448,256]{1,0:T(8,128)(2,1)S(1)}, u32[]{:S(2)}, u32[]{:S(2)}) collective-permute-start(bf16[448,256]{1,0:T(8,128)(2,1)S(1)} %add_convert_fusion.3), channel_id=1, source_target_pairs={{0,128},{64,192},{128,256},{192,320},{256,384},{320,448},{384,0},{... | collective-permute-start | bytes 688136 | tf_op jit(solution)/shard_map/ppermute | solution.py:190
  114.5 7.6 %collective-permute-done.13 = bf16[448,256]{1,0:T(8,128)(2,1)S(1)} collective-permute-done((bf16[448,256]{1,0:T(8,128)(2,1)}, bf16[448,256]{1,0:T(8,128)(2,1)S(1)}, u32[]{:S(2)}, u32[]{:S(2)}) %collective-permute-start.13) | collective-permute-done | bytes 229408 | tf_op jit(solution)/shard_map/ppermute | solution.py:190
  122.1 1.0 add_convert_fusion.1
  123.1 6.1 %collective-permute-start.14 = (bf16[448,256]{1,0:T(8,128)(2,1)S(1)}, bf16[448,256]{1,0:T(8,128)(2,1)S(1)}, u32[]{:S(2)}, u32[]{:S(2)}) collective-permute-start(bf16[448,256]{1,0:T(8,128)(2,1)S(1)} %add_convert_fusion.1), channel_id=1, source_target_pairs={{0,384},{64,448},{128,0},{192,64},{256,128},{320,192},{384,256},{4... | collective-permute-start | bytes 688136 | tf_op jit(solution)/shard_map/ppermute | solution.py:190
  129.2 2.8 %collective-permute-start.12 = (bf16[448,256]{1,0:T(8,128)(2,1)}, bf16[448,256]{1,0:T(8,128)(2,1)S(1)}, u32[]{:S(2)}, u32[]{:S(2)}) collective-permute-start(bf16[448,256]{1,0:T(8,128)(2,1)} %get-tuple-element.24), channel_id=1, source_target_pairs={{0,128},{64,192},{128,256},{192,320},{256,384},{320,448},{384,0},{... | collective-permute-start | bytes 688136 | tf_op jit(solution)/shard_map/ppermute | solution.py:190
  132.1 1.0 add_convert_fusion.2
  133.9 14.9 %all-to-all-start.2 = ((bf16[64,7,256]{2,1,0:T(8,128)(2,1)}), bf16[64,7,256]{2,1,0:T(8,128)(2,1)S(1)}, u32[]{:S(2)}, u32[]{:S(2)}) async-start(bf16[64,7,256]{2,1,0:T(8,128)(2,1)} %reshape.35), calls=%async_computation.2 | async-start | bytes 524288 | tf_op jit(solution)/shard_map/all_to_all | solution.py:181
  148.9 1.9 collective-permute-start.15
  150.8 1.5 collective-permute-done.15
  153.1 8.1 %all-to-all-done.2 = bf16[64,7,256]{2,1,0:T(8,128)(2,1)S(1)} async-done(((bf16[64,7,256]{2,1,0:T(8,128)(2,1)}), bf16[64,7,256]{2,1,0:T(8,128)(2,1)S(1)}, u32[]{:S(2)}, u32[]{:S(2)}) %all-to-all-start.2) | async-done | bytes 229408 | tf_op jit(solution)/shard_map/all_to_all | solution.py:181
  161.2 4.6 %all-to-all-start.3 = ((bf16[64,7,256]{2,1,0:T(8,128)(2,1)}), bf16[64,7,256]{2,1,0:T(8,128)(2,1)S(1)}, u32[]{:S(2)}, u32[]{:S(2)}) async-start(bf16[64,7,256]{2,1,0:T(8,128)(2,1)} %reshape.36), calls=%async_computation.3 | async-start | bytes 524288 | tf_op jit(solution)/shard_map/all_to_all | solution.py:181
  166.1 12.6 %all-to-all-done.3 = bf16[64,7,256]{2,1,0:T(8,128)(2,1)S(1)} async-done(((bf16[64,7,256]{2,1,0:T(8,128)(2,1)}), bf16[64,7,256]{2,1,0:T(8,128)(2,1)S(1)}, u32[]{:S(2)}, u32[]{:S(2)}) %all-to-all-start.3) | async-done | bytes 229408 | tf_op jit(solution)/shard_map/all_to_all | solution.py:181
  179.0 1.1 copy.26
  180.0 4.6 %all-to-all-start.4 = ((bf16[64,7,512]{2,1,0:T(8,128)(2,1)}), bf16[64,7,512]{2,1,0:T(8,128)(2,1)S(1)}, u32[]{:S(2)}, u32[]{:S(2)}) async-start(bf16[64,7,512]{2,1,0:T(8,128)(2,1)} %copy.26), calls=%async_computation.4 | async-start | bytes 1048576 | tf_op jit(solution)/shard_map/all_to_all | solution.py:181
  184.9 0.9 reshape.33.first
  185.8 0.9 reshape.34.second
  186.7 16.6 %all-to-all-done.4 = bf16[64,7,512]{2,1,0:T(8,128)(2,1)S(1)} async-done(((bf16[64,7,512]{2,1,0:T(8,128)(2,1)}), bf16[64,7,512]{2,1,0:T(8,128)(2,1)S(1)}, u32[]{:S(2)}, u32[]{:S(2)}) %all-to-all-start.4) | async-done | bytes 458784 | tf_op jit(solution)/shard_map/all_to_all | solution.py:181
  203.3 0.9 reshape.37.gradient
  204.2 4.1 %adam.1 = (bf16[1,448,512]{2,1,0:T(8,128)(2,1)}, f32[1,448,512]{2,1,0:T(8,128)}, f32[1,448,512]{2,1,0:T(8,128)}) custom-call(s32[2]{0:T(128)} %pad_add_fusion.place, bf16[448,512]{1,0:T(8,128)(2,1)} %copy-done.1, bf16[448,512]{1,0:T(8,128)(2,1)} %reshape.33.first, bf16[448,512]{1,0:T(8,128)(2,1)} %reshape.34.second, bf16[448,512]{1,0:T(8,128)(2,1)} %reshape.37.gradient), custom_call_target="tpu_custom_call" | custom-call | tf_op jit(solution)/shard_map/adam/pallas_call | solution.py:291
  (49 shorter events, 4.4 us)
Async XLA Ops:
  0.6 17.9 %copy-start = (bf16[1,1,256,3584]{3,2,1,0:T(8,128)(2,1)S(1)}, bf16[1,1,256,3584]{3,2,1,0:T(8,128)(2,1)}, u32[]{:S(2)}) copy-start(bf16[1,1,256,3584]{3,2,1,0:T(8,128)(2,1)} %param.12) | copy-start | bytes 5505028
  0.6 19.8 %copy-start.4 = (f32[16,7,512]{2,0,1:T(8,128)S(1)}, f32[16,7,512]{2,0,1:T(8,128)}, u32[]{:S(2)}) copy-start(f32[16,7,512]{2,0,1:T(8,128)} %param.8) | copy-start | bytes 688132
  0.7 19.9 %copy-start.5 = (f32[16,7,512]{2,0,1:T(8,128)S(1)}, f32[16,7,512]{2,0,1:T(8,128)}, u32[]{:S(2)}) copy-start(f32[16,7,512]{2,0,1:T(8,128)} %param.9) | copy-start | bytes 688132
  2.7 18.0 %copy-start.8 = (s32[64]{0:T(128)S(1)}, s32[64]{0:T(128)}, u32[]{:S(2)}) copy-start(s32[64]{0:T(128)} %param.10) | copy-start | bytes 772
  3.7 33.8 %all-to-all-start = ((bf16[64,7,512]{2,1,0:T(8,128)(2,1)}), bf16[64,7,512]{2,1,0:T(8,128)(2,1)S(1)}, u32[]{:S(2)}, u32[]{:S(2)}) async-start(bf16[64,7,512]{2,1,0:T(8,128)(2,1)} %copy.22), calls=%async_computation | async-start | bytes 1048576 | tf_op jit(solution)/shard_map/all_to_all | solution.py:181
  18.5 55.2 %collective-permute-start = (bf16[256,3584]{1,0:T(8,128)(2,1)S(1)}, bf16[256,3584]{1,0:T(8,128)(2,1)}, u32[]{:S(2)}, u32[]{:S(2)}) collective-permute-start(bf16[256,3584]{1,0:T(8,128)(2,1)S(1)} %bitcast.18), channel_id=1, source_target_pairs={{0,64},{64,0},{128,192},{192,128},{256,320},{320,256},{384,448},{4... | collective-permute-start | bytes 5505032 | tf_op jit(solution)/shard_map/ppermute | solution.py:193
  22.6 31.8 %copy-start.6 = (bf16[1,1,256,256]{3,2,1,0:T(8,128)(2,1)S(1)}, bf16[1,1,256,256]{3,2,1,0:T(8,128)(2,1)}, u32[]{:S(2)}) copy-start(bf16[1,1,256,256]{3,2,1,0:T(8,128)(2,1)} %param.13) | copy-start | bytes 393220
  37.5 0.8 copy-start.2
  38.3 70.9 %all-to-all-start.1 = ((bf16[64,14,512]{2,1,0:T(8,128)(2,1)}), bf16[64,14,512]{2,1,0:T(8,128)(2,1)S(1)}, u32[]{:S(2)}, u32[]{:S(2)}) async-start(bf16[64,14,512]{2,1,0:T(8,128)(2,1)} %copy.23), calls=%async_computation.1 | async-start | bytes 2097152 | tf_op jit(solution)/shard_map/all_to_all | solution.py:181
  44.2 37.0 %copy-start.1 = (bf16[448,512]{1,0:T(8,128)(2,1)}, bf16[448,512]{1,0:T(8,128)(2,1)S(1)}, u32[]{:S(2)}) copy-start(bf16[448,512]{1,0:T(8,128)(2,1)S(1)} %reshape.32.params) | copy-start | bytes 1376260
  45.1 7.4 %collective-permute-start.1 = (bf16[448,256]{1,0:T(8,128)(2,1)}, bf16[448,256]{1,0:T(8,128)(2,1)}, u32[]{:S(2)}, u32[]{:S(2)}) collective-permute-start(bf16[448,256]{1,0:T(8,128)(2,1)} %get-tuple-element.29), channel_id=1, source_target_pairs={{0,64},{64,0},{128,192},{192,128},{256,320},{320,256},{384,448},{4... | collective-permute-start | bytes 688136 | tf_op jit(solution)/shard_map/ppermute | solution.py:193
  47.7 17.9 %collective-permute-start.4 = (bf16[448,256]{1,0:T(8,128)(2,1)}, bf16[448,256]{1,0:T(8,128)(2,1)}, u32[]{:S(2)}, u32[]{:S(2)}) collective-permute-start(bf16[448,256]{1,0:T(8,128)(2,1)} %get-tuple-element.30.rest_0_), channel_id=1, source_target_pairs={{0,128},{64,192},{128,256},{192,320},{256,384},{320,448},{384,0},{... | collective-permute-start | bytes 688136 | tf_op jit(solution)/shard_map/ppermute | solution.py:190
  52.5 18.7 %collective-permute-start.3 = (bf16[448,256]{1,0:T(8,128)(2,1)}, bf16[448,256]{1,0:T(8,128)(2,1)}, u32[]{:S(2)}, u32[]{:S(2)}) collective-permute-start(bf16[448,256]{1,0:T(8,128)(2,1)} %collective-permute-done.1.rest_1_), channel_id=1, source_target_pairs={{0,384},{64,448},{128,0},{192,64},{256,128},{320,192},{384,256},{4... | collective-permute-start | bytes 688136 | tf_op jit(solution)/shard_map/ppermute | solution.py:190
  54.5 26.6 %collective-permute-start.2 = (bf16[448,256]{1,0:T(8,128)(2,1)}, bf16[448,256]{1,0:T(8,128)(2,1)}, u32[]{:S(2)}, u32[]{:S(2)}) collective-permute-start(bf16[448,256]{1,0:T(8,128)(2,1)} %get-tuple-element.30.rest_0_), channel_id=1, source_target_pairs={{0,384},{64,448},{128,0},{192,64},{256,128},{320,192},{384,256},{4... | collective-permute-start | bytes 688136 | tf_op jit(solution)/shard_map/ppermute | solution.py:190
  58.0 23.2 %collective-permute-start.5 = (bf16[448,256]{1,0:T(8,128)(2,1)}, bf16[448,256]{1,0:T(8,128)(2,1)}, u32[]{:S(2)}, u32[]{:S(2)}) collective-permute-start(bf16[448,256]{1,0:T(8,128)(2,1)} %collective-permute-done.1.rest_1_), channel_id=1, source_target_pairs={{0,128},{64,192},{128,256},{192,320},{256,384},{320,448},{384,0},{... | collective-permute-start | bytes 688136 | tf_op jit(solution)/shard_map/ppermute | solution.py:190
  65.6 19.9 %collective-permute-start.7 = (bf16[448,256]{1,0:T(8,128)(2,1)}, bf16[448,256]{1,0:T(8,128)(2,1)}, u32[]{:S(2)}, u32[]{:S(2)}) collective-permute-start(bf16[448,256]{1,0:T(8,128)(2,1)} %collective-permute-done.4.rest_4_), channel_id=1, source_target_pairs={{0,128},{64,192},{128,256},{192,320},{256,384},{320,448},{384,0},{... | collective-permute-start | bytes 688136 | tf_op jit(solution)/shard_map/ppermute | solution.py:190
  71.2 18.1 %collective-permute-start.8 = (bf16[448,256]{1,0:T(8,128)(2,1)}, bf16[448,256]{1,0:T(8,128)(2,1)}, u32[]{:S(2)}, u32[]{:S(2)}) collective-permute-start(bf16[448,256]{1,0:T(8,128)(2,1)} %collective-permute-done.3.rest_3_), channel_id=1, source_target_pairs={{0,384},{64,448},{128,0},{192,64},{256,128},{320,192},{384,256},{4... | collective-permute-start | bytes 688136 | tf_op jit(solution)/shard_map/ppermute | solution.py:190
  73.8 11.7 %collective-permute-start.6 = (bf16[256,128]{1,0:T(8,128)(2,1)S(1)}, bf16[256,128]{1,0:T(8,128)(2,1)S(1)}, u32[]{:S(2)}, u32[]{:S(2)}) collective-permute-start(bf16[256,128]{1,0:T(8,128)(2,1)S(1)} %get-tuple-element.36), channel_id=1, source_target_pairs={{0,64},{64,0},{128,192},{192,128},{256,320},{320,256},{384,448},{4... | collective-permute-start | bytes 196616 | tf_op jit(solution)/shard_map/ppermute | solution.py:193
  85.5 3.8 %copy-start.7 = (bf16[256,128]{1,0:T(8,128)(2,1)}, bf16[256,128]{1,0:T(8,128)(2,1)S(1)}, u32[]{:S(2)}) copy-start(bf16[256,128]{1,0:T(8,128)(2,1)S(1)} %collective-permute-done.6.hid_theirs) | copy-start | bytes 196612
  93.5 14.7 %collective-permute-start.9 = (bf16[448,256]{1,0:T(8,128)(2,1)}, bf16[448,256]{1,0:T(8,128)(2,1)S(1)}, u32[]{:S(2)}, u32[]{:S(2)}) collective-permute-start(bf16[448,256]{1,0:T(8,128)(2,1)} %get-tuple-element.17), channel_id=1, source_target_pairs={{0,128},{64,192},{128,256},{192,320},{256,384},{320,448},{384,0},{... | collective-permute-start | bytes 688136 | tf_op jit(solution)/shard_map/ppermute | solution.py:190
  96.3 3.8 %copy-start.9 = (bf16[448,256]{1,0:T(8,128)(2,1)S(1)}, bf16[448,256]{1,0:T(8,128)(2,1)}, u32[]{:S(2)}) copy-start(bf16[448,256]{1,0:T(8,128)(2,1)} %get-tuple-element.21) | copy-start | bytes 688132
  100.1 48.7 %copy-start.3 = (bf16[448,256]{1,0:T(8,128)(2,1)S(1)}, bf16[448,256]{1,0:T(8,128)(2,1)}, u32[]{:S(2)}) copy-start(bf16[448,256]{1,0:T(8,128)(2,1)} %get-tuple-element.23) | copy-start | bytes 688132
  100.1 32.0 %collective-permute-start.10 = (bf16[448,256]{1,0:T(8,128)(2,1)S(1)}, bf16[448,256]{1,0:T(8,128)(2,1)S(1)}, u32[]{:S(2)}, u32[]{:S(2)}) collective-permute-start(bf16[448,256]{1,0:T(8,128)(2,1)S(1)} %copy-done.9), channel_id=1, source_target_pairs={{0,384},{64,448},{128,0},{192,64},{256,128},{320,192},{384,256},{4... | collective-permute-start | bytes 688136 | tf_op jit(solution)/shard_map/ppermute | solution.py:190
  104.2 18.0 %collective-permute-start.13 = (bf16[448,256]{1,0:T(8,128)(2,1)}, bf16[448,256]{1,0:T(8,128)(2,1)S(1)}, u32[]{:S(2)}, u32[]{:S(2)}) collective-permute-start(bf16[448,256]{1,0:T(8,128)(2,1)} %get-tuple-element.26), channel_id=1, source_target_pairs={{0,384},{64,448},{128,0},{192,64},{256,128},{320,192},{384,256},{4... | collective-permute-start | bytes 688136 | tf_op jit(solution)/shard_map/ppermute | solution.py:190
  109.2 22.9 %collective-permute-start.11 = (bf16[448,256]{1,0:T(8,128)(2,1)S(1)}, bf16[448,256]{1,0:T(8,128)(2,1)S(1)}, u32[]{:S(2)}, u32[]{:S(2)}) collective-permute-start(bf16[448,256]{1,0:T(8,128)(2,1)S(1)} %add_convert_fusion.3), channel_id=1, source_target_pairs={{0,128},{64,192},{128,256},{192,320},{256,384},{320,448},{384,0},{... | collective-permute-start | bytes 688136 | tf_op jit(solution)/shard_map/ppermute | solution.py:190
  123.1 25.7 %collective-permute-start.14 = (bf16[448,256]{1,0:T(8,128)(2,1)S(1)}, bf16[448,256]{1,0:T(8,128)(2,1)S(1)}, u32[]{:S(2)}, u32[]{:S(2)}) collective-permute-start(bf16[448,256]{1,0:T(8,128)(2,1)S(1)} %add_convert_fusion.1), channel_id=1, source_target_pairs={{0,384},{64,448},{128,0},{192,64},{256,128},{320,192},{384,256},{4... | collective-permute-start | bytes 688136 | tf_op jit(solution)/shard_map/ppermute | solution.py:190
  129.2 19.6 %collective-permute-start.12 = (bf16[448,256]{1,0:T(8,128)(2,1)}, bf16[448,256]{1,0:T(8,128)(2,1)S(1)}, u32[]{:S(2)}, u32[]{:S(2)}) collective-permute-start(bf16[448,256]{1,0:T(8,128)(2,1)} %get-tuple-element.24), channel_id=1, source_target_pairs={{0,128},{64,192},{128,256},{192,320},{256,384},{320,448},{384,0},{... | collective-permute-start | bytes 688136 | tf_op jit(solution)/shard_map/ppermute | solution.py:190
  133.9 27.3 %all-to-all-start.2 = ((bf16[64,7,256]{2,1,0:T(8,128)(2,1)}), bf16[64,7,256]{2,1,0:T(8,128)(2,1)S(1)}, u32[]{:S(2)}, u32[]{:S(2)}) async-start(bf16[64,7,256]{2,1,0:T(8,128)(2,1)} %reshape.35), calls=%async_computation.2 | async-start | bytes 524288 | tf_op jit(solution)/shard_map/all_to_all | solution.py:181
  148.9 3.4 %collective-permute-start.15 = (bf16[448,256]{1,0:T(8,128)(2,1)S(1)}, bf16[448,256]{1,0:T(8,128)(2,1)S(1)}, u32[]{:S(2)}, u32[]{:S(2)}) collective-permute-start(bf16[448,256]{1,0:T(8,128)(2,1)S(1)} %add_convert_fusion), channel_id=1, source_target_pairs={{0,64},{64,0},{128,192},{192,128},{256,320},{320,256},{384,448},{4... | collective-permute-start | bytes 688136 | tf_op jit(solution)/shard_map/ppermute | solution.py:193
  161.2 17.5 %all-to-all-start.3 = ((bf16[64,7,256]{2,1,0:T(8,128)(2,1)}), bf16[64,7,256]{2,1,0:T(8,128)(2,1)S(1)}, u32[]{:S(2)}, u32[]{:S(2)}) async-start(bf16[64,7,256]{2,1,0:T(8,128)(2,1)} %reshape.36), calls=%async_computation.3 | async-start | bytes 524288 | tf_op jit(solution)/shard_map/all_to_all | solution.py:181
  180.0 23.3 %all-to-all-start.4 = ((bf16[64,7,512]{2,1,0:T(8,128)(2,1)}), bf16[64,7,512]{2,1,0:T(8,128)(2,1)S(1)}, u32[]{:S(2)}, u32[]{:S(2)}) async-start(bf16[64,7,512]{2,1,0:T(8,128)(2,1)} %copy.26), calls=%async_computation.4 | async-start | bytes 1048576 | tf_op jit(solution)/shard_map/all_to_all | solution.py:181

commit v2 on v1

--- a/solution.py
+++ b/solution.py
@@ -81,7 +81,7 @@
 
 def project_kernel(
     place, partial, hid_mine, hid_theirs, piece_mine, piece_theirs, tok_mine, tok_theirs, turned,
-    grad_ref, far_mine, last_mine, block, far_tok, far_rows, last_rows, sems,
+    grad_ref, far_mine, far_theirs, block, far_tok, far_rows, other_rows, sems,
 ):
     count = piece_mine.shape[0]
     half = hid_mine.shape[0]
@@ -93,7 +93,7 @@
             turned.at[pl.ds(piece_start(place, 2, 0, count), count)], far_rows, sems.at[2]
         ),
         pltpu.make_async_copy(
-            turned.at[pl.ds(piece_start(place, 3, 0, count), count)], last_rows, sems.at[3]
+            turned.at[pl.ds(piece_start(place, 2, 1, count), count)], other_rows, sems.at[3]
         ),
     ]
     for copy in copies:
@@ -113,7 +113,7 @@
     copies[3].wait()
     grads = grad_ref[...]
     far_mine[...] = jnp.dot(far_rows[...], grads, preferred_element_type=jnp.float32).astype(jnp.bfloat16)
-    last_mine[...] = jnp.dot(last_rows[...], grads, preferred_element_type=jnp.float32).astype(jnp.bfloat16)
+    far_theirs[...] = jnp.dot(other_rows[...], grads, preferred_element_type=jnp.float32).astype(jnp.bfloat16)
 
 
 def turn_kernel(tok_mine, tok_theirs, turned):
@@ -125,7 +125,7 @@
 
 def term_kernel(place, turned, grad_ref, *outs):
     count = outs[0].shape[0]
-    for slot, (step, side) in enumerate(((2, 1), (1, 0), (1, 1), (3, 1), (0, 0), (0, 1))):
+    for slot, (step, side) in enumerate(((1, 0), (1, 1), (3, 0), (3, 1), (0, 0), (0, 1))):
         outs[slot][...] = term_rows(turned, grad_ref, piece_start(place, step, side, count), count)
 
 
@@ -226,10 +226,18 @@
     far_mine = shift(plus_mine, 1)
     far_theirs = shift(minus_theirs, -1)
 
-    moments_sent = choose(
-        pick, ordered(jnp.concatenate([first_moment, second_moment], axis=1).astype(narrow))
+    stored = ordered(jnp.concatenate([first_moment, second_moment], axis=1).astype(narrow))
+    group = expert_count // 2
+    beside = lax.ppermute(stored, "expert", [(e, (e + group) % expert_count) for e in range(expert_count)])
+    upper = lax.axis_index("expert") // group
+    low = jnp.where(upper == 0, stored, beside)
+    high = jnp.where(upper == 0, beside, stored)
+    group_pick = lax.dynamic_slice_in_dim(pick, upper * group, group, 0)
+    moments_sent = choose(group_pick, jnp.concatenate([low, high], axis=1))
+    moments_here = lax.all_to_all(
+        moments_sent, "expert", split_axis=0, concat_axis=0, tiled=True,
+        axis_index_groups=[list(range(group)), list(range(group, expert_count))],
     )
-    moments_here = exchange(moments_sent)
 
     turned = pl.pallas_call(
         turn_kernel,
@@ -247,7 +255,7 @@
         scratch_shapes=[pltpu.VMEM((3, 2 * own_count, part_cols), narrow)],
         name="partial",
     )(place, inputs, tok_theirs, mine, theirs, minus_mine, minus_theirs, plus_mine, plus_theirs)
-    grad_proj, send_mine, last_mine = pl.pallas_call(
+    grad_proj, send_mine, send_theirs = pl.pallas_call(
         project_kernel,
         in_specs=in_smem() + in_vmem(5) + in_any(3),
         out_specs=in_vmem(3),
@@ -262,27 +270,31 @@
         name="project",
     )(place, partial, hid_mine, hid_theirs, far_mine, far_theirs, inputs, tok_theirs, turned)
     got_plus = shift(send_mine, 1)
-    early_mine = shift(last_mine, -1)
-    send_theirs, next_mine, next_theirs, last_theirs, sum_mine, sum_theirs = pl.pallas_call(
+    got_minus = shift(send_theirs, -1)
+    next_mine, next_theirs, last_mine, last_theirs, sum_mine, sum_theirs = pl.pallas_call(
         term_kernel,
         in_specs=in_smem() + in_vmem(2),
         out_specs=in_vmem(6),
         out_shape=[piece] * 6,
         name="terms",
     )(place, turned, grad_proj)
-    got_minus = shift(send_theirs, -1)
-    late_sent, next_theirs, moments_here = lax.optimization_barrier(
-        (add(next_mine, got_plus), next_theirs, moments_here)
-    )
-    late_mine = shift(late_sent, 1)
     early_theirs = shift(next_theirs, 1)
+    early_mine = shift(last_mine, -1)
+    late_mine = shift(add(next_mine, got_plus), 1)
     late_theirs = shift(add(last_theirs, got_minus), -1)
-    total_mine = add(sum_mine, early_mine, late_mine)
-    home_mine = exchange(total_mine.reshape(expert_count, span_rows, part_cols))
+    late_mine, late_theirs, moments_here = lax.optimization_barrier((late_mine, late_theirs, moments_here))
     total_other = swap(add(sum_theirs, early_theirs, late_theirs))
-    home_other = exchange(total_other.reshape(expert_count, span_rows, part_cols))
-    sums = jnp.concatenate([choose(same, home_mine), choose(same, home_other)], axis=-1)
-    grad_rows = rows_of(exchange(sums))
+    total = jnp.concatenate([add(sum_mine, early_mine, late_mine), total_other], axis=1)
+    home = exchange(total.reshape(expert_count, span_rows, col_total))
+
+    def moment_rows(kind):
+        sides = [
+            moments_here[:, (2 * side + kind) * span_rows : (2 * side + kind + 1) * span_rows]
+            for side in range(2)
+        ]
+        return rows_of(jnp.concatenate(sides, axis=0))
+
+    grad_rows = rows_of(exchange(choose(same, home)))
     bands = chip_count
     band = own_count // bands
     spec = pl.BlockSpec((band, col_total), lambda i: (i, 0))
@@ -300,8 +312,7 @@
         ],
         name="adam",
     )(
-        place, own_rows, rows_of(moments_here[:, :span_rows]), rows_of(moments_here[:, span_rows:]),
-        grad_rows,
+        place, own_rows, moment_rows(0), moment_rows(1), grad_rows,
     )
 
 

time: 210 us -> 205 us (0.976)
  blocking collectives: 0 us -> 29.5 us
  starting transfers between devices: 98.6 us -> 82.1 us
  waiting for transfers between devices: 68.2 us -> 51.8 us
    all_to_all x5 -> x2, waiting for transfers between devices: 52.2 us -> 21.3 us  [exchange(): lax.all_to_all(values, 'expert', split_axis=0, concat_axis=0, tiled=True)]
    all_to_all x0 -> x1, blocking collectives: none -> 29.5 us  [exchange(): lax.all_to_all(values, 'expert', split_axis=0, concat_axis=0, tiled=True)]
    all_to_all x5 -> x2, starting transfers between devices: 43.6 us -> 19.6 us  [exchange(): lax.all_to_all(values, 'expert', split_axis=0, concat_axis=0, tiled=True)]
    ppermute x12, waiting for transfers between devices: 14.5 us -> 23.7 us  [shift(): return lax.ppermute(value, 'dp', pairs)]
    ppermute x0 -> x1, waiting for transfers between devices: none -> 6.41 us  [on_device(): lax.ppermute(stored, 'expert', [(e, (e + group) % expert_count) for e in...]
    all_to_all x0 -> x1, starting transfers between devices: none -> 4.85 us  [on_device(): lax.all_to_all(moments_sent, 'expert', split_axis=0, concat_axis=0, tiled...]
    ppermute x0 -> x1, starting transfers between devices: none -> 3.58 us  [on_device(): lax.ppermute(stored, 'expert', [(e, (e + group) % expert_count) for e in...]
  transfers between devices with their start and end apart: 21 -> 20, of which waited for: 8 -> 10; matrix products, arithmetic and copies ran while one was open for 6% -> 5% of each run, Pallas kernels for 8% -> 8%
where the time goes in v2:
time: 205 us; the launch traced here: 204 us
  starting transfers between devices  82.1 us (40%)
  waiting for transfers between devices  51.8 us (25%)
  blocking collectives  29.5 us (14%)
  Pallas kernels  21.2 us (10%)
  local copies, waits for them, and re-layouts  10.6 us (5%)
  other arithmetic  4.99 us (2%)
    ppermute x12, starting transfers between devices, shift(): return lax.ppermute(value, 'dp', pairs)  46.4 us
    all_to_all x1, blocking collectives, exchange(): lax.all_to_all(values, 'expert', split_axis=0, concat_axis=0, tiled=True)  29.5 us
    ppermute x12, waiting for transfers between devices, shift(): return lax.ppermute(value, 'dp', pairs)  23.7 us
    all_to_all x2, waiting for transfers between devices, exchange(): lax.all_to_all(values, 'expert', split_axis=0, concat_axis=0, tiled=True)  21.3 us
    all_to_all x2, starting transfers between devices, exchange(): lax.all_to_all(values, 'expert', split_axis=0, concat_axis=0, tiled=True)  19.6 us
    ppermute x4, starting transfers between devices, swap(): return lax.ppermute(value, 'dp', [(i, i ^ 1) for i in range(dp_count)])  7.66 us
    ppermute x1, waiting for transfers between devices, on_device(): lax.ppermute(stored, 'expert', [(e, (e + group) % expert_count) for e in...  6.41 us
    all_to_all x1, starting transfers between devices, on_device(): lax.all_to_all(moments_sent, 'expert', split_axis=0, concat_axis=0, tiled...  4.85 us
  transfers between devices with their start and end apart: 20, of which 10 were waited for; matrix products, arithmetic and copies ran while one was open for 5% of the time, Pallas kernels for 8%

profile of v2, /device:TPU:16, one launch (start us, length us, event | category | flops | bytes accessed | tf_op | source)
XLA Modules:
  0.0 203.8 jit_solution(11083225058530855599)
XLA Ops:
  0.7 1.0 fusion.26
  1.7 1.0 convolution_convert_fusion.1
  2.7 1.1 copy.20
  3.7 14.9 %all-to-all-start = ((bf16[64,7,512]{2,1,0:T(8,128)(2,1)}), bf16[64,7,512]{2,1,0:T(8,128)(2,1)S(1)}, u32[]{:S(2)}, u32[]{:S(2)}) async-start(bf16[64,7,512]{2,1,0:T(8,128)(2,1)} %copy.20), calls=%async_computation | async-start | bytes 1048576 | tf_op jit(solution)/shard_map/all_to_all | solution.py:181
  18.7 1.9 collective-permute-start
  20.8 3.6 %collective-permute-start.13 = (bf16[16,14,512]{2,0,1:T(8,128)(2,1)S(1)}, bf16[16,14,512]{2,0,1:T(8,128)(2,1)S(1)}, u32[]{:S(2)}, u32[]{:S(2)}) collective-permute-start(bf16[16,14,512]{2,0,1:T(8,128)(2,1)S(1)} %pad_maximum_fusion.3), channel_id=1, source_target_pairs={{0,32},{1,33},{2,34},{3,35},{4,36},{5,37},{6,38},{7,39},{8,40},{9,... | collective-permute-start | bytes 688136 | tf_op jit(solution)/shard_map/ppermute | solution.py:231
  24.4 6.4 %collective-permute-done.13 = bf16[16,14,512]{2,0,1:T(8,128)(2,1)S(1)} collective-permute-done((bf16[16,14,512]{2,0,1:T(8,128)(2,1)S(1)}, bf16[16,14,512]{2,0,1:T(8,128)(2,1)S(1)}, u32[]{:S(2)}, u32[]{:S(2)}) %collective-permute-start.13) | collective-permute-done | bytes 229408 | tf_op jit(solution)/shard_map/ppermute | solution.py:231
  31.4 1.5 copy.21
  32.9 4.7 %all-to-all-done = bf16[64,7,512]{2,1,0:T(8,128)(2,1)S(1)} async-done(((bf16[64,7,512]{2,1,0:T(8,128)(2,1)}), bf16[64,7,512]{2,1,0:T(8,128)(2,1)S(1)}, u32[]{:S(2)}, u32[]{:S(2)}) %all-to-all-start) | async-done | bytes 458784 | tf_op jit(solution)/shard_map/all_to_all | solution.py:181
  38.5 4.9 %all-to-all-start.1 = ((bf16[32,28,512]{2,1,0:T(8,128)(2,1)}), bf16[32,28,512]{2,1,0:T(8,128)(2,1)S(1)}, u32[]{:S(2)}, u32[]{:S(2)}) async-start(bf16[32,28,512]{2,1,0:T(8,128)(2,1)} %copy.21), calls=%async_computation.1 | async-start | bytes 2097152 | tf_op jit(solution)/shard_map/all_to_all | solution.py:237
  43.3 1.2 reshape.29.params
  44.5 0.9 fusion.25
  45.4 1.9 collective-permute-start.1
  48.0 4.8 %collective-permute-start.4 = (bf16[448,256]{1,0:T(8,128)(2,1)}, bf16[448,256]{1,0:T(8,128)(2,1)}, u32[]{:S(2)}, u32[]{:S(2)}) collective-permute-start(bf16[448,256]{1,0:T(8,128)(2,1)} %get-tuple-element.34.rest_0_), channel_id=1, source_target_pairs={{0,128},{64,192},{128,256},{192,320},{256,384},{320,448},{384,0},{... | collective-permute-start | bytes 688136 | tf_op jit(solution)/shard_map/ppermute | solution.py:190
  52.8 1.9 collective-permute-start.3
  54.9 3.5 %collective-permute-start.2 = (bf16[448,256]{1,0:T(8,128)(2,1)}, bf16[448,256]{1,0:T(8,128)(2,1)}, u32[]{:S(2)}, u32[]{:S(2)}) collective-permute-start(bf16[448,256]{1,0:T(8,128)(2,1)} %get-tuple-element.34.rest_0_), channel_id=1, source_target_pairs={{0,384},{64,448},{128,0},{192,64},{256,128},{320,192},{384,256},{4... | collective-permute-start | bytes 688136 | tf_op jit(solution)/shard_map/ppermute | solution.py:190
  58.3 4.5 %collective-permute-start.5 = (bf16[448,256]{1,0:T(8,128)(2,1)}, bf16[448,256]{1,0:T(8,128)(2,1)}, u32[]{:S(2)}, u32[]{:S(2)}) collective-permute-start(bf16[448,256]{1,0:T(8,128)(2,1)} %collective-permute-done.1.rest_1_), channel_id=1, source_target_pairs={{0,128},{64,192},{128,256},{192,320},{256,384},{320,448},{384,0},{... | collective-permute-start | bytes 688136 | tf_op jit(solution)/shard_map/ppermute | solution.py:190
  62.8 1.9 collective-permute-done.4.rest_4_
  64.8 6.6 %collective-permute-start.7 = (bf16[448,256]{1,0:T(8,128)(2,1)}, bf16[448,256]{1,0:T(8,128)(2,1)}, u32[]{:S(2)}, u32[]{:S(2)}) collective-permute-start(bf16[448,256]{1,0:T(8,128)(2,1)} %collective-permute-done.4.rest_4_), channel_id=1, source_target_pairs={{0,128},{64,192},{128,256},{192,320},{256,384},{320,448},{384,0},{... | collective-permute-start | bytes 688136 | tf_op jit(solution)/shard_map/ppermute | solution.py:190
  71.4 1.9 collective-permute-start.8
  74.0 1.9 collective-permute-start.6
  76.6 4.8 %turn.1.turned = bf16[3584,512]{1,0:T(8,128)(2,1)} custom-call(bf16[256,3584]{1,0:T(8,128)(2,1)} %bitcast.15, bf16[256,3584]{1,0:T(8,128)(2,1)} %collective-permute-done.tok_theirs), custom_call_target="tpu_custom_call" | custom-call | tf_op jit(solution)/shard_map/turn/pallas_call | solution.py:242
  81.4 4.3 %partial.1 = f32[512,256]{1,0:T(8,128)} custom-call(s32[2]{0:T(128)} %pad_add_fusion.place, bf16[256,3584]{1,0:T(8,128)(2,1)} %bitcast.16, bf16[256,3584]{1,0:T(8,128)(2,1)} %collective-permute-done.tok_theirs, bf16[448,256]{1,0:T(8,128)(2,1)} %get-tuple-element.34.rest_0_, bf16[448,256]{1,0:T(8,128)(2,1)} %collective-permute-done.1.rest_1_, ...), custom_call_target="tpu_custom_call" | custom-call | tf_op jit(solution)/shard_map/partial/pallas_call | solution.py:250
  85.7 3.8 %collective-permute-done.8.piece_theirs = bf16[448,256]{1,0:T(8,128)(2,1)} collective-permute-done((bf16[448,256]{1,0:T(8,128)(2,1)}, bf16[448,256]{1,0:T(8,128)(2,1)}, u32[]{:S(2)}, u32[]{:S(2)}) %collective-permute-start.8) | collective-permute-done | bytes 229408 | tf_op jit(solution)/shard_map/ppermute | solution.py:190
  89.5 4.2 %project.1 = (bf16[512,256]{1,0:T(8,128)(2,1)}, bf16[448,256]{1,0:T(8,128)(2,1)}, bf16[448,256]{1,0:T(8,128)(2,1)}) custom-call(s32[2]{0:T(128)} %pad_add_fusion.place, f32[512,256]{1,0:T(8,128)} %partial.1, bf16[256,128]{1,0:T(8,128)(2,1)} %get-tuple-element.41.hid_mine, bf16[256,128]{1,0:T(8,128)(2,1)} %copy-done.7, ...), custom_call_target="tpu_custom_call" | custom-call | tf_op jit(solution)/shard_map/project/pallas_call | solution.py:258
  93.7 2.8 %collective-permute-start.9 = (bf16[448,256]{1,0:T(8,128)(2,1)}, bf16[448,256]{1,0:T(8,128)(2,1)S(1)}, u32[]{:S(2)}, u32[]{:S(2)}) collective-permute-start(bf16[448,256]{1,0:T(8,128)(2,1)} %get-tuple-element.17), channel_id=1, source_target_pairs={{0,128},{64,192},{128,256},{192,320},{256,384},{320,448},{384,0},{... | collective-permute-start | bytes 688136 | tf_op jit(solution)/shard_map/ppermute | solution.py:190
  96.5 3.8 %terms.1 = (bf16[448,256]{1,0:T(8,128)(2,1)}, bf16[448,256]{1,0:T(8,128)(2,1)}, bf16[448,256]{1,0:T(8,128)(2,1)}, bf16[448,256]{1,0:T(8,128)(2,1)}, bf16[448,256]{1,0:T(8,128)(2,1)}, /*index=5*/bf16[448,256]{1,0:T(8,128)(2,1)}) custom-call(s32[2]{0:T(128)} %pad_add_fusion.place, bf16[3584,512]{1,0:T(8,128)(2,1)} %turn.1.turned, ...), custom_call_target="tpu_custom_call" | custom-call | tf_op jit(solution)/shard_map/terms/pallas_call | solution.py:274
  100.3 4.1 %collective-permute-start.11 = (bf16[448,256]{1,0:T(8,128)(2,1)S(1)}, bf16[448,256]{1,0:T(8,128)(2,1)S(1)}, u32[]{:S(2)}, u32[]{:S(2)}) collective-permute-start(bf16[448,256]{1,0:T(8,128)(2,1)S(1)} %copy-done.9), channel_id=1, source_target_pairs={{0,384},{64,448},{128,0},{192,64},{256,128},{320,192},{384,256},{4... | collective-permute-start | bytes 688136 | tf_op jit(solution)/shard_map/ppermute | solution.py:190
  104.4 2.9 %collective-permute-done.9 = bf16[448,256]{1,0:T(8,128)(2,1)S(1)} collective-permute-done((bf16[448,256]{1,0:T(8,128)(2,1)}, bf16[448,256]{1,0:T(8,128)(2,1)S(1)}, u32[]{:S(2)}, u32[]{:S(2)}) %collective-permute-start.9) | collective-permute-done | bytes 229408 | tf_op jit(solution)/shard_map/ppermute | solution.py:190
  107.3 1.0 add_convert_fusion.3
  108.3 6.4 %collective-permute-start.10 = (bf16[448,256]{1,0:T(8,128)(2,1)S(1)}, bf16[448,256]{1,0:T(8,128)(2,1)S(1)}, u32[]{:S(2)}, u32[]{:S(2)}) collective-permute-start(bf16[448,256]{1,0:T(8,128)(2,1)S(1)} %add_convert_fusion.3), channel_id=1, source_target_pairs={{0,128},{64,192},{128,256},{192,320},{256,384},{320,448},{384,0},{... | collective-permute-start | bytes 688136 | tf_op jit(solution)/shard_map/ppermute | solution.py:190
  114.7 2.4 %collective-permute-done.11 = bf16[448,256]{1,0:T(8,128)(2,1)S(1)} collective-permute-done((bf16[448,256]{1,0:T(8,128)(2,1)S(1)}, bf16[448,256]{1,0:T(8,128)(2,1)S(1)}, u32[]{:S(2)}, u32[]{:S(2)}) %collective-permute-start.11) | collective-permute-done | bytes 229408 | tf_op jit(solution)/shard_map/ppermute | solution.py:190
  117.1 1.0 add_convert_fusion.2
  118.1 1.9 collective-permute-start.12
  120.0 6.0 %collective-permute-start.15 = (bf16[448,256]{1,0:T(8,128)(2,1)}, bf16[448,256]{1,0:T(8,128)(2,1)S(1)}, u32[]{:S(2)}, u32[]{:S(2)}) collective-permute-start(bf16[448,256]{1,0:T(8,128)(2,1)} %get-tuple-element.25), channel_id=1, source_target_pairs={{0,128},{64,192},{128,256},{192,320},{256,384},{320,448},{384,0},{... | collective-permute-start | bytes 688136 | tf_op jit(solution)/shard_map/ppermute | solution.py:190
  126.0 1.9 collective-permute-start.14
  128.0 11.7 %collective-permute-done.12 = bf16[448,256]{1,0:T(8,128)(2,1)S(1)} collective-permute-done((bf16[448,256]{1,0:T(8,128)(2,1)S(1)}, bf16[448,256]{1,0:T(8,128)(2,1)S(1)}, u32[]{:S(2)}, u32[]{:S(2)}) %collective-permute-start.12) | collective-permute-done | bytes 229408 | tf_op jit(solution)/shard_map/ppermute | solution.py:190
  139.7 1.0 add_convert_fusion
  140.7 1.9 collective-permute-start.16
  142.7 1.0 collective-permute-done.14
  144.3 29.5 %all_to_all.20 = bf16[64,7,512]{2,1,0:T(8,128)(2,1)S(1)} all-to-all(bf16[64,7,512]{2,1,0:T(8,128)(2,1)S(1)} %reshape.32), channel_id=1, replica_groups=mesh['dp'=8,'expert'=64] {'expert'}, dimensions={0} | all-to-all | bytes 917504 | tf_op jit(solution)/shard_map/all_to_all | solution.py:181
  174.2 1.1 copy.23
  175.2 4.6 %all-to-all-start.3 = ((bf16[64,7,512]{2,1,0:T(8,128)(2,1)}), bf16[64,7,512]{2,1,0:T(8,128)(2,1)S(1)}, u32[]{:S(2)}, u32[]{:S(2)}) async-start(bf16[64,7,512]{2,1,0:T(8,128)(2,1)} %copy.23), calls=%async_computation.3 | async-start | bytes 1048576 | tf_op jit(solution)/shard_map/all_to_all | solution.py:181
  180.3 0.9 reshape.30.first
  181.2 0.9 reshape.31.second
  182.2 16.6 %all-to-all-done.3 = bf16[64,7,512]{2,1,0:T(8,128)(2,1)S(1)} async-done(((bf16[64,7,512]{2,1,0:T(8,128)(2,1)}), bf16[64,7,512]{2,1,0:T(8,128)(2,1)S(1)}, u32[]{:S(2)}, u32[]{:S(2)}) %all-to-all-start.3) | async-done | bytes 458784 | tf_op jit(solution)/shard_map/all_to_all | solution.py:181
  198.8 0.9 reshape.33.gradient
  199.7 4.1 %adam.1 = (bf16[1,448,512]{2,1,0:T(8,128)(2,1)}, f32[1,448,512]{2,1,0:T(8,128)}, f32[1,448,512]{2,1,0:T(8,128)}) custom-call(s32[2]{0:T(128)} %pad_add_fusion.place, bf16[448,512]{1,0:T(8,128)(2,1)} %copy-done.1, bf16[448,512]{1,0:T(8,128)(2,1)} %reshape.30.first, bf16[448,512]{1,0:T(8,128)(2,1)} %reshape.31.second, bf16[448,512]{1,0:T(8,128)(2,1)} %reshape.33.gradient), custom_call_target="tpu_custom_call" | custom-call | tf_op jit(solution)/shard_map/adam/pallas_call | solution.py:303
  (50 shorter events, 4.4 us)
Async XLA Ops:
  0.6 18.0 %copy-start = (bf16[1,1,256,3584]{3,2,1,0:T(8,128)(2,1)S(1)}, bf16[1,1,256,3584]{3,2,1,0:T(8,128)(2,1)}, u32[]{:S(2)}) copy-start(bf16[1,1,256,3584]{3,2,1,0:T(8,128)(2,1)} %param.12) | copy-start | bytes 5505028
  0.6 20.0 %copy-start.4 = (f32[16,7,512]{2,0,1:T(8,128)S(1)}, f32[16,7,512]{2,0,1:T(8,128)}, u32[]{:S(2)}) copy-start(f32[16,7,512]{2,0,1:T(8,128)} %param.8) | copy-start | bytes 688132
  0.7 20.0 %copy-start.5 = (f32[16,7,512]{2,0,1:T(8,128)S(1)}, f32[16,7,512]{2,0,1:T(8,128)}, u32[]{:S(2)}) copy-start(f32[16,7,512]{2,0,1:T(8,128)} %param.9) | copy-start | bytes 688132
  3.7 20.7 %copy-start.8 = (s32[64]{0:T(128)S(1)}, s32[64]{0:T(128)}, u32[]{:S(2)}) copy-start(s32[64]{0:T(128)} %param.10) | copy-start | bytes 772
  3.7 34.0 %all-to-all-start = ((bf16[64,7,512]{2,1,0:T(8,128)(2,1)}), bf16[64,7,512]{2,1,0:T(8,128)(2,1)S(1)}, u32[]{:S(2)}, u32[]{:S(2)}) async-start(bf16[64,7,512]{2,1,0:T(8,128)(2,1)} %copy.20), calls=%async_computation | async-start | bytes 1048576 | tf_op jit(solution)/shard_map/all_to_all | solution.py:181
  18.7 55.3 %collective-permute-start = (bf16[256,3584]{1,0:T(8,128)(2,1)S(1)}, bf16[256,3584]{1,0:T(8,128)(2,1)}, u32[]{:S(2)}, u32[]{:S(2)}) collective-permute-start(bf16[256,3584]{1,0:T(8,128)(2,1)S(1)} %bitcast.18), channel_id=1, source_target_pairs={{0,64},{64,0},{128,192},{192,128},{256,320},{320,256},{384,448},{4... | collective-permute-start | bytes 5505032 | tf_op jit(solution)/shard_map/ppermute | solution.py:193
  20.8 10.0 %collective-permute-start.13 = (bf16[16,14,512]{2,0,1:T(8,128)(2,1)S(1)}, bf16[16,14,512]{2,0,1:T(8,128)(2,1)S(1)}, u32[]{:S(2)}, u32[]{:S(2)}) collective-permute-start(bf16[16,14,512]{2,0,1:T(8,128)(2,1)S(1)} %pad_maximum_fusion.3), channel_id=1, source_target_pairs={{0,32},{1,33},{2,34},{3,35},{4,36},{5,37},{6,38},{7,39},{8,40},{9,... | collective-permute-start | bytes 688136 | tf_op jit(solution)/shard_map/ppermute | solution.py:231
  32.9 21.8 %copy-start.6 = (bf16[1,1,256,256]{3,2,1,0:T(8,128)(2,1)S(1)}, bf16[1,1,256,256]{3,2,1,0:T(8,128)(2,1)}, u32[]{:S(2)}) copy-start(bf16[1,1,256,256]{3,2,1,0:T(8,128)(2,1)} %param.13) | copy-start | bytes 393220
  37.7 0.8 copy-start.2
  38.5 89.5 %all-to-all-start.1 = ((bf16[32,28,512]{2,1,0:T(8,128)(2,1)}), bf16[32,28,512]{2,1,0:T(8,128)(2,1)S(1)}, u32[]{:S(2)}, u32[]{:S(2)}) async-start(bf16[32,28,512]{2,1,0:T(8,128)(2,1)} %copy.21), calls=%async_computation.1 | async-start | bytes 2097152 | tf_op jit(solution)/shard_map/all_to_all | solution.py:237
  44.5 36.9 %copy-start.1 = (bf16[448,512]{1,0:T(8,128)(2,1)}, bf16[448,512]{1,0:T(8,128)(2,1)S(1)}, u32[]{:S(2)}) copy-start(bf16[448,512]{1,0:T(8,128)(2,1)S(1)} %reshape.29.params) | copy-start | bytes 1376260
  45.4 7.4 %collective-permute-start.1 = (bf16[448,256]{1,0:T(8,128)(2,1)}, bf16[448,256]{1,0:T(8,128)(2,1)}, u32[]{:S(2)}, u32[]{:S(2)}) collective-permute-start(bf16[448,256]{1,0:T(8,128)(2,1)} %get-tuple-element.33), channel_id=1, source_target_pairs={{0,64},{64,0},{128,192},{192,128},{256,320},{320,256},{384,448},{4... | collective-permute-start | bytes 688136 | tf_op jit(solution)/shard_map/ppermute | solution.py:193
  48.0 16.8 %collective-permute-start.4 = (bf16[448,256]{1,0:T(8,128)(2,1)}, bf16[448,256]{1,0:T(8,128)(2,1)}, u32[]{:S(2)}, u32[]{:S(2)}) collective-permute-start(bf16[448,256]{1,0:T(8,128)(2,1)} %get-tuple-element.34.rest_0_), channel_id=1, source_target_pairs={{0,128},{64,192},{128,256},{192,320},{256,384},{320,448},{384,0},{... | collective-permute-start | bytes 688136 | tf_op jit(solution)/shard_map/ppermute | solution.py:190
  52.8 18.6 %collective-permute-start.3 = (bf16[448,256]{1,0:T(8,128)(2,1)}, bf16[448,256]{1,0:T(8,128)(2,1)}, u32[]{:S(2)}, u32[]{:S(2)}) collective-permute-start(bf16[448,256]{1,0:T(8,128)(2,1)} %collective-permute-done.1.rest_1_), channel_id=1, source_target_pairs={{0,384},{64,448},{128,0},{192,64},{256,128},{320,192},{384,256},{4... | collective-permute-start | bytes 688136 | tf_op jit(solution)/shard_map/ppermute | solution.py:190
  54.9 26.5 %collective-permute-start.2 = (bf16[448,256]{1,0:T(8,128)(2,1)}, bf16[448,256]{1,0:T(8,128)(2,1)}, u32[]{:S(2)}, u32[]{:S(2)}) collective-permute-start(bf16[448,256]{1,0:T(8,128)(2,1)} %get-tuple-element.34.rest_0_), channel_id=1, source_target_pairs={{0,384},{64,448},{128,0},{192,64},{256,128},{320,192},{384,256},{4... | collective-permute-start | bytes 688136 | tf_op jit(solution)/shard_map/ppermute | solution.py:190
  58.3 23.1 %collective-permute-start.5 = (bf16[448,256]{1,0:T(8,128)(2,1)}, bf16[448,256]{1,0:T(8,128)(2,1)}, u32[]{:S(2)}, u32[]{:S(2)}) collective-permute-start(bf16[448,256]{1,0:T(8,128)(2,1)} %collective-permute-done.1.rest_1_), channel_id=1, source_target_pairs={{0,128},{64,192},{128,256},{192,320},{256,384},{320,448},{384,0},{... | collective-permute-start | bytes 688136 | tf_op jit(solution)/shard_map/ppermute | solution.py:190
  64.8 20.9 %collective-permute-start.7 = (bf16[448,256]{1,0:T(8,128)(2,1)}, bf16[448,256]{1,0:T(8,128)(2,1)}, u32[]{:S(2)}, u32[]{:S(2)}) collective-permute-start(bf16[448,256]{1,0:T(8,128)(2,1)} %collective-permute-done.4.rest_4_), channel_id=1, source_target_pairs={{0,128},{64,192},{128,256},{192,320},{256,384},{320,448},{384,0},{... | collective-permute-start | bytes 688136 | tf_op jit(solution)/shard_map/ppermute | solution.py:190
  71.4 18.1 %collective-permute-start.8 = (bf16[448,256]{1,0:T(8,128)(2,1)}, bf16[448,256]{1,0:T(8,128)(2,1)}, u32[]{:S(2)}, u32[]{:S(2)}) collective-permute-start(bf16[448,256]{1,0:T(8,128)(2,1)} %collective-permute-done.3.rest_3_), channel_id=1, source_target_pairs={{0,384},{64,448},{128,0},{192,64},{256,128},{320,192},{384,256},{4... | collective-permute-start | bytes 688136 | tf_op jit(solution)/shard_map/ppermute | solution.py:190
  74.0 11.7 %collective-permute-start.6 = (bf16[256,128]{1,0:T(8,128)(2,1)S(1)}, bf16[256,128]{1,0:T(8,128)(2,1)S(1)}, u32[]{:S(2)}, u32[]{:S(2)}) collective-permute-start(bf16[256,128]{1,0:T(8,128)(2,1)S(1)} %get-tuple-element.40), channel_id=1, source_target_pairs={{0,64},{64,0},{128,192},{192,128},{256,320},{320,256},{384,448},{4... | collective-permute-start | bytes 196616 | tf_op jit(solution)/shard_map/ppermute | solution.py:193
  85.7 3.8 %copy-start.7 = (bf16[256,128]{1,0:T(8,128)(2,1)}, bf16[256,128]{1,0:T(8,128)(2,1)S(1)}, u32[]{:S(2)}) copy-start(bf16[256,128]{1,0:T(8,128)(2,1)S(1)} %collective-permute-done.6.hid_theirs) | copy-start | bytes 196612
  93.7 13.6 %collective-permute-start.9 = (bf16[448,256]{1,0:T(8,128)(2,1)}, bf16[448,256]{1,0:T(8,128)(2,1)S(1)}, u32[]{:S(2)}, u32[]{:S(2)}) collective-permute-start(bf16[448,256]{1,0:T(8,128)(2,1)} %get-tuple-element.17), channel_id=1, source_target_pairs={{0,128},{64,192},{128,256},{192,320},{256,384},{320,448},{384,0},{... | collective-permute-start | bytes 688136 | tf_op jit(solution)/shard_map/ppermute | solution.py:190
  96.5 3.8 %copy-start.9 = (bf16[448,256]{1,0:T(8,128)(2,1)S(1)}, bf16[448,256]{1,0:T(8,128)(2,1)}, u32[]{:S(2)}) copy-start(bf16[448,256]{1,0:T(8,128)(2,1)} %get-tuple-element.19) | copy-start | bytes 688132
  100.3 43.3 %copy-start.3 = (bf16[448,256]{1,0:T(8,128)(2,1)S(1)}, bf16[448,256]{1,0:T(8,128)(2,1)}, u32[]{:S(2)}) copy-start(bf16[448,256]{1,0:T(8,128)(2,1)} %get-tuple-element.21) | copy-start | bytes 688132
  100.3 16.8 %collective-permute-start.11 = (bf16[448,256]{1,0:T(8,128)(2,1)S(1)}, bf16[448,256]{1,0:T(8,128)(2,1)S(1)}, u32[]{:S(2)}, u32[]{:S(2)}) collective-permute-start(bf16[448,256]{1,0:T(8,128)(2,1)S(1)} %copy-done.9), channel_id=1, source_target_pairs={{0,384},{64,448},{128,0},{192,64},{256,128},{320,192},{384,256},{4... | collective-permute-start | bytes 688136 | tf_op jit(solution)/shard_map/ppermute | solution.py:190
  108.3 19.7 %collective-permute-start.10 = (bf16[448,256]{1,0:T(8,128)(2,1)S(1)}, bf16[448,256]{1,0:T(8,128)(2,1)S(1)}, u32[]{:S(2)}, u32[]{:S(2)}) collective-permute-start(bf16[448,256]{1,0:T(8,128)(2,1)S(1)} %add_convert_fusion.3), channel_id=1, source_target_pairs={{0,128},{64,192},{128,256},{192,320},{256,384},{320,448},{384,0},{... | collective-permute-start | bytes 688136 | tf_op jit(solution)/shard_map/ppermute | solution.py:190
  118.1 21.6 %collective-permute-start.12 = (bf16[448,256]{1,0:T(8,128)(2,1)S(1)}, bf16[448,256]{1,0:T(8,128)(2,1)S(1)}, u32[]{:S(2)}, u32[]{:S(2)}) collective-permute-start(bf16[448,256]{1,0:T(8,128)(2,1)S(1)} %add_convert_fusion.2), channel_id=1, source_target_pairs={{0,384},{64,448},{128,0},{192,64},{256,128},{320,192},{384,256},{4... | collective-permute-start | bytes 688136 | tf_op jit(solution)/shard_map/ppermute | solution.py:190
  120.0 19.7 %collective-permute-start.15 = (bf16[448,256]{1,0:T(8,128)(2,1)}, bf16[448,256]{1,0:T(8,128)(2,1)S(1)}, u32[]{:S(2)}, u32[]{:S(2)}) collective-permute-start(bf16[448,256]{1,0:T(8,128)(2,1)} %get-tuple-element.25), channel_id=1, source_target_pairs={{0,128},{64,192},{128,256},{192,320},{256,384},{320,448},{384,0},{... | collective-permute-start | bytes 688136 | tf_op jit(solution)/shard_map/ppermute | solution.py:190
  126.0 17.6 %collective-permute-start.14 = (bf16[448,256]{1,0:T(8,128)(2,1)}, bf16[448,256]{1,0:T(8,128)(2,1)S(1)}, u32[]{:S(2)}, u32[]{:S(2)}) collective-permute-start(bf16[448,256]{1,0:T(8,128)(2,1)} %get-tuple-element.22), channel_id=1, source_target_pairs={{0,384},{64,448},{128,0},{192,64},{256,128},{320,192},{384,256},{4... | collective-permute-start | bytes 688136 | tf_op jit(solution)/shard_map/ppermute | solution.py:190
  140.7 3.4 %collective-permute-start.16 = (bf16[448,256]{1,0:T(8,128)(2,1)S(1)}, bf16[448,256]{1,0:T(8,128)(2,1)S(1)}, u32[]{:S(2)}, u32[]{:S(2)}) collective-permute-start(bf16[448,256]{1,0:T(8,128)(2,1)S(1)} %add_convert_fusion), channel_id=1, source_target_pairs={{0,64},{64,0},{128,192},{192,128},{256,320},{320,256},{384,448},{4... | collective-permute-start | bytes 688136 | tf_op jit(solution)/shard_map/ppermute | solution.py:193
  175.2 23.5 %all-to-all-start.3 = ((bf16[64,7,512]{2,1,0:T(8,128)(2,1)}), bf16[64,7,512]{2,1,0:T(8,128)(2,1)S(1)}, u32[]{:S(2)}, u32[]{:S(2)}) async-start(bf16[64,7,512]{2,1,0:T(8,128)(2,1)} %copy.23), calls=%async_computation.3 | async-start | bytes 1048576 | tf_op jit(solution)/shard_map/all_to_all | solution.py:181

commit v3 on v2

--- a/solution.py
+++ b/solution.py
@@ -7,6 +7,7 @@
 
 
 BLOCK = 128
+MEBI = 1 << 20
 
 
 beta_first = 0.9
@@ -80,28 +81,13 @@
 
 
 def project_kernel(
-    place, partial, hid_mine, hid_theirs, piece_mine, piece_theirs, tok_mine, tok_theirs, turned,
-    grad_ref, far_mine, far_theirs, block, far_tok, far_rows, other_rows, sems,
+    place, partial, hid_mine, hid_theirs, piece_mine, piece_theirs, far_tok, far_turned,
+    grad_ref, far_mine, far_theirs, block,
 ):
     count = piece_mine.shape[0]
     half = hid_mine.shape[0]
-    lanes = pl.ds(block_start(place, 2, count), 2 * count)
-    copies = [
-        pltpu.make_async_copy(tok_mine.at[:, lanes], far_tok.at[0:half], sems.at[0]),
-        pltpu.make_async_copy(tok_theirs.at[:, lanes], far_tok.at[half : 2 * half], sems.at[1]),
-        pltpu.make_async_copy(
-            turned.at[pl.ds(piece_start(place, 2, 0, count), count)], far_rows, sems.at[2]
-        ),
-        pltpu.make_async_copy(
-            turned.at[pl.ds(piece_start(place, 2, 1, count), count)], other_rows, sems.at[3]
-        ),
-    ]
-    for copy in copies:
-        copy.start()
+    width = block.shape[1] // 2
     join(place, block, piece_mine, piece_theirs)
-    width = block.shape[1] // 2
-    copies[0].wait()
-    copies[1].wait()
     for hid, low in ((hid_mine, 0), (hid_theirs, half)):
         projected = partial[low : low + half, :] + jnp.dot(
             far_tok[low : low + half, :], block[...], preferred_element_type=jnp.float32
@@ -109,18 +95,19 @@
         grad_gate, grad_up = grad_halves(projected, hid[...])
         grad_ref[low : low + half, :width] = grad_gate
         grad_ref[low : low + half, width:] = grad_up
-    copies[2].wait()
-    copies[3].wait()
-    grads = grad_ref[...]
-    far_mine[...] = jnp.dot(far_rows[...], grads, preferred_element_type=jnp.float32).astype(jnp.bfloat16)
-    far_theirs[...] = jnp.dot(other_rows[...], grads, preferred_element_type=jnp.float32).astype(jnp.bfloat16)
-
-
-def turn_kernel(tok_mine, tok_theirs, turned):
+    for out, core in ((far_mine, place[1]), (far_theirs, 1 - place[1])):
+        out[...] = term_rows(far_turned, grad_ref, core * count, count)
+
+
+def turn_kernel(place, tok_mine, tok_theirs, turned, far_tok, far_turned):
     half, wide = tok_mine.shape
+    far = far_tok.shape[1]
+    begin = pl.multiple_of(((place[0] + 2) % 4) * far, 128)
     for low, tok in ((0, tok_mine), (half, tok_theirs)):
-        for begin in range(0, wide, 512):
-            turned[begin : begin + 512, low : low + half] = tok[:, begin : begin + 512].T
+        for step in range(0, wide, 512):
+            turned[step : step + 512, low : low + half] = tok[:, step : step + 512].T
+        far_tok[low : low + half, :] = tok[:, pl.ds(begin, far)]
+    far_turned[...] = turned[pl.ds(begin, far), :]
 
 
 def term_kernel(place, turned, grad_ref, *outs):
@@ -152,10 +139,6 @@
 
 def in_smem():
     return [pl.BlockSpec(memory_space=pltpu.SMEM)]
-
-
-def in_any(count):
-    return [pl.BlockSpec(memory_space=pl.ANY) for _ in range(count)]
 
 
 def on_device(weights, first_moment, second_moment, placement, block_counts, tokens, hidden_grad):
@@ -239,13 +222,18 @@
         axis_index_groups=[list(range(group)), list(range(group, expert_count))],
     )
 
-    turned = pl.pallas_call(
+    turned, far_tok, far_turned = pl.pallas_call(
         turn_kernel,
-        in_specs=in_vmem(2),
-        out_specs=in_vmem(1)[0],
-        out_shape=jax.ShapeDtypeStruct((wide, 2 * row_total), narrow),
+        in_specs=in_smem() + in_vmem(2),
+        out_specs=in_vmem(3),
+        out_shape=[
+            jax.ShapeDtypeStruct((wide, 2 * row_total), narrow),
+            jax.ShapeDtypeStruct((2 * row_total, 2 * own_count), narrow),
+            jax.ShapeDtypeStruct((2 * own_count, 2 * row_total), narrow),
+        ],
         name="turn",
-    )(inputs, tok_theirs)
+        compiler_params=pltpu.CompilerParams(vmem_limit_bytes=12 * MEBI),
+    )(place, inputs, tok_theirs)
     piece = jax.ShapeDtypeStruct((own_count, part_cols), narrow)
     partial = pl.pallas_call(
         partial_kernel,
@@ -254,21 +242,17 @@
         out_shape=jax.ShapeDtypeStruct((2 * row_total, part_cols), jnp.float32),
         scratch_shapes=[pltpu.VMEM((3, 2 * own_count, part_cols), narrow)],
         name="partial",
+        compiler_params=pltpu.CompilerParams(vmem_limit_bytes=10 * MEBI),
     )(place, inputs, tok_theirs, mine, theirs, minus_mine, minus_theirs, plus_mine, plus_theirs)
     grad_proj, send_mine, send_theirs = pl.pallas_call(
         project_kernel,
-        in_specs=in_smem() + in_vmem(5) + in_any(3),
+        in_specs=in_smem() + in_vmem(7),
         out_specs=in_vmem(3),
         out_shape=[jax.ShapeDtypeStruct((2 * row_total, part_cols), narrow), piece, piece],
-        scratch_shapes=[
-            pltpu.VMEM((2 * own_count, part_cols), narrow),
-            pltpu.VMEM((2 * row_total, 2 * own_count), narrow),
-            pltpu.VMEM((own_count, 2 * row_total), narrow),
-            pltpu.VMEM((own_count, 2 * row_total), narrow),
-            pltpu.SemaphoreType.DMA((4,)),
-        ],
+        scratch_shapes=[pltpu.VMEM((2 * own_count, part_cols), narrow)],
         name="project",
-    )(place, partial, hid_mine, hid_theirs, far_mine, far_theirs, inputs, tok_theirs, turned)
+        compiler_params=pltpu.CompilerParams(vmem_limit_bytes=8 * MEBI),
+    )(place, partial, hid_mine, hid_theirs, far_mine, far_theirs, far_tok, far_turned)
     got_plus = shift(send_mine, 1)
     got_minus = shift(send_theirs, -1)
     next_mine, next_theirs, last_mine, last_theirs, sum_mine, sum_theirs = pl.pallas_call(
@@ -277,6 +261,7 @@
         out_specs=in_vmem(6),
         out_shape=[piece] * 6,
         name="terms",
+        compiler_params=pltpu.CompilerParams(vmem_limit_bytes=8 * MEBI),
     )(place, turned, grad_proj)
     early_theirs = shift(next_theirs, 1)
     early_mine = shift(last_mine, -1)
@@ -311,6 +296,7 @@
             jax.ShapeDtypeStruct(shape, jnp.float32),
         ],
         name="adam",
+        compiler_params=pltpu.CompilerParams(vmem_limit_bytes=12 * MEBI),
     )(
         place, own_rows, moment_rows(0), moment_rows(1), grad_rows,
     )

time: 205 us -> 186 us (0.907)
  the two profiles are of different devices: /device:TPU:16 before, /device:TPU:8 now
where the time goes in v3:
time: 186 us; the launch traced here: 185 us
  starting transfers between devices  82.6 us (44%)
  waiting for transfers between devices  47.4 us (25%)
  blocking collectives  32.2 us (17%)
  Pallas kernels  10.9 us (6%)
  local copies, waits for them, and re-layouts  7.06 us (4%)
    ppermute x12, starting transfers between devices, shift(): return lax.ppermute(value, 'dp', pairs)  46.9 us
    all_to_all x1, blocking collectives, exchange(): lax.all_to_all(values, 'expert', split_axis=0, concat_axis=0, tiled=True)  32.2 us
    all_to_all x2, waiting for transfers between devices, exchange(): lax.all_to_all(values, 'expert', split_axis=0, concat_axis=0, tiled=True)  20.4 us
    all_to_all x2, starting transfers between devices, exchange(): lax.all_to_all(values, 'expert', split_axis=0, concat_axis=0, tiled=True)  20.2 us
    ppermute x12, waiting for transfers between devices, shift(): return lax.ppermute(value, 'dp', pairs)  19.5 us
    ppermute x4, starting transfers between devices, swap(): return lax.ppermute(value, 'dp', [(i, i ^ 1) for i in range(dp_count)])  7.68 us
    ppermute x1, waiting for transfers between devices, on_device(): lax.ppermute(stored, 'expert', [(e, (e + group) % expert_count) for e in...  7.58 us
    all_to_all x1, starting transfers between devices, on_device(): lax.all_to_all(moments_sent, 'expert', split_axis=0, concat_axis=0, tiled...  5.5 us
  transfers between devices with their start and end apart: 20, of which 11 were waited for; matrix products, arithmetic and copies ran while one was open for 3% of the time, Pallas kernels for 4%

profile of v3, /device:TPU:8, one launch (start us, length us, event | category | flops | bytes accessed | tf_op | source)
XLA Modules:
  0.0 184.9 jit_solution(14542692609430675646)
XLA Ops:
  0.7 1.0 fusion.26
  1.7 1.0 convolution_convert_fusion.1
  2.7 1.1 copy.20
  3.7 15.0 %all-to-all-start = ((bf16[64,7,512]{2,1,0:T(8,128)(2,1)}), bf16[64,7,512]{2,1,0:T(8,128)(2,1)S(1)}, u32[]{:S(2)}, u32[]{:S(2)}) async-start(bf16[64,7,512]{2,1,0:T(8,128)(2,1)} %copy.20), calls=%async_computation | async-start | bytes 1048576 | tf_op jit(solution)/shard_map/all_to_all | solution.py:164
  18.8 1.9 %collective-permute-start = (bf16[256,3584]{1,0:T(8,128)(2,1)S(1)}, bf16[256,3584]{1,0:T(8,128)(2,1)}, u32[]{:S(2)}, u32[]{:S(2)}) collective-permute-start(bf16[256,3584]{1,0:T(8,128)(2,1)S(1)} %bitcast.15), channel_id=1, source_target_pairs={{0,64},{64,0},{128,192},{192,128},{256,320},{320,256},{384,448},{4... | collective-permute-start | bytes 5505032 | tf_op jit(solution)/shard_map/ppermute | solution.py:176
  20.9 2.3 %collective-permute-start.13 = (bf16[16,14,512]{2,0,1:T(8,128)(2,1)S(1)}, bf16[16,14,512]{2,0,1:T(8,128)(2,1)S(1)}, u32[]{:S(2)}, u32[]{:S(2)}) collective-permute-start(bf16[16,14,512]{2,0,1:T(8,128)(2,1)S(1)} %pad_maximum_fusion.3), channel_id=1, source_target_pairs={{0,32},{1,33},{2,34},{3,35},{4,36},{5,37},{6,38},{7,39},{8,40},{9,... | collective-permute-start | bytes 688136 | tf_op jit(solution)/shard_map/ppermute | solution.py:214
  23.2 7.6 %collective-permute-done.13 = bf16[16,14,512]{2,0,1:T(8,128)(2,1)S(1)} collective-permute-done((bf16[16,14,512]{2,0,1:T(8,128)(2,1)S(1)}, bf16[16,14,512]{2,0,1:T(8,128)(2,1)S(1)}, u32[]{:S(2)}, u32[]{:S(2)}) %collective-permute-start.13) | collective-permute-done | bytes 229408 | tf_op jit(solution)/shard_map/ppermute | solution.py:214
  30.9 0.5 convolution_convert_fusion
  31.4 1.5 copy.21
  32.9 4.3 %all-to-all-done = bf16[64,7,512]{2,1,0:T(8,128)(2,1)S(1)} async-done(((bf16[64,7,512]{2,1,0:T(8,128)(2,1)}), bf16[64,7,512]{2,1,0:T(8,128)(2,1)S(1)}, u32[]{:S(2)}, u32[]{:S(2)}) %all-to-all-start) | async-done | bytes 458784 | tf_op jit(solution)/shard_map/all_to_all | solution.py:164
  37.2 5.5 %all-to-all-start.1 = ((bf16[32,28,512]{2,1,0:T(8,128)(2,1)}), bf16[32,28,512]{2,1,0:T(8,128)(2,1)}, u32[]{:S(2)}, u32[]{:S(2)}) async-start(bf16[32,28,512]{2,1,0:T(8,128)(2,1)} %copy.21), calls=%async_computation.1 | async-start | bytes 2097152 | tf_op jit(solution)/shard_map/all_to_all | solution.py:220
  42.7 0.2 reshape.29.params
  42.9 1.9 %collective-permute-start.1 = (bf16[448,256]{1,0:T(8,128)(2,1)S(1)}, bf16[448,256]{1,0:T(8,128)(2,1)S(1)}, u32[]{:S(2)}, u32[]{:S(2)}) collective-permute-start(bf16[448,256]{1,0:T(8,128)(2,1)S(1)} %get-tuple-element.39), channel_id=1, source_target_pairs={{0,64},{64,0},{128,192},{192,128},{256,320},{320,256},{384,448},{4... | collective-permute-start | bytes 688136 | tf_op jit(solution)/shard_map/ppermute | solution.py:176
  45.5 4.5 %collective-permute-start.4 = (bf16[448,256]{1,0:T(8,128)(2,1)S(1)}, bf16[448,256]{1,0:T(8,128)(2,1)S(1)}, u32[]{:S(2)}, u32[]{:S(2)}) collective-permute-start(bf16[448,256]{1,0:T(8,128)(2,1)S(1)} %get-tuple-element.40.rest_0_), channel_id=1, source_target_pairs={{0,128},{64,192},{128,256},{192,320},{256,384},{320,448},{384,0},{... | collective-permute-start | bytes 688136 | tf_op jit(solution)/shard_map/ppermute | solution.py:173
  50.0 3.5 %collective-permute-start.3 = (bf16[448,256]{1,0:T(8,128)(2,1)S(1)}, bf16[448,256]{1,0:T(8,128)(2,1)S(1)}, u32[]{:S(2)}, u32[]{:S(2)}) collective-permute-start(bf16[448,256]{1,0:T(8,128)(2,1)S(1)} %collective-permute-done.1.rest_1_), channel_id=1, source_target_pairs={{0,384},{64,448},{128,0},{192,64},{256,128},{320,192},{384,256},{4... | collective-permute-start | bytes 688136 | tf_op jit(solution)/shard_map/ppermute | solution.py:173
  53.6 4.1 %collective-permute-start.2 = (bf16[448,256]{1,0:T(8,128)(2,1)S(1)}, bf16[448,256]{1,0:T(8,128)(2,1)S(1)}, u32[]{:S(2)}, u32[]{:S(2)}) collective-permute-start(bf16[448,256]{1,0:T(8,128)(2,1)S(1)} %get-tuple-element.40.rest_0_), channel_id=1, source_target_pairs={{0,384},{64,448},{128,0},{192,64},{256,128},{320,192},{384,256},{4... | collective-permute-start | bytes 688136 | tf_op jit(solution)/shard_map/ppermute | solution.py:173
  57.7 2.7 %collective-permute-start.5 = (bf16[448,256]{1,0:T(8,128)(2,1)S(1)}, bf16[448,256]{1,0:T(8,128)(2,1)S(1)}, u32[]{:S(2)}, u32[]{:S(2)}) collective-permute-start(bf16[448,256]{1,0:T(8,128)(2,1)S(1)} %collective-permute-done.1.rest_1_), channel_id=1, source_target_pairs={{0,128},{64,192},{128,256},{192,320},{256,384},{320,448},{384,0},{... | collective-permute-start | bytes 688136 | tf_op jit(solution)/shard_map/ppermute | solution.py:173
  60.4 2.1 %collective-permute-done.4.rest_4_ = bf16[448,256]{1,0:T(8,128)(2,1)S(1)} collective-permute-done((bf16[448,256]{1,0:T(8,128)(2,1)S(1)}, bf16[448,256]{1,0:T(8,128)(2,1)S(1)}, u32[]{:S(2)}, u32[]{:S(2)}) %collective-permute-start.4) | collective-permute-done | bytes 229408 | tf_op jit(solution)/shard_map/ppermute | solution.py:173
  62.5 3.3 %collective-permute-start.7 = (bf16[448,256]{1,0:T(8,128)(2,1)S(1)}, bf16[448,256]{1,0:T(8,128)(2,1)S(1)}, u32[]{:S(2)}, u32[]{:S(2)}) collective-permute-start(bf16[448,256]{1,0:T(8,128)(2,1)S(1)} %collective-permute-done.4.rest_4_), channel_id=1, source_target_pairs={{0,128},{64,192},{128,256},{192,320},{256,384},{320,448},{384,0},{... | collective-permute-start | bytes 688136 | tf_op jit(solution)/shard_map/ppermute | solution.py:173
  65.8 0.9 collective-permute-done.3.rest_3_
  66.7 5.1 %collective-permute-start.8 = (bf16[448,256]{1,0:T(8,128)(2,1)S(1)}, bf16[448,256]{1,0:T(8,128)(2,1)S(1)}, u32[]{:S(2)}, u32[]{:S(2)}) collective-permute-start(bf16[448,256]{1,0:T(8,128)(2,1)S(1)} %collective-permute-done.3.rest_3_), channel_id=1, source_target_pairs={{0,384},{64,448},{128,0},{192,64},{256,128},{320,192},{384,256},{4... | collective-permute-start | bytes 688136 | tf_op jit(solution)/shard_map/ppermute | solution.py:173
  71.8 1.9 %collective-permute-start.6 = (bf16[256,128]{1,0:T(8,128)(2,1)S(1)}, bf16[256,128]{1,0:T(8,128)(2,1)S(1)}, u32[]{:S(2)}, u32[]{:S(2)}) collective-permute-start(bf16[256,128]{1,0:T(8,128)(2,1)S(1)} %get-tuple-element.46), channel_id=1, source_target_pairs={{0,64},{64,0},{128,192},{192,128},{256,320},{320,256},{384,448},{4... | collective-permute-start | bytes 196616 | tf_op jit(solution)/shard_map/ppermute | solution.py:176
  73.8 2.6 %turn.1 = (bf16[3584,512]{1,0:T(8,128)(2,1)S(1)}, bf16[512,896]{1,0:T(8,128)(2,1)S(1)}, bf16[896,512]{1,0:T(8,128)(2,1)S(1)}) custom-call(s32[2]{0:T(128)S(1)} %pad_add_fusion.place, bf16[256,3584]{1,0:T(8,128)(2,1)S(1)} %bitcast.16, bf16[256,3584]{1,0:T(8,128)(2,1)} %collective-permute-done.tok_theirs), custom_call_target="tpu_custom_call" | custom-call | tf_op jit(solution)/shard_map/turn/pallas_call | solution.py:225
  76.5 0.5 collective-permute-done.2.rest_2_
  76.9 2.6 %partial.1 = f32[512,256]{1,0:T(8,128)S(1)} custom-call(s32[2]{0:T(128)S(1)} %pad_add_fusion.place, bf16[256,3584]{1,0:T(8,128)(2,1)S(1)} %bitcast.17, bf16[256,3584]{1,0:T(8,128)(2,1)} %collective-permute-done.tok_theirs, bf16[448,256]{1,0:T(8,128)(2,1)S(1)} %get-tuple-element.40.rest_0_, bf16[448,256]{1,0:T(8,128)(2,1)S(1)} %collective-permute-done.1.rest_1_, ...), custom_call_target="tpu_custom_call" | custom-call | tf_op jit(solution)/shard_map/partial/pallas_call | solution.py:238
  79.5 4.1 %collective-permute-done.7.piece_mine = bf16[448,256]{1,0:T(8,128)(2,1)S(1)} collective-permute-done((bf16[448,256]{1,0:T(8,128)(2,1)S(1)}, bf16[448,256]{1,0:T(8,128)(2,1)S(1)}, u32[]{:S(2)}, u32[]{:S(2)}) %collective-permute-start.7) | collective-permute-done | bytes 229408 | tf_op jit(solution)/shard_map/ppermute | solution.py:173
  83.6 1.6 collective-permute-done.8.piece_theirs
  85.2 1.5 project.1
  86.7 4.7 %collective-permute-start.9 = (bf16[448,256]{1,0:T(8,128)(2,1)S(1)}, bf16[448,256]{1,0:T(8,128)(2,1)S(1)}, u32[]{:S(2)}, u32[]{:S(2)}) collective-permute-start(bf16[448,256]{1,0:T(8,128)(2,1)S(1)} %get-tuple-element.23), channel_id=1, source_target_pairs={{0,128},{64,192},{128,256},{192,320},{256,384},{320,448},{384,0},{... | collective-permute-start | bytes 688136 | tf_op jit(solution)/shard_map/ppermute | solution.py:173
  91.5 3.2 %collective-permute-start.11 = (bf16[448,256]{1,0:T(8,128)(2,1)S(1)}, bf16[448,256]{1,0:T(8,128)(2,1)S(1)}, u32[]{:S(2)}, u32[]{:S(2)}) collective-permute-start(bf16[448,256]{1,0:T(8,128)(2,1)S(1)} %get-tuple-element.25), channel_id=1, source_target_pairs={{0,384},{64,448},{128,0},{192,64},{256,128},{320,192},{384,256},{4... | collective-permute-start | bytes 688136 | tf_op jit(solution)/shard_map/ppermute | solution.py:173
  94.7 1.4 terms.1
  96.1 3.5 %collective-permute-done.9 = bf16[448,256]{1,0:T(8,128)(2,1)S(1)} collective-permute-done((bf16[448,256]{1,0:T(8,128)(2,1)S(1)}, bf16[448,256]{1,0:T(8,128)(2,1)S(1)}, u32[]{:S(2)}, u32[]{:S(2)}) %collective-permute-start.9) | collective-permute-done | bytes 229408 | tf_op jit(solution)/shard_map/ppermute | solution.py:173
  99.7 4.1 %collective-permute-start.10 = (bf16[448,256]{1,0:T(8,128)(2,1)S(1)}, bf16[448,256]{1,0:T(8,128)(2,1)S(1)}, u32[]{:S(2)}, u32[]{:S(2)}) collective-permute-start(bf16[448,256]{1,0:T(8,128)(2,1)S(1)} %add_convert_fusion.3), channel_id=1, source_target_pairs={{0,128},{64,192},{128,256},{192,320},{256,384},{320,448},{384,0},{... | collective-permute-start | bytes 688136 | tf_op jit(solution)/shard_map/ppermute | solution.py:173
  103.8 3.9 %collective-permute-start.12 = (bf16[448,256]{1,0:T(8,128)(2,1)S(1)}, bf16[448,256]{1,0:T(8,128)(2,1)S(1)}, u32[]{:S(2)}, u32[]{:S(2)}) collective-permute-start(bf16[448,256]{1,0:T(8,128)(2,1)S(1)} %add_convert_fusion.2), channel_id=1, source_target_pairs={{0,384},{64,448},{128,0},{192,64},{256,128},{320,192},{384,256},{4... | collective-permute-start | bytes 688136 | tf_op jit(solution)/shard_map/ppermute | solution.py:173
  107.7 2.8 %collective-permute-start.15 = (bf16[448,256]{1,0:T(8,128)(2,1)S(1)}, bf16[448,256]{1,0:T(8,128)(2,1)S(1)}, u32[]{:S(2)}, u32[]{:S(2)}) collective-permute-start(bf16[448,256]{1,0:T(8,128)(2,1)S(1)} %get-tuple-element.31), channel_id=1, source_target_pairs={{0,128},{64,192},{128,256},{192,320},{256,384},{320,448},{384,0},{... | collective-permute-start | bytes 688136 | tf_op jit(solution)/shard_map/ppermute | solution.py:173
  110.6 5.1 %collective-permute-start.14 = (bf16[448,256]{1,0:T(8,128)(2,1)S(1)}, bf16[448,256]{1,0:T(8,128)(2,1)S(1)}, u32[]{:S(2)}, u32[]{:S(2)}) collective-permute-start(bf16[448,256]{1,0:T(8,128)(2,1)S(1)} %get-tuple-element.28), channel_id=1, source_target_pairs={{0,384},{64,448},{128,0},{192,64},{256,128},{320,192},{384,256},{4... | collective-permute-start | bytes 688136 | tf_op jit(solution)/shard_map/ppermute | solution.py:173
  115.7 5.2 %collective-permute-done.15 = bf16[448,256]{1,0:T(8,128)(2,1)S(1)} collective-permute-done((bf16[448,256]{1,0:T(8,128)(2,1)S(1)}, bf16[448,256]{1,0:T(8,128)(2,1)S(1)}, u32[]{:S(2)}, u32[]{:S(2)}) %collective-permute-start.15) | collective-permute-done | bytes 229408 | tf_op jit(solution)/shard_map/ppermute | solution.py:173
  121.0 1.9 %collective-permute-start.16 = (bf16[448,256]{1,0:T(8,128)(2,1)S(1)}, bf16[448,256]{1,0:T(8,128)(2,1)S(1)}, u32[]{:S(2)}, u32[]{:S(2)}) collective-permute-start(bf16[448,256]{1,0:T(8,128)(2,1)S(1)} %add_convert_fusion), channel_id=1, source_target_pairs={{0,64},{64,0},{128,192},{192,128},{256,320},{320,256},{384,448},{4... | collective-permute-start | bytes 688136 | tf_op jit(solution)/shard_map/ppermute | solution.py:176
  123.0 1.5 collective-permute-done.14
  124.8 32.2 %all_to_all.20 = bf16[64,7,512]{2,1,0:T(8,128)(2,1)S(1)} all-to-all(bf16[64,7,512]{2,1,0:T(8,128)(2,1)S(1)} %reshape.32), channel_id=1, replica_groups=mesh['dp'=8,'expert'=64] {'expert'}, dimensions={0} | all-to-all | bytes 917504 | tf_op jit(solution)/shard_map/all_to_all | solution.py:164
  157.0 0.3 convolution_convert_fusion.2
  157.4 1.1 copy.23
  158.4 5.2 %all-to-all-start.3 = ((bf16[64,7,512]{2,1,0:T(8,128)(2,1)}), bf16[64,7,512]{2,1,0:T(8,128)(2,1)S(1)}, u32[]{:S(2)}, u32[]{:S(2)}) async-start(bf16[64,7,512]{2,1,0:T(8,128)(2,1)} %copy.23), calls=%async_computation.3 | async-start | bytes 1048576 | tf_op jit(solution)/shard_map/all_to_all | solution.py:164
  163.6 1.7 fusion.24
  165.3 0.2 pad_maximum_fusion
  165.5 0.2 reshape.30.first
  165.8 16.0 %all-to-all-done.3 = bf16[64,7,512]{2,1,0:T(8,128)(2,1)S(1)} async-done(((bf16[64,7,512]{2,1,0:T(8,128)(2,1)}), bf16[64,7,512]{2,1,0:T(8,128)(2,1)S(1)}, u32[]{:S(2)}, u32[]{:S(2)}) %all-to-all-start.3) | async-done | bytes 458784 | tf_op jit(solution)/shard_map/all_to_all | solution.py:164
  182.0 2.8 %adam.1 = (bf16[1,448,512]{2,1,0:T(8,128)(2,1)}, f32[1,448,512]{2,1,0:T(8,128)}, f32[1,448,512]{2,1,0:T(8,128)}) custom-call(s32[2]{0:T(128)S(1)} %pad_add_fusion.place, bf16[448,512]{1,0:T(8,128)(2,1)S(1)} %reshape.29.params, bf16[448,512]{1,0:T(8,128)(2,1)S(1)} %reshape.30.first, bf16[448,512]{1,0:T(8,128)(2,1)S(1)} %reshape.31.second, ...), custom_call_target="tpu_custom_call" | custom-call | tf_op jit(solution)/shard_map/adam/pallas_call | solution.py:288
  (40 shorter events, 1.3 us)
Async XLA Ops:
  0.6 18.1 %copy-start = (bf16[1,1,256,3584]{3,2,1,0:T(8,128)(2,1)S(1)}, bf16[1,1,256,3584]{3,2,1,0:T(8,128)(2,1)}, u32[]{:S(2)}) copy-start(bf16[1,1,256,3584]{3,2,1,0:T(8,128)(2,1)} %param.12) | copy-start | bytes 5505028
  0.6 20.1 %copy-start.1 = (f32[16,7,512]{2,0,1:T(8,128)S(1)}, f32[16,7,512]{2,0,1:T(8,128)}, u32[]{:S(2)}) copy-start(f32[16,7,512]{2,0,1:T(8,128)} %param.8) | copy-start | bytes 688132
  0.7 20.1 %copy-start.2 = (f32[16,7,512]{2,0,1:T(8,128)S(1)}, f32[16,7,512]{2,0,1:T(8,128)}, u32[]{:S(2)}) copy-start(f32[16,7,512]{2,0,1:T(8,128)} %param.9) | copy-start | bytes 688132
  3.7 19.5 %copy-start.4 = (s32[64]{0:T(128)S(1)}, s32[64]{0:T(128)}, u32[]{:S(2)}) copy-start(s32[64]{0:T(128)} %param.10) | copy-start | bytes 772
  3.7 33.5 %all-to-all-start = ((bf16[64,7,512]{2,1,0:T(8,128)(2,1)}), bf16[64,7,512]{2,1,0:T(8,128)(2,1)S(1)}, u32[]{:S(2)}, u32[]{:S(2)}) async-start(bf16[64,7,512]{2,1,0:T(8,128)(2,1)} %copy.20), calls=%async_computation | async-start | bytes 1048576 | tf_op jit(solution)/shard_map/all_to_all | solution.py:164
  18.8 53.1 %collective-permute-start = (bf16[256,3584]{1,0:T(8,128)(2,1)S(1)}, bf16[256,3584]{1,0:T(8,128)(2,1)}, u32[]{:S(2)}, u32[]{:S(2)}) collective-permute-start(bf16[256,3584]{1,0:T(8,128)(2,1)S(1)} %bitcast.15), channel_id=1, source_target_pairs={{0,64},{64,0},{128,192},{192,128},{256,320},{320,256},{384,448},{4... | collective-permute-start | bytes 5505032 | tf_op jit(solution)/shard_map/ppermute | solution.py:176
  20.9 9.9 %collective-permute-start.13 = (bf16[16,14,512]{2,0,1:T(8,128)(2,1)S(1)}, bf16[16,14,512]{2,0,1:T(8,128)(2,1)S(1)}, u32[]{:S(2)}, u32[]{:S(2)}) collective-permute-start(bf16[16,14,512]{2,0,1:T(8,128)(2,1)S(1)} %pad_maximum_fusion.3), channel_id=1, source_target_pairs={{0,32},{1,33},{2,34},{3,35},{4,36},{5,37},{6,38},{7,39},{8,40},{9,... | collective-permute-start | bytes 688136 | tf_op jit(solution)/shard_map/ppermute | solution.py:214
  32.9 20.6 %copy-start.3 = (bf16[1,1,256,256]{3,2,1,0:T(8,128)(2,1)S(1)}, bf16[1,1,256,256]{3,2,1,0:T(8,128)(2,1)}, u32[]{:S(2)}) copy-start(bf16[1,1,256,256]{3,2,1,0:T(8,128)(2,1)} %param.13) | copy-start | bytes 393220
  37.2 78.5 %all-to-all-start.1 = ((bf16[32,28,512]{2,1,0:T(8,128)(2,1)}), bf16[32,28,512]{2,1,0:T(8,128)(2,1)}, u32[]{:S(2)}, u32[]{:S(2)}) async-start(bf16[32,28,512]{2,1,0:T(8,128)(2,1)} %copy.21), calls=%async_computation.1 | async-start | bytes 2097152 | tf_op jit(solution)/shard_map/all_to_all | solution.py:220
  42.9 7.1 %collective-permute-start.1 = (bf16[448,256]{1,0:T(8,128)(2,1)S(1)}, bf16[448,256]{1,0:T(8,128)(2,1)S(1)}, u32[]{:S(2)}, u32[]{:S(2)}) collective-permute-start(bf16[448,256]{1,0:T(8,128)(2,1)S(1)} %get-tuple-element.39), channel_id=1, source_target_pairs={{0,64},{64,0},{128,192},{192,128},{256,320},{320,256},{384,448},{4... | collective-permute-start | bytes 688136 | tf_op jit(solution)/shard_map/ppermute | solution.py:176
  45.5 17.0 %collective-permute-start.4 = (bf16[448,256]{1,0:T(8,128)(2,1)S(1)}, bf16[448,256]{1,0:T(8,128)(2,1)S(1)}, u32[]{:S(2)}, u32[]{:S(2)}) collective-permute-start(bf16[448,256]{1,0:T(8,128)(2,1)S(1)} %get-tuple-element.40.rest_0_), channel_id=1, source_target_pairs={{0,128},{64,192},{128,256},{192,320},{256,384},{320,448},{384,0},{... | collective-permute-start | bytes 688136 | tf_op jit(solution)/shard_map/ppermute | solution.py:173
  50.0 16.7 %collective-permute-start.3 = (bf16[448,256]{1,0:T(8,128)(2,1)S(1)}, bf16[448,256]{1,0:T(8,128)(2,1)S(1)}, u32[]{:S(2)}, u32[]{:S(2)}) collective-permute-start(bf16[448,256]{1,0:T(8,128)(2,1)S(1)} %collective-permute-done.1.rest_1_), channel_id=1, source_target_pairs={{0,384},{64,448},{128,0},{192,64},{256,128},{320,192},{384,256},{4... | collective-permute-start | bytes 688136 | tf_op jit(solution)/shard_map/ppermute | solution.py:173
  53.6 23.3 %collective-permute-start.2 = (bf16[448,256]{1,0:T(8,128)(2,1)S(1)}, bf16[448,256]{1,0:T(8,128)(2,1)S(1)}, u32[]{:S(2)}, u32[]{:S(2)}) collective-permute-start(bf16[448,256]{1,0:T(8,128)(2,1)S(1)} %get-tuple-element.40.rest_0_), channel_id=1, source_target_pairs={{0,384},{64,448},{128,0},{192,64},{256,128},{320,192},{384,256},{4... | collective-permute-start | bytes 688136 | tf_op jit(solution)/shard_map/ppermute | solution.py:173
  57.7 19.3 %collective-permute-start.5 = (bf16[448,256]{1,0:T(8,128)(2,1)S(1)}, bf16[448,256]{1,0:T(8,128)(2,1)S(1)}, u32[]{:S(2)}, u32[]{:S(2)}) collective-permute-start(bf16[448,256]{1,0:T(8,128)(2,1)S(1)} %collective-permute-done.1.rest_1_), channel_id=1, source_target_pairs={{0,128},{64,192},{128,256},{192,320},{256,384},{320,448},{384,0},{... | collective-permute-start | bytes 688136 | tf_op jit(solution)/shard_map/ppermute | solution.py:173
  62.5 21.1 %collective-permute-start.7 = (bf16[448,256]{1,0:T(8,128)(2,1)S(1)}, bf16[448,256]{1,0:T(8,128)(2,1)S(1)}, u32[]{:S(2)}, u32[]{:S(2)}) collective-permute-start(bf16[448,256]{1,0:T(8,128)(2,1)S(1)} %collective-permute-done.4.rest_4_), channel_id=1, source_target_pairs={{0,128},{64,192},{128,256},{192,320},{256,384},{320,448},{384,0},{... | collective-permute-start | bytes 688136 | tf_op jit(solution)/shard_map/ppermute | solution.py:173
  66.7 18.5 %collective-permute-start.8 = (bf16[448,256]{1,0:T(8,128)(2,1)S(1)}, bf16[448,256]{1,0:T(8,128)(2,1)S(1)}, u32[]{:S(2)}, u32[]{:S(2)}) collective-permute-start(bf16[448,256]{1,0:T(8,128)(2,1)S(1)} %collective-permute-done.3.rest_3_), channel_id=1, source_target_pairs={{0,384},{64,448},{128,0},{192,64},{256,128},{320,192},{384,256},{4... | collective-permute-start | bytes 688136 | tf_op jit(solution)/shard_map/ppermute | solution.py:173
  71.8 7.7 %collective-permute-start.6 = (bf16[256,128]{1,0:T(8,128)(2,1)S(1)}, bf16[256,128]{1,0:T(8,128)(2,1)S(1)}, u32[]{:S(2)}, u32[]{:S(2)}) collective-permute-start(bf16[256,128]{1,0:T(8,128)(2,1)S(1)} %get-tuple-element.46), channel_id=1, source_target_pairs={{0,64},{64,0},{128,192},{192,128},{256,320},{320,256},{384,448},{4... | collective-permute-start | bytes 196616 | tf_op jit(solution)/shard_map/ppermute | solution.py:176
  86.7 12.9 %collective-permute-start.9 = (bf16[448,256]{1,0:T(8,128)(2,1)S(1)}, bf16[448,256]{1,0:T(8,128)(2,1)S(1)}, u32[]{:S(2)}, u32[]{:S(2)}) collective-permute-start(bf16[448,256]{1,0:T(8,128)(2,1)S(1)} %get-tuple-element.23), channel_id=1, source_target_pairs={{0,128},{64,192},{128,256},{192,320},{256,384},{320,448},{384,0},{... | collective-permute-start | bytes 688136 | tf_op jit(solution)/shard_map/ppermute | solution.py:173
  91.5 12.3 %collective-permute-start.11 = (bf16[448,256]{1,0:T(8,128)(2,1)S(1)}, bf16[448,256]{1,0:T(8,128)(2,1)S(1)}, u32[]{:S(2)}, u32[]{:S(2)}) collective-permute-start(bf16[448,256]{1,0:T(8,128)(2,1)S(1)} %get-tuple-element.25), channel_id=1, source_target_pairs={{0,384},{64,448},{128,0},{192,64},{256,128},{320,192},{384,256},{4... | collective-permute-start | bytes 688136 | tf_op jit(solution)/shard_map/ppermute | solution.py:173
  99.7 16.0 %collective-permute-start.10 = (bf16[448,256]{1,0:T(8,128)(2,1)S(1)}, bf16[448,256]{1,0:T(8,128)(2,1)S(1)}, u32[]{:S(2)}, u32[]{:S(2)}) collective-permute-start(bf16[448,256]{1,0:T(8,128)(2,1)S(1)} %add_convert_fusion.3), channel_id=1, source_target_pairs={{0,128},{64,192},{128,256},{192,320},{256,384},{320,448},{384,0},{... | collective-permute-start | bytes 688136 | tf_op jit(solution)/shard_map/ppermute | solution.py:173
  103.8 11.9 %collective-permute-start.12 = (bf16[448,256]{1,0:T(8,128)(2,1)S(1)}, bf16[448,256]{1,0:T(8,128)(2,1)S(1)}, u32[]{:S(2)}, u32[]{:S(2)}) collective-permute-start(bf16[448,256]{1,0:T(8,128)(2,1)S(1)} %add_convert_fusion.2), channel_id=1, source_target_pairs={{0,384},{64,448},{128,0},{192,64},{256,128},{320,192},{384,256},{4... | collective-permute-start | bytes 688136 | tf_op jit(solution)/shard_map/ppermute | solution.py:173
  107.7 13.2 %collective-permute-start.15 = (bf16[448,256]{1,0:T(8,128)(2,1)S(1)}, bf16[448,256]{1,0:T(8,128)(2,1)S(1)}, u32[]{:S(2)}, u32[]{:S(2)}) collective-permute-start(bf16[448,256]{1,0:T(8,128)(2,1)S(1)} %get-tuple-element.31), channel_id=1, source_target_pairs={{0,128},{64,192},{128,256},{192,320},{256,384},{320,448},{384,0},{... | collective-permute-start | bytes 688136 | tf_op jit(solution)/shard_map/ppermute | solution.py:173
  110.6 13.9 %collective-permute-start.14 = (bf16[448,256]{1,0:T(8,128)(2,1)S(1)}, bf16[448,256]{1,0:T(8,128)(2,1)S(1)}, u32[]{:S(2)}, u32[]{:S(2)}) collective-permute-start(bf16[448,256]{1,0:T(8,128)(2,1)S(1)} %get-tuple-element.28), channel_id=1, source_target_pairs={{0,384},{64,448},{128,0},{192,64},{256,128},{320,192},{384,256},{4... | collective-permute-start | bytes 688136 | tf_op jit(solution)/shard_map/ppermute | solution.py:173
  121.0 3.6 %collective-permute-start.16 = (bf16[448,256]{1,0:T(8,128)(2,1)S(1)}, bf16[448,256]{1,0:T(8,128)(2,1)S(1)}, u32[]{:S(2)}, u32[]{:S(2)}) collective-permute-start(bf16[448,256]{1,0:T(8,128)(2,1)S(1)} %add_convert_fusion), channel_id=1, source_target_pairs={{0,64},{64,0},{128,192},{192,128},{256,320},{320,256},{384,448},{4... | collective-permute-start | bytes 688136 | tf_op jit(solution)/shard_map/ppermute | solution.py:176
  158.4 23.5 %all-to-all-start.3 = ((bf16[64,7,512]{2,1,0:T(8,128)(2,1)}), bf16[64,7,512]{2,1,0:T(8,128)(2,1)S(1)}, u32[]{:S(2)}, u32[]{:S(2)}) async-start(bf16[64,7,512]{2,1,0:T(8,128)(2,1)} %copy.23), calls=%async_computation.3 | async-start | bytes 1048576 | tf_op jit(solution)/shard_map/all_to_all | solution.py:164

commit v4 on v3

--- a/solution.py
+++ b/solution.py
@@ -166,9 +166,11 @@
     def choose(table, values):
         return jnp.einsum("jk,krc->jrc", table, values, preferred_element_type=jnp.float32).astype(narrow)
 
-    def shift(value, step):
+    def shift(value, step, cross=0):
         pairs = [
-            (2 * h + c, 2 * ((h + step) % chip_count) + c) for h in range(chip_count) for c in range(2)
+            (2 * h + c, 2 * ((h + step) % chip_count) + (c ^ cross))
+            for h in range(chip_count)
+            for c in range(2)
         ]
         return lax.ppermute(value, "dp", pairs)
 
@@ -204,8 +206,8 @@
     plus_mine = shift(mine, 1)
     minus_mine = shift(mine, -1)
     theirs = swap(give)
-    minus_theirs = shift(theirs, -1)
-    plus_theirs = shift(theirs, 1)
+    minus_theirs = shift(give, -1, 1)
+    plus_theirs = shift(give, 1, 1)
     far_mine = shift(plus_mine, 1)
     far_theirs = shift(minus_theirs, -1)
 
@@ -263,13 +265,15 @@
         name="terms",
         compiler_params=pltpu.CompilerParams(vmem_limit_bytes=8 * MEBI),
     )(place, turned, grad_proj)
-    early_theirs = shift(next_theirs, 1)
+    early_other = shift(next_theirs, 1, 1)
     early_mine = shift(last_mine, -1)
+    base_other = swap(sum_theirs)
     late_mine = shift(add(next_mine, got_plus), 1)
-    late_theirs = shift(add(last_theirs, got_minus), -1)
-    late_mine, late_theirs, moments_here = lax.optimization_barrier((late_mine, late_theirs, moments_here))
-    total_other = swap(add(sum_theirs, early_theirs, late_theirs))
-    total = jnp.concatenate([add(sum_mine, early_mine, late_mine), total_other], axis=1)
+    late_other = shift(add(last_theirs, got_minus), -1, 1)
+    late_mine, late_other, moments_here = lax.optimization_barrier((late_mine, late_other, moments_here))
+    total = jnp.concatenate(
+        [add(sum_mine, early_mine, late_mine), add(base_other, early_other, late_other)], axis=1
+    )
     home = exchange(total.reshape(expert_count, span_rows, col_total))
 
     def moment_rows(kind):
@@ -280,7 +284,7 @@
         return rows_of(jnp.concatenate(sides, axis=0))
 
     grad_rows = rows_of(exchange(choose(same, home)))
-    bands = chip_count
+    bands = span_rows
     band = own_count // bands
     spec = pl.BlockSpec((band, col_total), lambda i: (i, 0))
     out_spec = pl.BlockSpec((1, band, col_total), lambda i: (0, i, 0))

time: 186 us -> 195 us (1.048)
  the two profiles are of different devices: /device:TPU:8 before, /device:TPU:56 now
where the time goes in v4:
time: 195 us; the launch traced here: 194 us
  starting transfers between devices  79.1 us (41%)
  waiting for transfers between devices  59.2 us (30%)
  blocking collectives  29.4 us (15%)
  Pallas kernels  12 us (6%)
  local copies, waits for them, and re-layouts  7.31 us (4%)
  other arithmetic  3.3 us (2%)
    ppermute x12, starting transfers between devices, shift(): return lax.ppermute(value, 'dp', pairs)  44.6 us
    all_to_all x1, blocking collectives, exchange(): lax.all_to_all(values, 'expert', split_axis=0, concat_axis=0, tiled=True)  29.4 us
    ppermute x12, waiting for transfers between devices, shift(): return lax.ppermute(value, 'dp', pairs)  27.8 us
    all_to_all x2, waiting for transfers between devices, exchange(): lax.all_to_all(values, 'expert', split_axis=0, concat_axis=0, tiled=True)  22.8 us
    all_to_all x2, starting transfers between devices, exchange(): lax.all_to_all(values, 'expert', split_axis=0, concat_axis=0, tiled=True)  20.3 us
    ppermute x1, waiting for transfers between devices, on_device(): lax.ppermute(stored, 'expert', [(e, (e + group) % expert_count) for e in...  8.52 us
    ppermute x4, starting transfers between devices, swap(): return lax.ppermute(value, 'dp', [(i, i ^ 1) for i in range(dp_count)])  7.82 us
    all_to_all x1, starting transfers between devices, on_device(): lax.all_to_all(moments_sent, 'expert', split_axis=0, concat_axis=0, tiled...  4.21 us
  transfers between devices with their start and end apart: 20, of which 10 were waited for; matrix products, arithmetic and copies ran while one was open for 5% of the time, Pallas kernels for 4%

profile of v4, /device:TPU:56, one launch (start us, length us, event | category | flops | bytes accessed | tf_op | source)
XLA Modules:
  0.0 194.0 jit_solution(10879948993817093565)
XLA Ops:
  0.7 2.1 %collective-permute-start = (bf16[256,3584]{1,0:T(8,128)(2,1)}, bf16[256,3584]{1,0:T(8,128)(2,1)}, u32[]{:S(2)}, u32[]{:S(2)}) collective-permute-start(bf16[256,3584]{1,0:T(8,128)(2,1)} %bitcast.15), channel_id=1, source_target_pairs={{0,64},{64,0},{128,192},{192,128},{256,320},{320,256},{384,448},{4... | collective-permute-start | bytes 5505032 | tf_op jit(solution)/shard_map/ppermute | solution.py:178
  2.7 0.8 fusion.26
  3.6 1.0 convolution_convert_fusion.1
  4.6 1.1 copy.20
  5.6 15.0 %all-to-all-start = ((bf16[64,7,512]{2,1,0:T(8,128)(2,1)}), bf16[64,7,512]{2,1,0:T(8,128)(2,1)S(1)}, u32[]{:S(2)}, u32[]{:S(2)}) async-start(bf16[64,7,512]{2,1,0:T(8,128)(2,1)} %copy.20), calls=%async_computation | async-start | bytes 1048576 | tf_op jit(solution)/shard_map/all_to_all | solution.py:164
  20.8 2.3 %collective-permute-start.13 = (bf16[16,14,512]{2,0,1:T(8,128)(2,1)S(1)}, bf16[16,14,512]{2,0,1:T(8,128)(2,1)S(1)}, u32[]{:S(2)}, u32[]{:S(2)}) collective-permute-start(bf16[16,14,512]{2,0,1:T(8,128)(2,1)S(1)} %pad_maximum_fusion.3), channel_id=1, source_target_pairs={{0,32},{1,33},{2,34},{3,35},{4,36},{5,37},{6,38},{7,39},{8,40},{9,... | collective-permute-start | bytes 688136 | tf_op jit(solution)/shard_map/ppermute | solution.py:216
  23.8 8.5 %collective-permute-done.13 = bf16[16,14,512]{2,0,1:T(8,128)(2,1)S(1)} collective-permute-done((bf16[16,14,512]{2,0,1:T(8,128)(2,1)S(1)}, bf16[16,14,512]{2,0,1:T(8,128)(2,1)S(1)}, u32[]{:S(2)}, u32[]{:S(2)}) %collective-permute-start.13) | collective-permute-done | bytes 229408 | tf_op jit(solution)/shard_map/ppermute | solution.py:216
  32.4 0.5 convolution_convert_fusion
  32.9 1.5 copy.21
  34.4 5.3 %all-to-all-done = bf16[64,7,512]{2,1,0:T(8,128)(2,1)S(1)} async-done(((bf16[64,7,512]{2,1,0:T(8,128)(2,1)}), bf16[64,7,512]{2,1,0:T(8,128)(2,1)S(1)}, u32[]{:S(2)}, u32[]{:S(2)}) %all-to-all-start) | async-done | bytes 458784 | tf_op jit(solution)/shard_map/all_to_all | solution.py:164
  39.8 0.8 copy-done.1
  40.6 4.2 %all-to-all-start.1 = ((bf16[32,28,512]{2,1,0:T(8,128)(2,1)}), bf16[32,28,512]{2,1,0:T(8,128)(2,1)S(1)}, u32[]{:S(2)}, u32[]{:S(2)}) async-start(bf16[32,28,512]{2,1,0:T(8,128)(2,1)} %copy.21), calls=%async_computation.1 | async-start | bytes 2097152 | tf_op jit(solution)/shard_map/all_to_all | solution.py:222
  44.8 1.2 reshape.29.params
  46.1 1.9 collective-permute-start.1
  48.0 4.2 %collective-permute-start.3 = (bf16[448,256]{1,0:T(8,128)(2,1)S(1)}, bf16[448,256]{1,0:T(8,128)(2,1)S(1)}, u32[]{:S(2)}, u32[]{:S(2)}) collective-permute-start(bf16[448,256]{1,0:T(8,128)(2,1)S(1)} %get-tuple-element.39), channel_id=1, source_target_pairs={{0,448},{64,384},{128,64},{192,0},{256,192},{320,128},{384,320},{4... | collective-permute-start | bytes 688136 | tf_op jit(solution)/shard_map/ppermute | solution.py:175
  52.2 3.9 %collective-permute-start.4 = (bf16[448,256]{1,0:T(8,128)(2,1)S(1)}, bf16[448,256]{1,0:T(8,128)(2,1)S(1)}, u32[]{:S(2)}, u32[]{:S(2)}) collective-permute-start(bf16[448,256]{1,0:T(8,128)(2,1)S(1)} %get-tuple-element.40.rest_0_), channel_id=1, source_target_pairs={{0,128},{64,192},{128,256},{192,320},{256,384},{320,448},{384,0},{... | collective-permute-start | bytes 688136 | tf_op jit(solution)/shard_map/ppermute | solution.py:175
  56.2 2.8 %collective-permute-start.2 = (bf16[448,256]{1,0:T(8,128)(2,1)S(1)}, bf16[448,256]{1,0:T(8,128)(2,1)S(1)}, u32[]{:S(2)}, u32[]{:S(2)}) collective-permute-start(bf16[448,256]{1,0:T(8,128)(2,1)S(1)} %get-tuple-element.40.rest_0_), channel_id=1, source_target_pairs={{0,384},{64,448},{128,0},{192,64},{256,128},{320,192},{384,256},{4... | collective-permute-start | bytes 688136 | tf_op jit(solution)/shard_map/ppermute | solution.py:175
  59.0 4.2 %collective-permute-start.5 = (bf16[448,256]{1,0:T(8,128)(2,1)S(1)}, bf16[448,256]{1,0:T(8,128)(2,1)S(1)}, u32[]{:S(2)}, u32[]{:S(2)}) collective-permute-start(bf16[448,256]{1,0:T(8,128)(2,1)S(1)} %get-tuple-element.39), channel_id=1, source_target_pairs={{0,192},{64,128},{128,320},{192,256},{256,448},{320,384},{384,64},... | collective-permute-start | bytes 688136 | tf_op jit(solution)/shard_map/ppermute | solution.py:175
  63.2 5.1 %collective-permute-done.4.rest_4_ = bf16[448,256]{1,0:T(8,128)(2,1)S(1)} collective-permute-done((bf16[448,256]{1,0:T(8,128)(2,1)S(1)}, bf16[448,256]{1,0:T(8,128)(2,1)S(1)}, u32[]{:S(2)}, u32[]{:S(2)}) %collective-permute-start.4) | collective-permute-done | bytes 229408 | tf_op jit(solution)/shard_map/ppermute | solution.py:175
  68.3 3.0 %collective-permute-start.7 = (bf16[448,256]{1,0:T(8,128)(2,1)S(1)}, bf16[448,256]{1,0:T(8,128)(2,1)S(1)}, u32[]{:S(2)}, u32[]{:S(2)}) collective-permute-start(bf16[448,256]{1,0:T(8,128)(2,1)S(1)} %collective-permute-done.4.rest_4_), channel_id=1, source_target_pairs={{0,128},{64,192},{128,256},{192,320},{256,384},{320,448},{384,0},{... | collective-permute-start | bytes 688136 | tf_op jit(solution)/shard_map/ppermute | solution.py:175
  71.3 3.8 %collective-permute-start.8 = (bf16[448,256]{1,0:T(8,128)(2,1)S(1)}, bf16[448,256]{1,0:T(8,128)(2,1)S(1)}, u32[]{:S(2)}, u32[]{:S(2)}) collective-permute-start(bf16[448,256]{1,0:T(8,128)(2,1)S(1)} %collective-permute-done.3.rest_3_), channel_id=1, source_target_pairs={{0,384},{64,448},{128,0},{192,64},{256,128},{320,192},{384,256},{4... | collective-permute-start | bytes 688136 | tf_op jit(solution)/shard_map/ppermute | solution.py:175
  75.1 1.9 collective-permute-start.6
  77.1 2.6 %turn.1 = (bf16[3584,512]{1,0:T(8,128)(2,1)S(1)}, bf16[512,896]{1,0:T(8,128)(2,1)S(1)}, bf16[896,512]{1,0:T(8,128)(2,1)S(1)}) custom-call(s32[2]{0:T(128)S(1)} %pad_add_fusion.place, bf16[256,3584]{1,0:T(8,128)(2,1)S(1)} %bitcast.16, bf16[256,3584]{1,0:T(8,128)(2,1)} %collective-permute-done.tok_theirs), custom_call_target="tpu_custom_call" | custom-call | tf_op jit(solution)/shard_map/turn/pallas_call | solution.py:227
  79.8 2.6 %partial.1 = f32[512,256]{1,0:T(8,128)S(1)} custom-call(s32[2]{0:T(128)S(1)} %pad_add_fusion.place, bf16[256,3584]{1,0:T(8,128)(2,1)S(1)} %bitcast.17, bf16[256,3584]{1,0:T(8,128)(2,1)} %collective-permute-done.tok_theirs, bf16[448,256]{1,0:T(8,128)(2,1)S(1)} %get-tuple-element.40.rest_0_, bf16[448,256]{1,0:T(8,128)(2,1)S(1)} %collective-permute-done.1.rest_1_, ...), custom_call_target="tpu_custom_call" | custom-call | tf_op jit(solution)/shard_map/partial/pallas_call | solution.py:240
  82.4 2.0 %collective-permute-done.7.piece_mine = bf16[448,256]{1,0:T(8,128)(2,1)S(1)} collective-permute-done((bf16[448,256]{1,0:T(8,128)(2,1)S(1)}, bf16[448,256]{1,0:T(8,128)(2,1)S(1)}, u32[]{:S(2)}, u32[]{:S(2)}) %collective-permute-start.7) | collective-permute-done | bytes 229408 | tf_op jit(solution)/shard_map/ppermute | solution.py:175
  84.3 1.8 collective-permute-done.8.piece_theirs
  86.1 1.5 project.1
  87.6 3.2 %collective-permute-start.9 = (bf16[448,256]{1,0:T(8,128)(2,1)S(1)}, bf16[448,256]{1,0:T(8,128)(2,1)S(1)}, u32[]{:S(2)}, u32[]{:S(2)}) collective-permute-start(bf16[448,256]{1,0:T(8,128)(2,1)S(1)} %get-tuple-element.23), channel_id=1, source_target_pairs={{0,128},{64,192},{128,256},{192,320},{256,384},{320,448},{384,0},{... | collective-permute-start | bytes 688136 | tf_op jit(solution)/shard_map/ppermute | solution.py:175
  90.7 3.6 %collective-permute-start.11 = (bf16[448,256]{1,0:T(8,128)(2,1)S(1)}, bf16[448,256]{1,0:T(8,128)(2,1)S(1)}, u32[]{:S(2)}, u32[]{:S(2)}) collective-permute-start(bf16[448,256]{1,0:T(8,128)(2,1)S(1)} %get-tuple-element.25), channel_id=1, source_target_pairs={{0,384},{64,448},{128,0},{192,64},{256,128},{320,192},{384,256},{4... | collective-permute-start | bytes 688136 | tf_op jit(solution)/shard_map/ppermute | solution.py:175
  94.3 1.4 terms.1
  95.7 5.1 %collective-permute-done.9 = bf16[448,256]{1,0:T(8,128)(2,1)S(1)} collective-permute-done((bf16[448,256]{1,0:T(8,128)(2,1)S(1)}, bf16[448,256]{1,0:T(8,128)(2,1)S(1)}, u32[]{:S(2)}, u32[]{:S(2)}) %collective-permute-start.9) | collective-permute-done | bytes 229408 | tf_op jit(solution)/shard_map/ppermute | solution.py:175
  100.8 0.7 add_convert_fusion.3
  101.6 6.5 %collective-permute-start.10 = (bf16[448,256]{1,0:T(8,128)(2,1)}, bf16[448,256]{1,0:T(8,128)(2,1)S(1)}, u32[]{:S(2)}, u32[]{:S(2)}) collective-permute-start(bf16[448,256]{1,0:T(8,128)(2,1)} %add_convert_fusion.3), channel_id=1, source_target_pairs={{0,128},{64,192},{128,256},{192,320},{256,384},{320,448},{384,0},{... | collective-permute-start | bytes 688136 | tf_op jit(solution)/shard_map/ppermute | solution.py:175
  108.0 0.7 add_convert_fusion.2
  108.8 1.9 collective-permute-start.12
  110.7 5.8 %collective-permute-start.16 = (bf16[448,256]{1,0:T(8,128)(2,1)S(1)}, bf16[448,256]{1,0:T(8,128)(2,1)S(1)}, u32[]{:S(2)}, u32[]{:S(2)}) collective-permute-start(bf16[448,256]{1,0:T(8,128)(2,1)S(1)} %get-tuple-element.31), channel_id=1, source_target_pairs={{0,192},{64,128},{128,320},{192,256},{256,448},{320,384},{384,64},... | collective-permute-start | bytes 688136 | tf_op jit(solution)/shard_map/ppermute | solution.py:175
  116.5 1.9 collective-permute-start.15
  118.4 1.9 collective-permute-start.14
  120.3 3.8 %collective-permute-done.12 = bf16[448,256]{1,0:T(8,128)(2,1)S(1)} collective-permute-done((bf16[448,256]{1,0:T(8,128)(2,1)}, bf16[448,256]{1,0:T(8,128)(2,1)S(1)}, u32[]{:S(2)}, u32[]{:S(2)}) %collective-permute-start.12) | collective-permute-done | bytes 229408 | tf_op jit(solution)/shard_map/ppermute | solution.py:175
  124.2 1.6 collective-permute-done.16
  125.7 1.0 add_convert_fusion
  126.8 8.5 %collective-permute-done.14 = bf16[448,256]{1,0:T(8,128)(2,1)S(1)} collective-permute-done((bf16[448,256]{1,0:T(8,128)(2,1)S(1)}, bf16[448,256]{1,0:T(8,128)(2,1)S(1)}, u32[]{:S(2)}, u32[]{:S(2)}) %collective-permute-start.14) | collective-permute-done | bytes 229408 | tf_op jit(solution)/shard_map/ppermute | solution.py:175
  135.6 29.4 %all_to_all.20 = bf16[64,7,512]{2,1,0:T(8,128)(2,1)S(1)} all-to-all(bf16[64,7,512]{2,1,0:T(8,128)(2,1)S(1)} %reshape.32), channel_id=1, replica_groups=mesh['dp'=8,'expert'=64] {'expert'}, dimensions={0} | all-to-all | bytes 917504 | tf_op jit(solution)/shard_map/all_to_all | solution.py:164
  165.0 0.3 convolution_convert_fusion.2
  165.3 1.1 copy.23
  166.4 5.3 %all-to-all-start.3 = ((bf16[64,7,512]{2,1,0:T(8,128)(2,1)}), bf16[64,7,512]{2,1,0:T(8,128)(2,1)S(1)}, u32[]{:S(2)}, u32[]{:S(2)}) async-start(bf16[64,7,512]{2,1,0:T(8,128)(2,1)} %copy.23), calls=%async_computation.3 | async-start | bytes 1048576 | tf_op jit(solution)/shard_map/all_to_all | solution.py:164
  172.4 17.5 %all-to-all-done.3 = bf16[64,7,512]{2,1,0:T(8,128)(2,1)S(1)} async-done(((bf16[64,7,512]{2,1,0:T(8,128)(2,1)}), bf16[64,7,512]{2,1,0:T(8,128)(2,1)S(1)}, u32[]{:S(2)}, u32[]{:S(2)}) %all-to-all-start.3) | async-done | bytes 458784 | tf_op jit(solution)/shard_map/all_to_all | solution.py:164
  190.1 3.9 %adam.1 = (bf16[1,448,512]{2,1,0:T(8,128)(2,1)}, f32[1,448,512]{2,1,0:T(8,128)}, f32[1,448,512]{2,1,0:T(8,128)}) custom-call(s32[2]{0:T(128)S(1)} %pad_add_fusion.place, bf16[448,512]{1,0:T(8,128)(2,1)S(1)} %reshape.29.params, bf16[448,512]{1,0:T(8,128)(2,1)S(1)} %reshape.30.first, bf16[448,512]{1,0:T(8,128)(2,1)S(1)} %reshape.31.second, ...), custom_call_target="tpu_custom_call" | custom-call | tf_op jit(solution)/shard_map/adam/pallas_call | solution.py:292
  (42 shorter events, 1.7 us)
Async XLA Ops:
  0.6 20.0 %copy-start.2 = (f32[16,7,512]{2,0,1:T(8,128)S(1)}, f32[16,7,512]{2,0,1:T(8,128)}, u32[]{:S(2)}) copy-start(f32[16,7,512]{2,0,1:T(8,128)} %param.8) | copy-start | bytes 688132
  0.6 20.1 %copy-start.3 = (f32[16,7,512]{2,0,1:T(8,128)S(1)}, f32[16,7,512]{2,0,1:T(8,128)}, u32[]{:S(2)}) copy-start(f32[16,7,512]{2,0,1:T(8,128)} %param.9) | copy-start | bytes 688132
  0.7 74.4 %collective-permute-start = (bf16[256,3584]{1,0:T(8,128)(2,1)}, bf16[256,3584]{1,0:T(8,128)(2,1)}, u32[]{:S(2)}, u32[]{:S(2)}) collective-permute-start(bf16[256,3584]{1,0:T(8,128)(2,1)} %bitcast.15), channel_id=1, source_target_pairs={{0,64},{64,0},{128,192},{192,128},{256,320},{320,256},{384,448},{4... | collective-permute-start | bytes 5505032 | tf_op jit(solution)/shard_map/ppermute | solution.py:178
  5.6 18.2 %copy-start.5 = (s32[64]{0:T(128)S(1)}, s32[64]{0:T(128)}, u32[]{:S(2)}) copy-start(s32[64]{0:T(128)} %param.10) | copy-start | bytes 772
  5.6 34.2 %all-to-all-start = ((bf16[64,7,512]{2,1,0:T(8,128)(2,1)}), bf16[64,7,512]{2,1,0:T(8,128)(2,1)S(1)}, u32[]{:S(2)}, u32[]{:S(2)}) async-start(bf16[64,7,512]{2,1,0:T(8,128)(2,1)} %copy.20), calls=%async_computation | async-start | bytes 1048576 | tf_op jit(solution)/shard_map/all_to_all | solution.py:164
  20.8 11.5 %collective-permute-start.13 = (bf16[16,14,512]{2,0,1:T(8,128)(2,1)S(1)}, bf16[16,14,512]{2,0,1:T(8,128)(2,1)S(1)}, u32[]{:S(2)}, u32[]{:S(2)}) collective-permute-start(bf16[16,14,512]{2,0,1:T(8,128)(2,1)S(1)} %pad_maximum_fusion.3), channel_id=1, source_target_pairs={{0,32},{1,33},{2,34},{3,35},{4,36},{5,37},{6,38},{7,39},{8,40},{9,... | collective-permute-start | bytes 688136 | tf_op jit(solution)/shard_map/ppermute | solution.py:216
  34.4 21.6 %copy-start.4 = (bf16[1,1,256,256]{3,2,1,0:T(8,128)(2,1)S(1)}, bf16[1,1,256,256]{3,2,1,0:T(8,128)(2,1)}, u32[]{:S(2)}) copy-start(bf16[1,1,256,256]{3,2,1,0:T(8,128)(2,1)} %param.13) | copy-start | bytes 393220
  34.4 42.7 %copy-start = (bf16[1,1,256,3584]{3,2,1,0:T(8,128)(2,1)S(1)}, bf16[1,1,256,3584]{3,2,1,0:T(8,128)(2,1)}, u32[]{:S(2)}) copy-start(bf16[1,1,256,3584]{3,2,1,0:T(8,128)(2,1)} %param.12) | copy-start | bytes 5505028
  39.8 0.8 copy-start.1
  40.6 79.7 %all-to-all-start.1 = ((bf16[32,28,512]{2,1,0:T(8,128)(2,1)}), bf16[32,28,512]{2,1,0:T(8,128)(2,1)S(1)}, u32[]{:S(2)}, u32[]{:S(2)}) async-start(bf16[32,28,512]{2,1,0:T(8,128)(2,1)} %copy.21), calls=%async_computation.1 | async-start | bytes 2097152 | tf_op jit(solution)/shard_map/all_to_all | solution.py:222
  46.1 13.0 %collective-permute-start.1 = (bf16[448,256]{1,0:T(8,128)(2,1)S(1)}, bf16[448,256]{1,0:T(8,128)(2,1)S(1)}, u32[]{:S(2)}, u32[]{:S(2)}) collective-permute-start(bf16[448,256]{1,0:T(8,128)(2,1)S(1)} %get-tuple-element.39), channel_id=1, source_target_pairs={{0,64},{64,0},{128,192},{192,128},{256,320},{320,256},{384,448},{4... | collective-permute-start | bytes 688136 | tf_op jit(solution)/shard_map/ppermute | solution.py:178
  48.0 23.3 %collective-permute-start.3 = (bf16[448,256]{1,0:T(8,128)(2,1)S(1)}, bf16[448,256]{1,0:T(8,128)(2,1)S(1)}, u32[]{:S(2)}, u32[]{:S(2)}) collective-permute-start(bf16[448,256]{1,0:T(8,128)(2,1)S(1)} %get-tuple-element.39), channel_id=1, source_target_pairs={{0,448},{64,384},{128,64},{192,0},{256,192},{320,128},{384,320},{4... | collective-permute-start | bytes 688136 | tf_op jit(solution)/shard_map/ppermute | solution.py:175
  52.2 16.2 %collective-permute-start.4 = (bf16[448,256]{1,0:T(8,128)(2,1)S(1)}, bf16[448,256]{1,0:T(8,128)(2,1)S(1)}, u32[]{:S(2)}, u32[]{:S(2)}) collective-permute-start(bf16[448,256]{1,0:T(8,128)(2,1)S(1)} %get-tuple-element.40.rest_0_), channel_id=1, source_target_pairs={{0,128},{64,192},{128,256},{192,320},{256,384},{320,448},{384,0},{... | collective-permute-start | bytes 688136 | tf_op jit(solution)/shard_map/ppermute | solution.py:175
  56.2 23.6 %collective-permute-start.2 = (bf16[448,256]{1,0:T(8,128)(2,1)S(1)}, bf16[448,256]{1,0:T(8,128)(2,1)S(1)}, u32[]{:S(2)}, u32[]{:S(2)}) collective-permute-start(bf16[448,256]{1,0:T(8,128)(2,1)S(1)} %get-tuple-element.40.rest_0_), channel_id=1, source_target_pairs={{0,384},{64,448},{128,0},{192,64},{256,128},{320,192},{384,256},{4... | collective-permute-start | bytes 688136 | tf_op jit(solution)/shard_map/ppermute | solution.py:175
  59.0 20.7 %collective-permute-start.5 = (bf16[448,256]{1,0:T(8,128)(2,1)S(1)}, bf16[448,256]{1,0:T(8,128)(2,1)S(1)}, u32[]{:S(2)}, u32[]{:S(2)}) collective-permute-start(bf16[448,256]{1,0:T(8,128)(2,1)S(1)} %get-tuple-element.39), channel_id=1, source_target_pairs={{0,192},{64,128},{128,320},{192,256},{256,448},{320,384},{384,64},... | collective-permute-start | bytes 688136 | tf_op jit(solution)/shard_map/ppermute | solution.py:175
  68.3 16.0 %collective-permute-start.7 = (bf16[448,256]{1,0:T(8,128)(2,1)S(1)}, bf16[448,256]{1,0:T(8,128)(2,1)S(1)}, u32[]{:S(2)}, u32[]{:S(2)}) collective-permute-start(bf16[448,256]{1,0:T(8,128)(2,1)S(1)} %collective-permute-done.4.rest_4_), channel_id=1, source_target_pairs={{0,128},{64,192},{128,256},{192,320},{256,384},{320,448},{384,0},{... | collective-permute-start | bytes 688136 | tf_op jit(solution)/shard_map/ppermute | solution.py:175
  71.3 14.8 %collective-permute-start.8 = (bf16[448,256]{1,0:T(8,128)(2,1)S(1)}, bf16[448,256]{1,0:T(8,128)(2,1)S(1)}, u32[]{:S(2)}, u32[]{:S(2)}) collective-permute-start(bf16[448,256]{1,0:T(8,128)(2,1)S(1)} %collective-permute-done.3.rest_3_), channel_id=1, source_target_pairs={{0,384},{64,448},{128,0},{192,64},{256,128},{320,192},{384,256},{4... | collective-permute-start | bytes 688136 | tf_op jit(solution)/shard_map/ppermute | solution.py:175
  75.1 7.2 %collective-permute-start.6 = (bf16[256,128]{1,0:T(8,128)(2,1)S(1)}, bf16[256,128]{1,0:T(8,128)(2,1)S(1)}, u32[]{:S(2)}, u32[]{:S(2)}) collective-permute-start(bf16[256,128]{1,0:T(8,128)(2,1)S(1)} %get-tuple-element.46), channel_id=1, source_target_pairs={{0,64},{64,0},{128,192},{192,128},{256,320},{320,256},{384,448},{4... | collective-permute-start | bytes 196616 | tf_op jit(solution)/shard_map/ppermute | solution.py:178
  87.6 13.3 %collective-permute-start.9 = (bf16[448,256]{1,0:T(8,128)(2,1)S(1)}, bf16[448,256]{1,0:T(8,128)(2,1)S(1)}, u32[]{:S(2)}, u32[]{:S(2)}) collective-permute-start(bf16[448,256]{1,0:T(8,128)(2,1)S(1)} %get-tuple-element.23), channel_id=1, source_target_pairs={{0,128},{64,192},{128,256},{192,320},{256,384},{320,448},{384,0},{... | collective-permute-start | bytes 688136 | tf_op jit(solution)/shard_map/ppermute | solution.py:175
  90.7 17.3 %collective-permute-start.11 = (bf16[448,256]{1,0:T(8,128)(2,1)S(1)}, bf16[448,256]{1,0:T(8,128)(2,1)S(1)}, u32[]{:S(2)}, u32[]{:S(2)}) collective-permute-start(bf16[448,256]{1,0:T(8,128)(2,1)S(1)} %get-tuple-element.25), channel_id=1, source_target_pairs={{0,384},{64,448},{128,0},{192,64},{256,128},{320,192},{384,256},{4... | collective-permute-start | bytes 688136 | tf_op jit(solution)/shard_map/ppermute | solution.py:175
  101.6 18.8 %collective-permute-start.10 = (bf16[448,256]{1,0:T(8,128)(2,1)}, bf16[448,256]{1,0:T(8,128)(2,1)S(1)}, u32[]{:S(2)}, u32[]{:S(2)}) collective-permute-start(bf16[448,256]{1,0:T(8,128)(2,1)} %add_convert_fusion.3), channel_id=1, source_target_pairs={{0,128},{64,192},{128,256},{192,320},{256,384},{320,448},{384,0},{... | collective-permute-start | bytes 688136 | tf_op jit(solution)/shard_map/ppermute | solution.py:175
  108.8 15.4 %collective-permute-start.12 = (bf16[448,256]{1,0:T(8,128)(2,1)}, bf16[448,256]{1,0:T(8,128)(2,1)S(1)}, u32[]{:S(2)}, u32[]{:S(2)}) collective-permute-start(bf16[448,256]{1,0:T(8,128)(2,1)} %add_convert_fusion.2), channel_id=1, source_target_pairs={{0,448},{64,384},{128,64},{192,0},{256,192},{320,128},{384,320},{4... | collective-permute-start | bytes 688136 | tf_op jit(solution)/shard_map/ppermute | solution.py:175
  110.7 15.0 %collective-permute-start.16 = (bf16[448,256]{1,0:T(8,128)(2,1)S(1)}, bf16[448,256]{1,0:T(8,128)(2,1)S(1)}, u32[]{:S(2)}, u32[]{:S(2)}) collective-permute-start(bf16[448,256]{1,0:T(8,128)(2,1)S(1)} %get-tuple-element.31), channel_id=1, source_target_pairs={{0,192},{64,128},{128,320},{192,256},{256,448},{320,384},{384,64},... | collective-permute-start | bytes 688136 | tf_op jit(solution)/shard_map/ppermute | solution.py:175
  116.5 9.3 %collective-permute-start.15 = (bf16[448,256]{1,0:T(8,128)(2,1)S(1)}, bf16[448,256]{1,0:T(8,128)(2,1)}, u32[]{:S(2)}, u32[]{:S(2)}) collective-permute-start(bf16[448,256]{1,0:T(8,128)(2,1)S(1)} %get-tuple-element.30), channel_id=1, source_target_pairs={{0,64},{64,0},{128,192},{192,128},{256,320},{320,256},{384,448},{4... | collective-permute-start | bytes 688136 | tf_op jit(solution)/shard_map/ppermute | solution.py:178
  118.4 16.9 %collective-permute-start.14 = (bf16[448,256]{1,0:T(8,128)(2,1)S(1)}, bf16[448,256]{1,0:T(8,128)(2,1)S(1)}, u32[]{:S(2)}, u32[]{:S(2)}) collective-permute-start(bf16[448,256]{1,0:T(8,128)(2,1)S(1)} %get-tuple-element.28), channel_id=1, source_target_pairs={{0,384},{64,448},{128,0},{192,64},{256,128},{320,192},{384,256},{4... | collective-permute-start | bytes 688136 | tf_op jit(solution)/shard_map/ppermute | solution.py:175
  166.4 23.5 %all-to-all-start.3 = ((bf16[64,7,512]{2,1,0:T(8,128)(2,1)}), bf16[64,7,512]{2,1,0:T(8,128)(2,1)S(1)}, u32[]{:S(2)}, u32[]{:S(2)}) async-start(bf16[64,7,512]{2,1,0:T(8,128)(2,1)} %copy.23), calls=%async_computation.3 | async-start | bytes 1048576 | tf_op jit(solution)/shard_map/all_to_all | solution.py:164

commit v5 on v4

--- a/solution.py
+++ b/solution.py
@@ -47,12 +47,16 @@
     return jnp.dot(rows, grad_ref[...], preferred_element_type=jnp.float32).astype(jnp.bfloat16)
 
 
+def chip_at(place, step):
+    return (place[0] + step * (1 + 2 * place[1])) % 4
+
+
 def piece_start(place, step, side, count):
-    return pl.multiple_of((2 * ((place[0] + step) % 4) + (place[1] + side) % 2) * count, 16)
+    return pl.multiple_of((2 * chip_at(place, step) + (place[1] + side) % 2) * count, 16)
 
 
 def block_start(place, step, count):
-    return pl.multiple_of(((place[0] + step) % 4) * 2 * count, 128)
+    return pl.multiple_of(chip_at(place, step) * 2 * count, 128)
 
 
 def join(place, block, mine, theirs):
@@ -166,9 +170,17 @@
     def choose(table, values):
         return jnp.einsum("jk,krc->jrc", table, values, preferred_element_type=jnp.float32).astype(narrow)
 
-    def shift(value, step, cross=0):
+    def shift(value, step):
         pairs = [
-            (2 * h + c, 2 * ((h + step) % chip_count) + (c ^ cross))
+            (2 * h + c, 2 * ((h + (1 - 2 * c) * step) % chip_count) + c)
+            for h in range(chip_count)
+            for c in range(2)
+        ]
+        return lax.ppermute(value, "dp", pairs)
+
+    def shift_other(value, step, sense):
+        pairs = [
+            (2 * h + c, 2 * ((h + sense * (1 - 2 * c) * step) % chip_count) + 1 - c)
             for h in range(chip_count)
             for c in range(2)
         ]
@@ -206,8 +218,8 @@
     plus_mine = shift(mine, 1)
     minus_mine = shift(mine, -1)
     theirs = swap(give)
-    minus_theirs = shift(give, -1, 1)
-    plus_theirs = shift(give, 1, 1)
+    minus_theirs = shift_other(give, -1, -1)
+    plus_theirs = shift_other(give, 1, -1)
     far_mine = shift(plus_mine, 1)
     far_theirs = shift(minus_theirs, -1)
 
@@ -265,11 +277,11 @@
         name="terms",
         compiler_params=pltpu.CompilerParams(vmem_limit_bytes=8 * MEBI),
     )(place, turned, grad_proj)
-    early_other = shift(next_theirs, 1, 1)
+    early_other = shift_other(next_theirs, 1, 1)
     early_mine = shift(last_mine, -1)
     base_other = swap(sum_theirs)
     late_mine = shift(add(next_mine, got_plus), 1)
-    late_other = shift(add(last_theirs, got_minus), -1, 1)
+    late_other = shift_other(add(last_theirs, got_minus), -1, 1)
     late_mine, late_other, moments_here = lax.optimization_barrier((late_mine, late_other, moments_here))
     total = jnp.concatenate(
         [add(sum_mine, early_mine, late_mine), add(base_other, early_other, late_other)], axis=1
@@ -284,7 +296,7 @@
         return rows_of(jnp.concatenate(sides, axis=0))
 
     grad_rows = rows_of(exchange(choose(same, home)))
-    bands = span_rows
+    bands = 2
     band = own_count // bands
     spec = pl.BlockSpec((band, col_total), lambda i: (i, 0))
     out_spec = pl.BlockSpec((1, band, col_total), lambda i: (0, i, 0))

time: 195 us -> 189 us (0.969)
  the two profiles are of different devices: /device:TPU:56 before, /device:TPU:8 now
where the time goes in v5:
time: 189 us; the launch traced here: 188 us
  starting transfers between devices  87.3 us (46%)
  waiting for transfers between devices  44.9 us (24%)
  blocking collectives  30.8 us (16%)
  Pallas kernels  10.5 us (6%)
  local copies, waits for them, and re-layouts  7.31 us (4%)
  other arithmetic  3.3 us (2%)
    ppermute x8, starting transfers between devices, shift(): return lax.ppermute(value, 'dp', pairs)  36.7 us
    all_to_all x1, blocking collectives, exchange(): lax.all_to_all(values, 'expert', split_axis=0, concat_axis=0, tiled=True)  30.8 us
    all_to_all x2, waiting for transfers between devices, exchange(): lax.all_to_all(values, 'expert', split_axis=0, concat_axis=0, tiled=True)  23.4 us
    all_to_all x2, starting transfers between devices, exchange(): lax.all_to_all(values, 'expert', split_axis=0, concat_axis=0, tiled=True)  20.5 us
    ppermute x4, starting transfers between devices, shift_other(): return lax.ppermute(value, 'dp', pairs)  15.4 us
    ppermute x8, waiting for transfers between devices, shift(): return lax.ppermute(value, 'dp', pairs)  9.91 us
    ppermute x1, waiting for transfers between devices, on_device(): lax.ppermute(stored, 'expert', [(e, (e + group) % expert_count) for e in...  8.52 us
    ppermute x4, starting transfers between devices, swap(): return lax.ppermute(value, 'dp', [(i, i ^ 1) for i in range(dp_count)])  8.2 us
  transfers between devices with their start and end apart: 20, of which 8 were waited for; matrix products, arithmetic and copies ran while one was open for 5% of the time, Pallas kernels for 4%

profile of v5, /device:TPU:8, one launch (start us, length us, event | category | flops | bytes accessed | tf_op | source)
XLA Modules:
  0.0 187.8 jit_solution(17353756316818420396)
XLA Ops:
  0.7 2.1 %collective-permute-start = (bf16[256,3584]{1,0:T(8,128)(2,1)}, bf16[256,3584]{1,0:T(8,128)(2,1)}, u32[]{:S(2)}, u32[]{:S(2)}) collective-permute-start(bf16[256,3584]{1,0:T(8,128)(2,1)} %bitcast.15), channel_id=1, source_target_pairs={{0,64},{64,0},{128,192},{192,128},{256,320},{320,256},{384,448},{4... | collective-permute-start | bytes 5505032 | tf_op jit(solution)/shard_map/ppermute | solution.py:190
  2.7 0.8 fusion.26
  3.6 1.0 convolution_convert_fusion.1
  4.6 1.1 copy.20
  5.6 15.0 %all-to-all-start = ((bf16[64,7,512]{2,1,0:T(8,128)(2,1)}), bf16[64,7,512]{2,1,0:T(8,128)(2,1)S(1)}, u32[]{:S(2)}, u32[]{:S(2)}) async-start(bf16[64,7,512]{2,1,0:T(8,128)(2,1)} %copy.20), calls=%async_computation | async-start | bytes 1048576 | tf_op jit(solution)/shard_map/all_to_all | solution.py:168
  20.8 2.3 %collective-permute-start.13 = (bf16[16,14,512]{2,0,1:T(8,128)(2,1)S(1)}, bf16[16,14,512]{2,0,1:T(8,128)(2,1)S(1)}, u32[]{:S(2)}, u32[]{:S(2)}) collective-permute-start(bf16[16,14,512]{2,0,1:T(8,128)(2,1)S(1)} %pad_maximum_fusion.3), channel_id=1, source_target_pairs={{0,32},{1,33},{2,34},{3,35},{4,36},{5,37},{6,38},{7,39},{8,40},{9,... | collective-permute-start | bytes 688136 | tf_op jit(solution)/shard_map/ppermute | solution.py:228
  23.8 8.5 %collective-permute-done.13 = bf16[16,14,512]{2,0,1:T(8,128)(2,1)S(1)} collective-permute-done((bf16[16,14,512]{2,0,1:T(8,128)(2,1)S(1)}, bf16[16,14,512]{2,0,1:T(8,128)(2,1)S(1)}, u32[]{:S(2)}, u32[]{:S(2)}) %collective-permute-start.13) | collective-permute-done | bytes 229408 | tf_op jit(solution)/shard_map/ppermute | solution.py:228
  32.4 0.5 convolution_convert_fusion
  32.9 1.5 copy.21
  34.4 5.3 %all-to-all-done = bf16[64,7,512]{2,1,0:T(8,128)(2,1)S(1)} async-done(((bf16[64,7,512]{2,1,0:T(8,128)(2,1)}), bf16[64,7,512]{2,1,0:T(8,128)(2,1)S(1)}, u32[]{:S(2)}, u32[]{:S(2)}) %all-to-all-start) | async-done | bytes 458784 | tf_op jit(solution)/shard_map/all_to_all | solution.py:168
  39.8 0.8 copy-done.1
  40.6 4.2 %all-to-all-start.1 = ((bf16[32,28,512]{2,1,0:T(8,128)(2,1)}), bf16[32,28,512]{2,1,0:T(8,128)(2,1)S(1)}, u32[]{:S(2)}, u32[]{:S(2)}) async-start(bf16[32,28,512]{2,1,0:T(8,128)(2,1)} %copy.21), calls=%async_computation.1 | async-start | bytes 2097152 | tf_op jit(solution)/shard_map/all_to_all | solution.py:234
  44.8 1.2 reshape.29.params
  46.1 1.9 %collective-permute-start.1 = (bf16[448,256]{1,0:T(8,128)(2,1)S(1)}, bf16[448,256]{1,0:T(8,128)(2,1)S(1)}, u32[]{:S(2)}, u32[]{:S(2)}) collective-permute-start(bf16[448,256]{1,0:T(8,128)(2,1)S(1)} %get-tuple-element.39), channel_id=1, source_target_pairs={{0,64},{64,0},{128,192},{192,128},{256,320},{320,256},{384,448},{4... | collective-permute-start | bytes 688136 | tf_op jit(solution)/shard_map/ppermute | solution.py:190
  48.0 4.6 %collective-permute-start.3 = (bf16[448,256]{1,0:T(8,128)(2,1)S(1)}, bf16[448,256]{1,0:T(8,128)(2,1)S(1)}, u32[]{:S(2)}, u32[]{:S(2)}) collective-permute-start(bf16[448,256]{1,0:T(8,128)(2,1)S(1)} %get-tuple-element.39), channel_id=1, source_target_pairs={{0,192},{64,384},{128,320},{192,0},{256,448},{320,128},{384,64},{4... | collective-permute-start | bytes 688136 | tf_op jit(solution)/shard_map/ppermute | solution.py:187
  52.6 4.8 %collective-permute-start.4 = (bf16[448,256]{1,0:T(8,128)(2,1)S(1)}, bf16[448,256]{1,0:T(8,128)(2,1)S(1)}, u32[]{:S(2)}, u32[]{:S(2)}) collective-permute-start(bf16[448,256]{1,0:T(8,128)(2,1)S(1)} %get-tuple-element.40.rest_0_), channel_id=1, source_target_pairs={{0,128},{64,448},{128,256},{192,64},{256,384},{320,192},{384,0},{4... | collective-permute-start | bytes 688136 | tf_op jit(solution)/shard_map/ppermute | solution.py:179
  57.5 3.1 %collective-permute-start.2 = (bf16[448,256]{1,0:T(8,128)(2,1)S(1)}, bf16[448,256]{1,0:T(8,128)(2,1)S(1)}, u32[]{:S(2)}, u32[]{:S(2)}) collective-permute-start(bf16[448,256]{1,0:T(8,128)(2,1)S(1)} %get-tuple-element.40.rest_0_), channel_id=1, source_target_pairs={{0,384},{64,192},{128,0},{192,320},{256,128},{320,448},{384,256},{... | collective-permute-start | bytes 688136 | tf_op jit(solution)/shard_map/ppermute | solution.py:179
  60.7 3.9 %collective-permute-start.5 = (bf16[448,256]{1,0:T(8,128)(2,1)S(1)}, bf16[448,256]{1,0:T(8,128)(2,1)S(1)}, u32[]{:S(2)}, u32[]{:S(2)}) collective-permute-start(bf16[448,256]{1,0:T(8,128)(2,1)S(1)} %get-tuple-element.39), channel_id=1, source_target_pairs={{0,448},{64,128},{128,64},{192,256},{256,192},{320,384},{384,320},... | collective-permute-start | bytes 688136 | tf_op jit(solution)/shard_map/ppermute | solution.py:187
  64.6 2.0 %collective-permute-done.4.rest_4_ = bf16[448,256]{1,0:T(8,128)(2,1)S(1)} collective-permute-done((bf16[448,256]{1,0:T(8,128)(2,1)S(1)}, bf16[448,256]{1,0:T(8,128)(2,1)S(1)}, u32[]{:S(2)}, u32[]{:S(2)}) %collective-permute-start.4) | collective-permute-done | bytes 229408 | tf_op jit(solution)/shard_map/ppermute | solution.py:179
  66.6 8.7 %collective-permute-start.7 = (bf16[448,256]{1,0:T(8,128)(2,1)S(1)}, bf16[448,256]{1,0:T(8,128)(2,1)S(1)}, u32[]{:S(2)}, u32[]{:S(2)}) collective-permute-start(bf16[448,256]{1,0:T(8,128)(2,1)S(1)} %collective-permute-done.4.rest_4_), channel_id=1, source_target_pairs={{0,128},{64,448},{128,256},{192,64},{256,384},{320,192},{384,0},{4... | collective-permute-start | bytes 688136 | tf_op jit(solution)/shard_map/ppermute | solution.py:179
  75.3 1.9 %collective-permute-start.8 = (bf16[448,256]{1,0:T(8,128)(2,1)S(1)}, bf16[448,256]{1,0:T(8,128)(2,1)S(1)}, u32[]{:S(2)}, u32[]{:S(2)}) collective-permute-start(bf16[448,256]{1,0:T(8,128)(2,1)S(1)} %collective-permute-done.3.rest_3_), channel_id=1, source_target_pairs={{0,384},{64,192},{128,0},{192,320},{256,128},{320,448},{384,256},{... | collective-permute-start | bytes 688136 | tf_op jit(solution)/shard_map/ppermute | solution.py:179
  77.3 1.9 %collective-permute-start.6 = (bf16[256,128]{1,0:T(8,128)(2,1)S(1)}, bf16[256,128]{1,0:T(8,128)(2,1)S(1)}, u32[]{:S(2)}, u32[]{:S(2)}) collective-permute-start(bf16[256,128]{1,0:T(8,128)(2,1)S(1)} %get-tuple-element.46), channel_id=1, source_target_pairs={{0,64},{64,0},{128,192},{192,128},{256,320},{320,256},{384,448},{4... | collective-permute-start | bytes 196616 | tf_op jit(solution)/shard_map/ppermute | solution.py:190
  79.3 2.6 %turn.1 = (bf16[3584,512]{1,0:T(8,128)(2,1)S(1)}, bf16[512,896]{1,0:T(8,128)(2,1)S(1)}, bf16[896,512]{1,0:T(8,128)(2,1)S(1)}) custom-call(s32[2]{0:T(128)S(1)} %pad_add_fusion.place, bf16[256,3584]{1,0:T(8,128)(2,1)S(1)} %bitcast.16, bf16[256,3584]{1,0:T(8,128)(2,1)} %collective-permute-done.tok_theirs), custom_call_target="tpu_custom_call" | custom-call | tf_op jit(solution)/shard_map/turn/pallas_call | solution.py:239
  81.9 2.6 %partial.1 = f32[512,256]{1,0:T(8,128)S(1)} custom-call(s32[2]{0:T(128)S(1)} %pad_add_fusion.place, bf16[256,3584]{1,0:T(8,128)(2,1)S(1)} %bitcast.17, bf16[256,3584]{1,0:T(8,128)(2,1)} %collective-permute-done.tok_theirs, bf16[448,256]{1,0:T(8,128)(2,1)S(1)} %get-tuple-element.40.rest_0_, bf16[448,256]{1,0:T(8,128)(2,1)S(1)} %collective-permute-done.1.rest_1_, ...), custom_call_target="tpu_custom_call" | custom-call | tf_op jit(solution)/shard_map/partial/pallas_call | solution.py:252
  84.6 2.6 %collective-permute-done.8.piece_theirs = bf16[448,256]{1,0:T(8,128)(2,1)S(1)} collective-permute-done((bf16[448,256]{1,0:T(8,128)(2,1)S(1)}, bf16[448,256]{1,0:T(8,128)(2,1)S(1)}, u32[]{:S(2)}, u32[]{:S(2)}) %collective-permute-start.8) | collective-permute-done | bytes 229408 | tf_op jit(solution)/shard_map/ppermute | solution.py:179
  87.1 1.5 project.1
  88.6 4.8 %collective-permute-start.9 = (bf16[448,256]{1,0:T(8,128)(2,1)S(1)}, bf16[448,256]{1,0:T(8,128)(2,1)S(1)}, u32[]{:S(2)}, u32[]{:S(2)}) collective-permute-start(bf16[448,256]{1,0:T(8,128)(2,1)S(1)} %get-tuple-element.23), channel_id=1, source_target_pairs={{0,128},{64,448},{128,256},{192,64},{256,384},{320,192},{384,0},{4... | collective-permute-start | bytes 688136 | tf_op jit(solution)/shard_map/ppermute | solution.py:179
  93.4 3.2 %collective-permute-start.11 = (bf16[448,256]{1,0:T(8,128)(2,1)S(1)}, bf16[448,256]{1,0:T(8,128)(2,1)S(1)}, u32[]{:S(2)}, u32[]{:S(2)}) collective-permute-start(bf16[448,256]{1,0:T(8,128)(2,1)S(1)} %get-tuple-element.25), channel_id=1, source_target_pairs={{0,384},{64,192},{128,0},{192,320},{256,128},{320,448},{384,256},{... | collective-permute-start | bytes 688136 | tf_op jit(solution)/shard_map/ppermute | solution.py:179
  96.6 1.4 terms.1
  98.0 5.0 %collective-permute-done.9 = bf16[448,256]{1,0:T(8,128)(2,1)S(1)} collective-permute-done((bf16[448,256]{1,0:T(8,128)(2,1)S(1)}, bf16[448,256]{1,0:T(8,128)(2,1)S(1)}, u32[]{:S(2)}, u32[]{:S(2)}) %collective-permute-start.9) | collective-permute-done | bytes 229408 | tf_op jit(solution)/shard_map/ppermute | solution.py:179
  103.0 0.7 add_convert_fusion.3
  103.7 4.5 %collective-permute-start.10 = (bf16[448,256]{1,0:T(8,128)(2,1)}, bf16[448,256]{1,0:T(8,128)(2,1)S(1)}, u32[]{:S(2)}, u32[]{:S(2)}) collective-permute-start(bf16[448,256]{1,0:T(8,128)(2,1)} %add_convert_fusion.3), channel_id=1, source_target_pairs={{0,128},{64,448},{128,256},{192,64},{256,384},{320,192},{384,0},{4... | collective-permute-start | bytes 688136 | tf_op jit(solution)/shard_map/ppermute | solution.py:179
  108.3 0.7 add_convert_fusion.2
  109.0 1.9 %collective-permute-start.12 = (bf16[448,256]{1,0:T(8,128)(2,1)}, bf16[448,256]{1,0:T(8,128)(2,1)S(1)}, u32[]{:S(2)}, u32[]{:S(2)}) collective-permute-start(bf16[448,256]{1,0:T(8,128)(2,1)} %add_convert_fusion.2), channel_id=1, source_target_pairs={{0,448},{64,128},{128,64},{192,256},{256,192},{320,384},{384,320},... | collective-permute-start | bytes 688136 | tf_op jit(solution)/shard_map/ppermute | solution.py:187
  111.0 5.1 %collective-permute-start.16 = (bf16[448,256]{1,0:T(8,128)(2,1)S(1)}, bf16[448,256]{1,0:T(8,128)(2,1)S(1)}, u32[]{:S(2)}, u32[]{:S(2)}) collective-permute-start(bf16[448,256]{1,0:T(8,128)(2,1)S(1)} %get-tuple-element.31), channel_id=1, source_target_pairs={{0,192},{64,384},{128,320},{192,0},{256,448},{320,128},{384,64},{4... | collective-permute-start | bytes 688136 | tf_op jit(solution)/shard_map/ppermute | solution.py:187
  116.0 2.3 %collective-permute-start.15 = (bf16[448,256]{1,0:T(8,128)(2,1)S(1)}, bf16[448,256]{1,0:T(8,128)(2,1)}, u32[]{:S(2)}, u32[]{:S(2)}) collective-permute-start(bf16[448,256]{1,0:T(8,128)(2,1)S(1)} %get-tuple-element.30), channel_id=1, source_target_pairs={{0,64},{64,0},{128,192},{192,128},{256,320},{320,256},{384,448},{4... | collective-permute-start | bytes 688136 | tf_op jit(solution)/shard_map/ppermute | solution.py:190
  118.3 5.6 %collective-permute-start.14 = (bf16[448,256]{1,0:T(8,128)(2,1)S(1)}, bf16[448,256]{1,0:T(8,128)(2,1)S(1)}, u32[]{:S(2)}, u32[]{:S(2)}) collective-permute-start(bf16[448,256]{1,0:T(8,128)(2,1)S(1)} %get-tuple-element.28), channel_id=1, source_target_pairs={{0,384},{64,192},{128,0},{192,320},{256,128},{320,448},{384,256},{... | collective-permute-start | bytes 688136 | tf_op jit(solution)/shard_map/ppermute | solution.py:179
  124.0 3.0 %collective-permute-done.16 = bf16[448,256]{1,0:T(8,128)(2,1)S(1)} collective-permute-done((bf16[448,256]{1,0:T(8,128)(2,1)S(1)}, bf16[448,256]{1,0:T(8,128)(2,1)S(1)}, u32[]{:S(2)}, u32[]{:S(2)}) %collective-permute-start.16) | collective-permute-done | bytes 229408 | tf_op jit(solution)/shard_map/ppermute | solution.py:187
  127.1 1.0 add_convert_fusion
  128.1 0.3 collective-permute-done.14
  128.7 30.8 %all_to_all.20 = bf16[64,7,512]{2,1,0:T(8,128)(2,1)S(1)} all-to-all(bf16[64,7,512]{2,1,0:T(8,128)(2,1)S(1)} %reshape.32), channel_id=1, replica_groups=mesh['dp'=8,'expert'=64] {'expert'}, dimensions={0} | all-to-all | bytes 917504 | tf_op jit(solution)/shard_map/all_to_all | solution.py:168
  159.5 0.3 convolution_convert_fusion.2
  159.9 1.1 copy.23
  160.9 5.4 %all-to-all-start.3 = ((bf16[64,7,512]{2,1,0:T(8,128)(2,1)}), bf16[64,7,512]{2,1,0:T(8,128)(2,1)S(1)}, u32[]{:S(2)}, u32[]{:S(2)}) async-start(bf16[64,7,512]{2,1,0:T(8,128)(2,1)} %copy.23), calls=%async_computation.3 | async-start | bytes 1048576 | tf_op jit(solution)/shard_map/all_to_all | solution.py:168
  166.4 0.2 fusion.24
  166.6 0.2 pad_maximum_fusion
  167.1 18.1 %all-to-all-done.3 = bf16[64,7,512]{2,1,0:T(8,128)(2,1)S(1)} async-done(((bf16[64,7,512]{2,1,0:T(8,128)(2,1)}), bf16[64,7,512]{2,1,0:T(8,128)(2,1)S(1)}, u32[]{:S(2)}, u32[]{:S(2)}) %all-to-all-start.3) | async-done | bytes 458784 | tf_op jit(solution)/shard_map/all_to_all | solution.py:168
  185.4 2.4 %adam.1 = (bf16[1,448,512]{2,1,0:T(8,128)(2,1)}, f32[1,448,512]{2,1,0:T(8,128)}, f32[1,448,512]{2,1,0:T(8,128)}) custom-call(s32[2]{0:T(128)S(1)} %pad_add_fusion.place, bf16[448,512]{1,0:T(8,128)(2,1)S(1)} %reshape.29.params, bf16[448,512]{1,0:T(8,128)(2,1)S(1)} %reshape.30.first, bf16[448,512]{1,0:T(8,128)(2,1)S(1)} %reshape.31.second, ...), custom_call_target="tpu_custom_call" | custom-call | tf_op jit(solution)/shard_map/adam/pallas_call | solution.py:304
  (42 shorter events, 1.3 us)
Async XLA Ops:
  0.6 20.0 %copy-start.2 = (f32[16,7,512]{2,0,1:T(8,128)S(1)}, f32[16,7,512]{2,0,1:T(8,128)}, u32[]{:S(2)}) copy-start(f32[16,7,512]{2,0,1:T(8,128)} %param.8) | copy-start | bytes 688132
  0.6 20.1 %copy-start.3 = (f32[16,7,512]{2,0,1:T(8,128)S(1)}, f32[16,7,512]{2,0,1:T(8,128)}, u32[]{:S(2)}) copy-start(f32[16,7,512]{2,0,1:T(8,128)} %param.9) | copy-start | bytes 688132
  0.7 76.6 %collective-permute-start = (bf16[256,3584]{1,0:T(8,128)(2,1)}, bf16[256,3584]{1,0:T(8,128)(2,1)}, u32[]{:S(2)}, u32[]{:S(2)}) collective-permute-start(bf16[256,3584]{1,0:T(8,128)(2,1)} %bitcast.15), channel_id=1, source_target_pairs={{0,64},{64,0},{128,192},{192,128},{256,320},{320,256},{384,448},{4... | collective-permute-start | bytes 5505032 | tf_op jit(solution)/shard_map/ppermute | solution.py:190
  5.6 18.2 %copy-start.5 = (s32[64]{0:T(128)S(1)}, s32[64]{0:T(128)}, u32[]{:S(2)}) copy-start(s32[64]{0:T(128)} %param.10) | copy-start | bytes 772
  5.6 34.2 %all-to-all-start = ((bf16[64,7,512]{2,1,0:T(8,128)(2,1)}), bf16[64,7,512]{2,1,0:T(8,128)(2,1)S(1)}, u32[]{:S(2)}, u32[]{:S(2)}) async-start(bf16[64,7,512]{2,1,0:T(8,128)(2,1)} %copy.20), calls=%async_computation | async-start | bytes 1048576 | tf_op jit(solution)/shard_map/all_to_all | solution.py:168
  20.8 11.5 %collective-permute-start.13 = (bf16[16,14,512]{2,0,1:T(8,128)(2,1)S(1)}, bf16[16,14,512]{2,0,1:T(8,128)(2,1)S(1)}, u32[]{:S(2)}, u32[]{:S(2)}) collective-permute-start(bf16[16,14,512]{2,0,1:T(8,128)(2,1)S(1)} %pad_maximum_fusion.3), channel_id=1, source_target_pairs={{0,32},{1,33},{2,34},{3,35},{4,36},{5,37},{6,38},{7,39},{8,40},{9,... | collective-permute-start | bytes 688136 | tf_op jit(solution)/shard_map/ppermute | solution.py:228
  34.4 23.0 %copy-start.4 = (bf16[1,1,256,256]{3,2,1,0:T(8,128)(2,1)S(1)}, bf16[1,1,256,256]{3,2,1,0:T(8,128)(2,1)}, u32[]{:S(2)}) copy-start(bf16[1,1,256,256]{3,2,1,0:T(8,128)(2,1)} %param.13) | copy-start | bytes 393220
  34.4 44.9 %copy-start = (bf16[1,1,256,3584]{3,2,1,0:T(8,128)(2,1)S(1)}, bf16[1,1,256,3584]{3,2,1,0:T(8,128)(2,1)}, u32[]{:S(2)}) copy-start(bf16[1,1,256,3584]{3,2,1,0:T(8,128)(2,1)} %param.12) | copy-start | bytes 5505028
  39.8 0.8 copy-start.1
  40.6 83.4 %all-to-all-start.1 = ((bf16[32,28,512]{2,1,0:T(8,128)(2,1)}), bf16[32,28,512]{2,1,0:T(8,128)(2,1)S(1)}, u32[]{:S(2)}, u32[]{:S(2)}) async-start(bf16[32,28,512]{2,1,0:T(8,128)(2,1)} %copy.21), calls=%async_computation.1 | async-start | bytes 2097152 | tf_op jit(solution)/shard_map/all_to_all | solution.py:234
  46.1 14.6 %collective-permute-start.1 = (bf16[448,256]{1,0:T(8,128)(2,1)S(1)}, bf16[448,256]{1,0:T(8,128)(2,1)S(1)}, u32[]{:S(2)}, u32[]{:S(2)}) collective-permute-start(bf16[448,256]{1,0:T(8,128)(2,1)S(1)} %get-tuple-element.39), channel_id=1, source_target_pairs={{0,64},{64,0},{128,192},{192,128},{256,320},{320,256},{384,448},{4... | collective-permute-start | bytes 688136 | tf_op jit(solution)/shard_map/ppermute | solution.py:190
  48.0 27.3 %collective-permute-start.3 = (bf16[448,256]{1,0:T(8,128)(2,1)S(1)}, bf16[448,256]{1,0:T(8,128)(2,1)S(1)}, u32[]{:S(2)}, u32[]{:S(2)}) collective-permute-start(bf16[448,256]{1,0:T(8,128)(2,1)S(1)} %get-tuple-element.39), channel_id=1, source_target_pairs={{0,192},{64,384},{128,320},{192,0},{256,448},{320,128},{384,64},{4... | collective-permute-start | bytes 688136 | tf_op jit(solution)/shard_map/ppermute | solution.py:187
  52.6 14.0 %collective-permute-start.4 = (bf16[448,256]{1,0:T(8,128)(2,1)S(1)}, bf16[448,256]{1,0:T(8,128)(2,1)S(1)}, u32[]{:S(2)}, u32[]{:S(2)}) collective-permute-start(bf16[448,256]{1,0:T(8,128)(2,1)S(1)} %get-tuple-element.40.rest_0_), channel_id=1, source_target_pairs={{0,128},{64,448},{128,256},{192,64},{256,384},{320,192},{384,0},{4... | collective-permute-start | bytes 688136 | tf_op jit(solution)/shard_map/ppermute | solution.py:179
  57.5 24.4 %collective-permute-start.2 = (bf16[448,256]{1,0:T(8,128)(2,1)S(1)}, bf16[448,256]{1,0:T(8,128)(2,1)S(1)}, u32[]{:S(2)}, u32[]{:S(2)}) collective-permute-start(bf16[448,256]{1,0:T(8,128)(2,1)S(1)} %get-tuple-element.40.rest_0_), channel_id=1, source_target_pairs={{0,384},{64,192},{128,0},{192,320},{256,128},{320,448},{384,256},{... | collective-permute-start | bytes 688136 | tf_op jit(solution)/shard_map/ppermute | solution.py:179
  60.7 21.2 %collective-permute-start.5 = (bf16[448,256]{1,0:T(8,128)(2,1)S(1)}, bf16[448,256]{1,0:T(8,128)(2,1)S(1)}, u32[]{:S(2)}, u32[]{:S(2)}) collective-permute-start(bf16[448,256]{1,0:T(8,128)(2,1)S(1)} %get-tuple-element.39), channel_id=1, source_target_pairs={{0,448},{64,128},{128,64},{192,256},{256,192},{320,384},{384,320},... | collective-permute-start | bytes 688136 | tf_op jit(solution)/shard_map/ppermute | solution.py:187
  66.6 18.0 %collective-permute-start.7 = (bf16[448,256]{1,0:T(8,128)(2,1)S(1)}, bf16[448,256]{1,0:T(8,128)(2,1)S(1)}, u32[]{:S(2)}, u32[]{:S(2)}) collective-permute-start(bf16[448,256]{1,0:T(8,128)(2,1)S(1)} %collective-permute-done.4.rest_4_), channel_id=1, source_target_pairs={{0,128},{64,448},{128,256},{192,64},{256,384},{320,192},{384,0},{4... | collective-permute-start | bytes 688136 | tf_op jit(solution)/shard_map/ppermute | solution.py:179
  75.3 11.8 %collective-permute-start.8 = (bf16[448,256]{1,0:T(8,128)(2,1)S(1)}, bf16[448,256]{1,0:T(8,128)(2,1)S(1)}, u32[]{:S(2)}, u32[]{:S(2)}) collective-permute-start(bf16[448,256]{1,0:T(8,128)(2,1)S(1)} %collective-permute-done.3.rest_3_), channel_id=1, source_target_pairs={{0,384},{64,192},{128,0},{192,320},{256,128},{320,448},{384,256},{... | collective-permute-start | bytes 688136 | tf_op jit(solution)/shard_map/ppermute | solution.py:179
  77.3 7.2 %collective-permute-start.6 = (bf16[256,128]{1,0:T(8,128)(2,1)S(1)}, bf16[256,128]{1,0:T(8,128)(2,1)S(1)}, u32[]{:S(2)}, u32[]{:S(2)}) collective-permute-start(bf16[256,128]{1,0:T(8,128)(2,1)S(1)} %get-tuple-element.46), channel_id=1, source_target_pairs={{0,64},{64,0},{128,192},{192,128},{256,320},{320,256},{384,448},{4... | collective-permute-start | bytes 196616 | tf_op jit(solution)/shard_map/ppermute | solution.py:190
  88.6 14.4 %collective-permute-start.9 = (bf16[448,256]{1,0:T(8,128)(2,1)S(1)}, bf16[448,256]{1,0:T(8,128)(2,1)S(1)}, u32[]{:S(2)}, u32[]{:S(2)}) collective-permute-start(bf16[448,256]{1,0:T(8,128)(2,1)S(1)} %get-tuple-element.23), channel_id=1, source_target_pairs={{0,128},{64,448},{128,256},{192,64},{256,384},{320,192},{384,0},{4... | collective-permute-start | bytes 688136 | tf_op jit(solution)/shard_map/ppermute | solution.py:179
  93.4 14.9 %collective-permute-start.11 = (bf16[448,256]{1,0:T(8,128)(2,1)S(1)}, bf16[448,256]{1,0:T(8,128)(2,1)S(1)}, u32[]{:S(2)}, u32[]{:S(2)}) collective-permute-start(bf16[448,256]{1,0:T(8,128)(2,1)S(1)} %get-tuple-element.25), channel_id=1, source_target_pairs={{0,384},{64,192},{128,0},{192,320},{256,128},{320,448},{384,256},{... | collective-permute-start | bytes 688136 | tf_op jit(solution)/shard_map/ppermute | solution.py:179
  103.7 20.3 %collective-permute-start.10 = (bf16[448,256]{1,0:T(8,128)(2,1)}, bf16[448,256]{1,0:T(8,128)(2,1)S(1)}, u32[]{:S(2)}, u32[]{:S(2)}) collective-permute-start(bf16[448,256]{1,0:T(8,128)(2,1)} %add_convert_fusion.3), channel_id=1, source_target_pairs={{0,128},{64,448},{128,256},{192,64},{256,384},{320,192},{384,0},{4... | collective-permute-start | bytes 688136 | tf_op jit(solution)/shard_map/ppermute | solution.py:179
  109.0 15.0 %collective-permute-start.12 = (bf16[448,256]{1,0:T(8,128)(2,1)}, bf16[448,256]{1,0:T(8,128)(2,1)S(1)}, u32[]{:S(2)}, u32[]{:S(2)}) collective-permute-start(bf16[448,256]{1,0:T(8,128)(2,1)} %add_convert_fusion.2), channel_id=1, source_target_pairs={{0,448},{64,128},{128,64},{192,256},{256,192},{320,384},{384,320},... | collective-permute-start | bytes 688136 | tf_op jit(solution)/shard_map/ppermute | solution.py:187
  111.0 16.1 %collective-permute-start.16 = (bf16[448,256]{1,0:T(8,128)(2,1)S(1)}, bf16[448,256]{1,0:T(8,128)(2,1)S(1)}, u32[]{:S(2)}, u32[]{:S(2)}) collective-permute-start(bf16[448,256]{1,0:T(8,128)(2,1)S(1)} %get-tuple-element.31), channel_id=1, source_target_pairs={{0,192},{64,384},{128,320},{192,0},{256,448},{320,128},{384,64},{4... | collective-permute-start | bytes 688136 | tf_op jit(solution)/shard_map/ppermute | solution.py:187
  116.0 11.0 %collective-permute-start.15 = (bf16[448,256]{1,0:T(8,128)(2,1)S(1)}, bf16[448,256]{1,0:T(8,128)(2,1)}, u32[]{:S(2)}, u32[]{:S(2)}) collective-permute-start(bf16[448,256]{1,0:T(8,128)(2,1)S(1)} %get-tuple-element.30), channel_id=1, source_target_pairs={{0,64},{64,0},{128,192},{192,128},{256,320},{320,256},{384,448},{4... | collective-permute-start | bytes 688136 | tf_op jit(solution)/shard_map/ppermute | solution.py:190
  118.3 10.1 %collective-permute-start.14 = (bf16[448,256]{1,0:T(8,128)(2,1)S(1)}, bf16[448,256]{1,0:T(8,128)(2,1)S(1)}, u32[]{:S(2)}, u32[]{:S(2)}) collective-permute-start(bf16[448,256]{1,0:T(8,128)(2,1)S(1)} %get-tuple-element.28), channel_id=1, source_target_pairs={{0,384},{64,192},{128,0},{192,320},{256,128},{320,448},{384,256},{... | collective-permute-start | bytes 688136 | tf_op jit(solution)/shard_map/ppermute | solution.py:179
  160.9 24.3 %all-to-all-start.3 = ((bf16[64,7,512]{2,1,0:T(8,128)(2,1)}), bf16[64,7,512]{2,1,0:T(8,128)(2,1)S(1)}, u32[]{:S(2)}, u32[]{:S(2)}) async-start(bf16[64,7,512]{2,1,0:T(8,128)(2,1)} %copy.23), calls=%async_computation.3 | async-start | bytes 1048576 | tf_op jit(solution)/shard_map/all_to_all | solution.py:168
